TPU v7x, 512 devices: a 8x2x16 block of a 8x8x16 slice. The times are simulated.
512 devices in a mesh: grp: 2 (over y), seq: 32 (over z, core), head: 8 (over x).
Axes of the slice: x: 8, y: 2, z: 16, core: 2. Of those that a mesh axis runs over, the one named last changes fastest.
The devices are a block of a 8x8x16 slice.
Arguments:
- draft_features: bfloat16 [16384, 8192], P(('grp', 'seq'), 'head'), parts along dimension 0, may hold values from -6 to 6
- w_key: bfloat16 [8192, 1024], P(None, 'head'), may hold values from -0.0625 to 0.0625
- w_value: bfloat16 [8192, 1024], P(None, 'head'), may hold values from -0.0625 to 0.0625
- accepted: int32 [2048], P(('grp', 'seq')), parts along dimension 0, may hold values from 1 to 8
- owner_group: int32 [2048], P(('grp', 'seq')), parts along dimension 0, may hold values from 0 to 31, as said below
- page_slot: int32 [2048], P(('grp', 'seq')), parts along dimension 0, may hold values from 0 to 63, as said below
Outputs:
- key_cache: bfloat16 [4096, 8, 1024], P(('grp', 'seq'), None, 'head'), parts along dimension 0
- value_cache: bfloat16 [4096, 8, 1024], P(('grp', 'seq'), None, 'head'), parts along dimension 0
There are 2 independent parts, one for each index of `grp`. A program takes and returns all parts, laid end to end along the dimension named above; an argument that names none is the same for every part. Nothing has to cross between parts.
Inputs may be any that keep to these rules, and one draw needn't show every extreme that they name: `owner_group`: the requests of one index of seq go to exactly 16 distinct owners, 2 to each; some owner receives 64 requests. `page_slot`: the requests of one owner have distinct slots.
All inputs are finite; a program needn't handle non-finite values.
Results may differ from a plain program's by a relative error of at most 0.001.
Values may be sent and summed in bfloat16 or wider, within the bound.
No kernel may reach another device: no remote copies, remote signals or barrier semaphores. Data moves between devices by JAX's collectives and lax.ppermute only.
A program may use at most 64 MiB of HBM per device.

v0:
```python
import jax
import jax.numpy as jnp
from jax import lax
from jax.sharding import PartitionSpec as P


def turned_gather(arrays, axis, dims):
    turned = [jnp.moveaxis(a, dim, 0) for a, dim in zip(arrays, dims)]
    both = jnp.concatenate([t.reshape(len(t), -1) for t in turned], axis=1)
    filled, at, gathered = (lax.all_gather(both, axis, axis=0, tiled=True), 0, [])
    for t, dim in zip(turned, dims):
        piece = filled[:, at : at + t[0].size].reshape(-1, *t.shape[1:])
        gathered.append(jnp.moveaxis(piece, 0, dim))
        at += t[0].size
    return tuple(gathered)


def pair_slots(owner_ids, slot_cap):
    row_count = owner_ids.shape[-1]
    same_owner = owner_ids[..., :, None] == owner_ids[..., None, :]
    before = lax.broadcasted_iota(jnp.int32, (row_count, row_count), 1) < lax.broadcasted_iota(
        jnp.int32, (row_count, row_count), 0
    )
    within = jnp.sum(jnp.where(same_owner & before, 1, 0), axis=-1).astype(jnp.int32)
    return owner_ids * slot_cap + within


def one_hot(labels, columns):
    return (
        labels[:, None] == lax.broadcasted_iota(jnp.int32, (labels.shape[0], columns), 1)
    ).astype(jnp.bfloat16)


def pack_rows(payload, slot_ids, slot_total):
    select = one_hot(slot_ids, slot_total)
    packed = lax.dot_general(
        select, payload, (((0,), (0,)), ((), ())), preferred_element_type=jnp.float32
    )
    return packed.astype(jnp.bfloat16)


def placement(all_owner, all_page, owner_self, req_dev, slot_cap, seq_count):
    slot_total = slot_cap * seq_count
    slot_ids = pair_slots(all_owner.reshape(seq_count, req_dev), slot_cap).reshape(-1)
    source = lax.broadcasted_iota(jnp.int32, (seq_count, req_dev), 0).reshape(-1)
    column = source * slot_cap + slot_ids - all_owner * slot_cap
    target = jnp.where(all_owner == owner_self, all_page, -1)
    to_page = one_hot(target, slot_total)
    from_column = one_hot(column, slot_total)
    placing = lax.dot_general(
        to_page, from_column, (((0,), (0,)), ((), ())), preferred_element_type=jnp.float32
    )
    return placing.astype(jnp.bfloat16)


def local(draft_features, w_key, w_value, accepted, owner_group, page_slot):
    req_dev = accepted.shape[0]
    draft_rows = draft_features.shape[0] // req_dev
    head_cols = w_key.shape[1]
    seq_count = lax.axis_size("seq")
    owner_self = lax.axis_index("seq")
    slot_cap = max(2, 2 * req_dev // seq_count)
    slot_total = slot_cap * seq_count
    send_slots = pair_slots(owner_group, slot_cap)
    live_rows = lax.broadcasted_iota(jnp.int32, (req_dev, draft_rows), 1) < accepted[:, None]
    all_owner, all_page = turned_gather((owner_group, page_slot), "seq", (0, 0))
    placing = placement(all_owner, all_page, owner_self, req_dev, slot_cap, seq_count)
    portion = lax.all_gather(draft_features, "head", axis=1, tiled=True)
    key_sum = jnp.dot(portion, w_key, preferred_element_type=jnp.float32)
    value_sum = jnp.dot(portion, w_value, preferred_element_type=jnp.float32)
    key_local = jnp.where(
        live_rows[:, :, None], key_sum.reshape(req_dev, draft_rows, head_cols), 0.0
    )
    value_local = jnp.where(
        live_rows[:, :, None], value_sum.reshape(req_dev, draft_rows, head_cols), 0.0
    )
    key_local = key_local.astype(jnp.bfloat16).reshape(req_dev, draft_rows * head_cols)
    value_local = value_local.astype(jnp.bfloat16).reshape(req_dev, draft_rows * head_cols)
    key_send = pack_rows(key_local, send_slots, slot_total)
    value_send = pack_rows(value_local, send_slots, slot_total)
    key_arrived, value_arrived = (
        lax.all_to_all(key_send, "seq", split_axis=0, concat_axis=0, tiled=True),
        lax.all_to_all(value_send, "seq", split_axis=0, concat_axis=0, tiled=True),
    )
    key_cache = jnp.dot(placing, key_arrived, preferred_element_type=jnp.float32).astype(
        jnp.bfloat16
    )
    value_cache = jnp.dot(placing, value_arrived, preferred_element_type=jnp.float32).astype(
        jnp.bfloat16
    )
    return (
        key_cache.reshape(slot_total, draft_rows, head_cols),
        value_cache.reshape(slot_total, draft_rows, head_cols),
    )


def solution(mesh):
    placed = (
        P(("grp", "seq"), "head"),
        P(None, "head"),
        P(None, "head"),
        P(("grp", "seq")),
        P(("grp", "seq")),
        P(("grp", "seq")),
    )
    return jax.shard_map(
        local,
        mesh=mesh,
        in_specs=placed,
        out_specs=(P(("grp", "seq"), None, "head"), P(("grp", "seq"), None, "head")),
        check_vma=False,
    )
```

profile of v0, /device:TPU:65, one launch (start us, length us, event | category | flops | bytes accessed | tf_op | source)
XLA Modules:
  0.0 168.6 jit_solution(16775143756500642981)
XLA Ops:
  7.2 0.0 copy-start
  7.2 0.1 all-gather.3.cloned.1.call-start
  7.3 0.7 all-gather.3.cloned.1.call-update
  8.0 0.1 mul.28
  8.1 0.7 add_bitcast_fusion
  8.8 70.2 %all-gather = s32[32,32,2]{1,2,0:T(2,128)S(1)} all-gather(s32[1,32,2]{1,2,0:T(2,128)S(1)} %add_bitcast_fusion), channel_id=1, replica_groups=mesh['grp'=2,'seq'=32,'head'=8] {'seq'}, dimensions={0}, use_global_device_ids=true | all-gather | bytes 8448 | tf_op jit(solution)/shard_map/all_gather | solution.py:10
  79.0 0.1 reshape.89
  79.1 0.1 eq.72
  79.1 0.8 select_reduce_fusion
  79.9 0.1 reduce_sum.21
  80.0 0.9 select_reduce_fusion.1
  80.9 0.7 multiply_add_fusion
  81.6 0.7 iota_compare_fusion.4
  82.3 23.1 %all-gather.3.cloned.1.call-done = bf16[256,8192]{1,0:T(8,128)(2,1)} async-done(((bf16[256,1024]{1,0:T(8,128)(2,1)}), bf16[256,8192]{1,0:T(8,128)(2,1)}) %all-gather.3.cloned.1.call-update) | async-done | bytes 4194320 | tf_op jit(solution)/shard_map/all_gather | solution.py:68
  105.4 3.4 %fusion.11 = bf16[256,128]{1,0:T(8,128)(2,1)S(1)} fusion(bf16[256,8192]{1,0:T(8,128)(2,1)} %all-gather.3.cloned.1.call-done, bf16[8192,128]{1,0:T(8,128)(2,1)S(1)} %copy-done), kind=kOutput, calls=%fused_computation.31 | convolution fusion | flops 536870912 | bytes 6356992 | tf_op jit(solution)/shard_map/dot_general | solution.py:70
  108.9 0.1 broadcast_in_dim.53
  109.0 0.3 convolution_convert_fusion.2
  109.3 0.7 all_to_all.19
  110.0 14.0 %all-to-all-start.1 = ((bf16[32,2,1024]{2,1,0:T(2,128)(2,1)}), bf16[32,2,1024]{2,1,0:T(2,128)(2,1)S(1)}, u32[]{:S(2)}, u32[]{:S(2)}) async-start(bf16[32,2,1024]{2,1,0:T(2,128)(2,1)} %all_to_all.19), calls=%async_computation.1 | async-start | bytes 262144 | tf_op jit(solution)/shard_map/all_to_all | solution.py:83
  124.0 4.1 %fusion.10 = bf16[256,128]{1,0:T(8,128)(2,1)S(1)} fusion(bf16[256,8192]{1,0:T(8,128)(2,1)} %all-gather.3.cloned.1.call-done, bf16[8192,128]{1,0:T(8,128)(2,1)} %param.7), kind=kOutput, calls=%fused_computation.30 | convolution fusion | flops 536870912 | bytes 6356992 | tf_op jit(solution)/shard_map/dot_general | solution.py:69
  128.1 0.3 convolution_convert_fusion.3
  128.4 0.7 all_to_all.16
  129.2 10.4 %all-to-all-done.1 = bf16[32,2,1024]{2,1,0:T(2,128)(2,1)S(1)} async-done(((bf16[32,2,1024]{2,1,0:T(2,128)(2,1)}), bf16[32,2,1024]{2,1,0:T(2,128)(2,1)S(1)}, u32[]{:S(2)}, u32[]{:S(2)}) %all-to-all-start.1) | async-done | bytes 131104 | tf_op jit(solution)/shard_map/all_to_all | solution.py:83
  139.6 5.4 %all-to-all-start = ((bf16[32,2,1024]{2,1,0:T(2,128)(2,1)}), bf16[32,2,1024]{2,1,0:T(2,128)(2,1)S(1)}, u32[]{:S(2)}, u32[]{:S(2)}) async-start(bf16[32,2,1024]{2,1,0:T(2,128)(2,1)} %all_to_all.16), calls=%async_computation | async-start | bytes 262144 | tf_op jit(solution)/shard_map/all_to_all | solution.py:82
  145.0 0.6 convolution_convert_fusion.4
  145.6 0.1 all_to_all.21
  145.6 0.2 fusion.1
  145.8 0.7 copy.13
  146.5 14.4 %all-to-all-done = bf16[32,2,1024]{2,1,0:T(2,128)(2,1)S(1)} async-done(((bf16[32,2,1024]{2,1,0:T(2,128)(2,1)}), bf16[32,2,1024]{2,1,0:T(2,128)(2,1)S(1)}, u32[]{:S(2)}, u32[]{:S(2)}) %all-to-all-start) | async-done | bytes 131104 | tf_op jit(solution)/shard_map/all_to_all | solution.py:82
  160.9 0.1 all_to_all.18
  160.9 0.2 fusion
  161.1 0.7 copy.12
  (8 shorter events, 0.1 us)
Async XLA Ops:
  7.2 98.2 %copy-start = (bf16[8192,128]{1,0:T(8,128)(2,1)S(1)}, bf16[8192,128]{1,0:T(8,128)(2,1)}, u32[]{:S(2)}) copy-start(bf16[8192,128]{1,0:T(8,128)(2,1)} %param.8) | copy-start | bytes 6291460
  7.2 98.2 %all-gather.3.cloned.1.call-start = ((), (), s32[]{:S(2)}) async-start(), calls=%async_computation.2 | async-start | bytes 4718592 | tf_op jit(solution)/shard_map/all_gather | solution.py:68
  110.0 29.6 %all-to-all-start.1 = ((bf16[32,2,1024]{2,1,0:T(2,128)(2,1)}), bf16[32,2,1024]{2,1,0:T(2,128)(2,1)S(1)}, u32[]{:S(2)}, u32[]{:S(2)}) async-start(bf16[32,2,1024]{2,1,0:T(2,128)(2,1)} %all_to_all.19), calls=%async_computation.1 | async-start | bytes 262144 | tf_op jit(solution)/shard_map/all_to_all | solution.py:83
  139.6 21.3 %all-to-all-start = ((bf16[32,2,1024]{2,1,0:T(2,128)(2,1)}), bf16[32,2,1024]{2,1,0:T(2,128)(2,1)S(1)}, u32[]{:S(2)}, u32[]{:S(2)}) async-start(bf16[32,2,1024]{2,1,0:T(2,128)(2,1)} %all_to_all.16), calls=%async_computation | async-start | bytes 262144 | tf_op jit(solution)/shard_map/all_to_all | solution.py:82
Sparse Core Ops, SparseCore 0:
  10.1 95.2 all-gather.2
where the time goes:
time: 169 us
  blocking collectives  70.2 us (42%)
  waiting for transfers between devices  48.6 us (29%)
  starting transfers between devices  19.4 us (11%)
  between operations  14.2 us (8%)
  matrix products  9.04 us (5%)
  other arithmetic  3.82 us (2%)
  local copies, waits for them, and re-layouts  3.37 us (2%)
    all_gather x1, blocking collectives, turned_gather(): lax.all_gather(both, axis, axis=0, tiled=True)  70.2 us
    all_gather x1, waiting for transfers between devices, local(): portion = lax.all_gather(draft_features, 'head', axis=1, tiled=True)  23.1 us
    all_to_all x1, waiting for transfers between devices, local(): lax.all_to_all(key_send, 'seq', split_axis=0, concat_axis=0, tiled=True)  14.4 us
    all_to_all x1, starting transfers between devices, local(): lax.all_to_all(value_send, 'seq', split_axis=0, concat_axis=0, tiled=True)  14 us
    all_to_all x1, waiting for transfers between devices, local(): lax.all_to_all(value_send, 'seq', split_axis=0, concat_axis=0, tiled=True)  10.4 us
    all_to_all x1, starting transfers between devices, local(): lax.all_to_all(key_send, 'seq', split_axis=0, concat_axis=0, tiled=True)  5.39 us
    dot_general x1, matrix products, local(): key_sum = jnp.dot(portion, w_key, preferred_element_type=jnp.float32)  4.11 us
    dot_general x1, matrix products, local(): value_sum = jnp.dot(portion, w_value, preferred_element_type=jnp.float32)  3.43 us
  transfers between devices with their start and end apart: 3, of which 3 were waited for; matrix products, arithmetic and copies ran while one was open for 6% of the time, Pallas kernels for 0%

commit v1 on v0

v1 whole, which is shorter than its diff:
```python
import functools

import jax
import jax.numpy as jnp
from jax import lax
from jax.experimental import pallas as pl
from jax.experimental.pallas import tpu as pltpu
from jax.sharding import PartitionSpec as P

CHUNKS = 2


def gather_ring(block):
    heads = lax.axis_size("head")
    up = [(i, (i + 1) % heads) for i in range(heads)]
    down = [(i, (i - 1) % heads) for i in range(heads)]
    own = jnp.split(block, CHUNKS, axis=0)
    held = [(0, own)]
    rising, falling = list(own), list(own)
    for step in range(1, (heads + 1) // 2):
        for c in range(CHUNKS):
            rising[c] = lax.ppermute(rising[c], "head", up)
            falling[c] = lax.ppermute(falling[c], "head", down)
        held.append((heads - step, list(rising)))
        held.append((step, list(falling)))
    if heads % 2 == 0:
        last = [
            lax.ppermute(rising[c], "head", up) if c % 2 == 0 else lax.ppermute(falling[c], "head", down)
            for c in range(CHUNKS)
        ]
        held.append((heads // 2, last))
    return held


def iota(shape, dim):
    return lax.broadcasted_iota(jnp.int32, shape, dim)


def project_pack_kernel(offsets, slot_cap, draft, me_ref, route_ref, *refs):
    blocks = refs[: len(offsets) * CHUNKS]
    wk_ref, wv_ref, out_ref = refs[len(offsets) * CHUNKS :]
    depth = blocks[0].shape[1]
    heads = len(offsets)
    total = None
    for i, offset in enumerate(offsets):
        rows = jnp.concatenate([b[...] for b in blocks[i * CHUNKS : (i + 1) * CHUNKS]], axis=0)
        origin = lax.rem(me_ref[0] + offset, heads)
        at = pl.ds(pl.multiple_of(origin * depth, depth), depth)
        weights = jnp.concatenate([wk_ref[at, :], wv_ref[at, :]], axis=1)
        part = jnp.dot(rows, weights, preferred_element_type=jnp.float32)
        total = part if total is None else total + part
    projected = total.astype(jnp.bfloat16)
    req = route_ref.shape[1]
    accepted = route_ref[0:1, :].astype(jnp.float32)
    owner = route_ref[1:2, :].astype(jnp.float32)
    page = route_ref[2:3, :].astype(jnp.float32)
    diagonal = iota((req, req), 0) == iota((req, req), 1)
    owner_col = jnp.sum(jnp.where(diagonal, owner, 0.0), axis=1, keepdims=True)
    earlier = (owner_col == owner) & (iota((req, req), 0) < iota((req, req), 1))
    within = jnp.sum(jnp.where(earlier, 1.0, 0.0), axis=0, keepdims=True)
    slot = owner * slot_cap + within
    row_count = req * draft
    lane, sub = iota((req, row_count), 1), iota((req, row_count), 0)
    mine = (lane >= sub * draft) & (lane < sub * draft + draft)
    slot_col = jnp.sum(jnp.where(diagonal, slot, 0.0), axis=1, keepdims=True)
    accepted_col = jnp.sum(jnp.where(diagonal, accepted, 0.0), axis=1, keepdims=True)
    draft_row = (lane - sub * draft).astype(jnp.float32)
    wanted = jnp.where(
        mine & (draft_row < accepted_col), slot_col * draft + draft_row + 1.0, 0.0
    )
    target = jnp.sum(wanted, axis=0, keepdims=True) - 1.0
    owners = out_ref.shape[0]
    slots = owners * slot_cap
    select = jnp.where(
        iota((slots * draft, row_count), 0).astype(jnp.float32) == target, 1.0, 0.0
    ).astype(jnp.bfloat16)
    packed = jnp.dot(select, projected, preferred_element_type=jnp.float32).astype(jnp.bfloat16)
    head_cols = wk_ref.shape[1]
    span = slot_cap * draft
    out_ref[:, 0:span, :] = packed[:, :head_cols].reshape(owners, span, head_cols)
    out_ref[:, span : 2 * span, :] = packed[:, head_cols:].reshape(owners, span, head_cols)
    part_lanes = head_cols // slot_cap
    dest = lax.div(iota((owners * draft, req), 0), draft).astype(jnp.float32)
    note_lane = iota((owners * draft, head_cols), 1)
    notes = jnp.full((owners * draft, head_cols), -1.0, jnp.float32)
    for s in range(slot_cap):
        found = jnp.sum(
            jnp.where(dest * slot_cap + s == slot, page + 1.0, 0.0), axis=1, keepdims=True
        ) - 1.0
        notes = jnp.where(note_lane >= s * part_lanes, found, notes)
    out_ref[:, 2 * span :, :] = notes.astype(jnp.bfloat16).reshape(owners, draft, head_cols)


def place_kernel(slot_cap, arrived_ref, key_ref, value_ref):
    sources, _, head_cols = arrived_ref.shape
    pages, draft, _ = key_ref.shape
    span = slot_cap * draft
    rows = sources * draft
    part_lanes = head_cols // slot_cap
    notes = arrived_ref[:, 2 * span :, :].reshape(rows, head_cols).astype(jnp.float32)
    draft_row = lax.rem(iota((rows, 1), 0), draft).astype(jnp.float32)
    spot = iota((rows, pages * draft), 1).astype(jnp.float32)
    total = None
    for s in range(slot_cap):
        page = notes[:, s * part_lanes : s * part_lanes + 1]
        goes = jnp.where(page >= 0.0, page * draft + draft_row, -1.0)
        select = jnp.where(goes == spot, 1.0, 0.0).astype(jnp.bfloat16)
        keys = arrived_ref[:, s * draft : (s + 1) * draft, :].reshape(rows, head_cols)
        values = arrived_ref[:, span + s * draft : span + (s + 1) * draft, :].reshape(rows, head_cols)
        both = jnp.concatenate([keys, values], axis=1)
        part = lax.dot_general(
            select, both, (((0,), (0,)), ((), ())), preferred_element_type=jnp.float32
        )
        total = part if total is None else total + part
    placed = total.astype(jnp.bfloat16)
    key_ref[...] = placed[:, :head_cols].reshape(pages, draft, head_cols)
    value_ref[...] = placed[:, head_cols:].reshape(pages, draft, head_cols)


def local(draft_features, w_key, w_value, accepted, owner_group, page_slot):
    req_dev = accepted.shape[0]
    draft = draft_features.shape[0] // req_dev
    depth = draft_features.shape[1]
    head_cols = w_key.shape[1]
    seq_count = lax.axis_size("seq")
    slot_cap = max(2, 2 * req_dev // seq_count)
    slot_total = slot_cap * seq_count
    route = jnp.stack([accepted, owner_group, page_slot])
    me = lax.axis_index("head").astype(jnp.int32).reshape(1)
    held = gather_ring(draft_features)
    offsets = tuple(offset for offset, _ in held)
    blocks = [b for _, chunks in held for b in chunks]
    vmem = pl.BlockSpec(memory_space=pltpu.VMEM)
    note_rows = 2 * slot_cap * draft + draft
    packed = pl.pallas_call(
        functools.partial(project_pack_kernel, offsets, slot_cap, draft),
        out_shape=jax.ShapeDtypeStruct((seq_count, note_rows, head_cols), jnp.bfloat16),
        in_specs=[pl.BlockSpec(memory_space=pltpu.SMEM), vmem] + [vmem] * (len(blocks) + 2),
        out_specs=vmem,
        cost_estimate=pl.CostEstimate(
            flops=4 * req_dev * draft * depth * len(offsets) * head_cols,
            bytes_accessed=2 * (req_dev * draft + 2 * head_cols) * depth * len(offsets),
            transcendentals=0,
        ),
        name="project_pack",
    )(me, route, *blocks, w_key, w_value)
    arrived = lax.all_to_all(packed, "seq", split_axis=0, concat_axis=0, tiled=True)
    cache = jax.ShapeDtypeStruct((slot_total, draft, head_cols), jnp.bfloat16)
    return pl.pallas_call(
        functools.partial(place_kernel, slot_cap),
        out_shape=(cache, cache),
        in_specs=[vmem],
        out_specs=(vmem, vmem),
        name="place",
    )(arrived)


def solution(mesh):
    placed = (
        P(("grp", "seq"), "head"),
        P(None, "head"),
        P(None, "head"),
        P(("grp", "seq")),
        P(("grp", "seq")),
        P(("grp", "seq")),
    )
    return jax.shard_map(
        local,
        mesh=mesh,
        in_specs=placed,
        out_specs=(P(("grp", "seq"), None, "head"), P(("grp", "seq"), None, "head")),
        check_vma=False,
    )
```

time: 169 us -> 135 us (0.80)
  waiting for transfers between devices: 48.6 us -> 6.69 us
  starting transfers between devices: 19.4 us -> 43.9 us
  between operations: 14.2 us -> 1.01 us
  matrix products: 9.04 us -> 0 us
  Pallas kernels: 0 us -> 7.99 us
  other arithmetic: 3.82 us -> 1.28 us
  blocking collectives: 70.2 us -> 72.6 us
  local copies, waits for them, and re-layouts: 3.37 us -> 1.12 us
    all_to_all x0 -> x1, blocking collectives: none -> 72.6 us  [local(): lax.all_to_all(packed, 'seq', split_axis=0, concat_axis=0, tiled=True)]
    all_gather x1 -> x0, blocking collectives: 70.2 us -> none  [turned_gather(): lax.all_gather(both, axis, axis=0, tiled=True)]
    ppermute x0 -> x14, starting transfers between devices: none -> 43.9 us  [the longest x6 26.9 us: gather_ring(): falling[c] = lax.ppermute(falling[c], 'head', down)]
    all_to_all x2 -> x0, waiting for transfers between devices: 24.8 us -> none  [the longest x1 14.4 us: local(): lax.all_to_all(key_send, 'seq', split_axis=0, concat_axis=0, tiled=True)]
    all_gather x1 -> x0, waiting for transfers between devices: 23.1 us -> none  [local(): portion = lax.all_gather(draft_features, 'head', axis=1, tiled=True)]
    all_to_all x2 -> x0, starting transfers between devices: 19.4 us -> none  [the longest x1 14 us: local(): lax.all_to_all(value_send, 'seq', split_axis=0, concat_axis=0, tiled=True)]
    dot_general x7 -> x0, matrix products: 9.04 us -> none  [the longest x1 4.11 us: local(): key_sum = jnp.dot(portion, w_key, preferred_element_type=jnp.float32)]
    pallas_call x0 -> x2, Pallas kernels: none -> 7.99 us  [the longest x1 5.82 us: local(): pl.pallas_call(functools.partial(project_pack_kernel, offsets, slot_cap,...]
  transfers between devices with their start and end apart: 3 -> 14, of which waited for: 3 -> 2; matrix products, arithmetic and copies ran while one was open for 6% -> 1% of each run, Pallas kernels for 0% -> 0%
where the time goes in v1:
time: 135 us
  blocking collectives  72.6 us (54%)
  starting transfers between devices  43.9 us (33%)
  Pallas kernels  7.99 us (6%)
  waiting for transfers between devices  6.69 us (5%)
    all_to_all x1, blocking collectives, local(): lax.all_to_all(packed, 'seq', split_axis=0, concat_axis=0, tiled=True)  72.6 us
    ppermute x6, starting transfers between devices, gather_ring(): falling[c] = lax.ppermute(falling[c], 'head', down)  26.9 us
    ppermute x6, starting transfers between devices, gather_ring(): rising[c] = lax.ppermute(rising[c], 'head', up)  11.7 us
    pallas_call x1, Pallas kernels, local(): pl.pallas_call(functools.partial(project_pack_kernel, offsets, slot_cap,...  5.82 us
    ppermute x1, waiting for transfers between devices, gather_ring(): lax.ppermute(rising[c], 'head', up)  5.12 us
    ppermute x1, starting transfers between devices, gather_ring(): lax.ppermute(falling[c], 'head', down)  3.39 us
  transfers between devices with their start and end apart: 14, of which 2 were waited for; matrix products, arithmetic and copies ran while one was open for 1% of the time, Pallas kernels for 0%

profile of v1, /device:TPU:65, one launch (start us, length us, event | category | flops | bytes accessed | tf_op | source)
XLA Modules:
  0.0 134.6 jit_solution(104909982803460271)
XLA Ops:
  0.6 1.1 fusion
  1.7 6.3 %collective-permute-start.3 = (bf16[128,1024]{1,0:T(8,128)(2,1)S(1)}, bf16[128,1024]{1,0:T(8,128)(2,1)S(1)}, u32[]{:S(2)}, u32[]{:S(2)}) collective-permute-start(bf16[128,1024]{1,0:T(8,128)(2,1)S(1)} %get-tuple-element.2.refs_1_), channel_id=1, source_target_pairs={{0,7},{1,0},{2,1},{3,2},{4,3},{5,4},{6,5},{7,6},{8,15},{9,8},{10,9... | collective-permute-start | bytes 786440 | tf_op jit(solution)/shard_map/ppermute | solution.py:23
  8.0 2.0 %collective-permute-start = (bf16[128,1024]{1,0:T(8,128)(2,1)S(1)}, bf16[128,1024]{1,0:T(8,128)(2,1)S(1)}, u32[]{:S(2)}, u32[]{:S(2)}) collective-permute-start(bf16[128,1024]{1,0:T(8,128)(2,1)S(1)} %get-tuple-element.3.refs_0_), channel_id=1, source_target_pairs={{0,1},{1,2},{2,3},{3,4},{4,5},{5,6},{6,7},{7,0},{8,9},{9,10},{10,1... | collective-permute-start | bytes 786440 | tf_op jit(solution)/shard_map/ppermute | solution.py:22
  10.0 2.0 %collective-permute-start.1 = (bf16[128,1024]{1,0:T(8,128)(2,1)S(1)}, bf16[128,1024]{1,0:T(8,128)(2,1)S(1)}, u32[]{:S(2)}, u32[]{:S(2)}) collective-permute-start(bf16[128,1024]{1,0:T(8,128)(2,1)S(1)} %get-tuple-element.2.refs_1_), channel_id=1, source_target_pairs={{0,1},{1,2},{2,3},{3,4},{4,5},{5,6},{6,7},{7,0},{8,9},{9,10},{10,1... | collective-permute-start | bytes 786440 | tf_op jit(solution)/shard_map/ppermute | solution.py:22
  11.9 4.6 %collective-permute-start.2 = (bf16[128,1024]{1,0:T(8,128)(2,1)S(1)}, bf16[128,1024]{1,0:T(8,128)(2,1)S(1)}, u32[]{:S(2)}, u32[]{:S(2)}) collective-permute-start(bf16[128,1024]{1,0:T(8,128)(2,1)S(1)} %get-tuple-element.3.refs_0_), channel_id=1, source_target_pairs={{0,7},{1,0},{2,1},{3,2},{4,3},{5,4},{6,5},{7,6},{8,15},{9,8},{10,9... | collective-permute-start | bytes 786440 | tf_op jit(solution)/shard_map/ppermute | solution.py:23
  16.6 0.0 collective-permute-done.3.refs_5_
  16.6 3.4 %collective-permute-start.7 = (bf16[128,1024]{1,0:T(8,128)(2,1)S(1)}, bf16[128,1024]{1,0:T(8,128)(2,1)S(1)}, u32[]{:S(2)}, u32[]{:S(2)}) collective-permute-start(bf16[128,1024]{1,0:T(8,128)(2,1)S(1)} %collective-permute-done.3.refs_5_), channel_id=1, source_target_pairs={{0,7},{1,0},{2,1},{3,2},{4,3},{5,4},{6,5},{7,6},{8,15},{9,8},{10,9... | collective-permute-start | bytes 786440 | tf_op jit(solution)/shard_map/ppermute | solution.py:23
  20.0 0.0 collective-permute-done.refs_2_
  20.0 2.0 %collective-permute-start.4 = (bf16[128,1024]{1,0:T(8,128)(2,1)S(1)}, bf16[128,1024]{1,0:T(8,128)(2,1)S(1)}, u32[]{:S(2)}, u32[]{:S(2)}) collective-permute-start(bf16[128,1024]{1,0:T(8,128)(2,1)S(1)} %collective-permute-done.refs_2_), channel_id=1, source_target_pairs={{0,1},{1,2},{2,3},{3,4},{4,5},{5,6},{6,7},{7,0},{8,9},{9,10},{10,1... | collective-permute-start | bytes 786440 | tf_op jit(solution)/shard_map/ppermute | solution.py:22
  22.0 0.0 collective-permute-done.1.refs_3_
  22.0 2.0 %collective-permute-start.5 = (bf16[128,1024]{1,0:T(8,128)(2,1)S(1)}, bf16[128,1024]{1,0:T(8,128)(2,1)S(1)}, u32[]{:S(2)}, u32[]{:S(2)}) collective-permute-start(bf16[128,1024]{1,0:T(8,128)(2,1)S(1)} %collective-permute-done.1.refs_3_), channel_id=1, source_target_pairs={{0,1},{1,2},{2,3},{3,4},{4,5},{5,6},{6,7},{7,0},{8,9},{9,10},{10,1... | collective-permute-start | bytes 786440 | tf_op jit(solution)/shard_map/ppermute | solution.py:22
  23.9 0.0 collective-permute-done.2.refs_4_
  24.0 4.6 %collective-permute-start.6 = (bf16[128,1024]{1,0:T(8,128)(2,1)S(1)}, bf16[128,1024]{1,0:T(8,128)(2,1)S(1)}, u32[]{:S(2)}, u32[]{:S(2)}) collective-permute-start(bf16[128,1024]{1,0:T(8,128)(2,1)S(1)} %collective-permute-done.2.refs_4_), channel_id=1, source_target_pairs={{0,7},{1,0},{2,1},{3,2},{4,3},{5,4},{6,5},{7,6},{8,15},{9,8},{10,9... | collective-permute-start | bytes 786440 | tf_op jit(solution)/shard_map/ppermute | solution.py:23
  28.6 0.0 collective-permute-done.7.refs_9_
  28.6 3.4 %collective-permute-start.11 = (bf16[128,1024]{1,0:T(8,128)(2,1)S(1)}, bf16[128,1024]{1,0:T(8,128)(2,1)S(1)}, u32[]{:S(2)}, u32[]{:S(2)}) collective-permute-start(bf16[128,1024]{1,0:T(8,128)(2,1)S(1)} %collective-permute-done.7.refs_9_), channel_id=1, source_target_pairs={{0,7},{1,0},{2,1},{3,2},{4,3},{5,4},{6,5},{7,6},{8,15},{9,8},{10,9... | collective-permute-start | bytes 786440 | tf_op jit(solution)/shard_map/ppermute | solution.py:23
  32.0 0.0 collective-permute-done.4.refs_6_
  32.0 2.0 %collective-permute-start.8 = (bf16[128,1024]{1,0:T(8,128)(2,1)S(1)}, bf16[128,1024]{1,0:T(8,128)(2,1)S(1)}, u32[]{:S(2)}, u32[]{:S(2)}) collective-permute-start(bf16[128,1024]{1,0:T(8,128)(2,1)S(1)} %collective-permute-done.4.refs_6_), channel_id=1, source_target_pairs={{0,1},{1,2},{2,3},{3,4},{4,5},{5,6},{6,7},{7,0},{8,9},{9,10},{10,1... | collective-permute-start | bytes 786440 | tf_op jit(solution)/shard_map/ppermute | solution.py:22
  34.0 0.0 collective-permute-done.5.refs_7_
  34.0 2.0 %collective-permute-start.9 = (bf16[128,1024]{1,0:T(8,128)(2,1)S(1)}, bf16[128,1024]{1,0:T(8,128)(2,1)S(1)}, u32[]{:S(2)}, u32[]{:S(2)}) collective-permute-start(bf16[128,1024]{1,0:T(8,128)(2,1)S(1)} %collective-permute-done.5.refs_7_), channel_id=1, source_target_pairs={{0,1},{1,2},{2,3},{3,4},{4,5},{5,6},{6,7},{7,0},{8,9},{9,10},{10,1... | collective-permute-start | bytes 786440 | tf_op jit(solution)/shard_map/ppermute | solution.py:22
  35.9 0.0 collective-permute-done.6.refs_8_
  36.0 4.6 %collective-permute-start.10 = (bf16[128,1024]{1,0:T(8,128)(2,1)S(1)}, bf16[128,1024]{1,0:T(8,128)(2,1)}, u32[]{:S(2)}, u32[]{:S(2)}) collective-permute-start(bf16[128,1024]{1,0:T(8,128)(2,1)S(1)} %collective-permute-done.6.refs_8_), channel_id=1, source_target_pairs={{0,7},{1,0},{2,1},{3,2},{4,3},{5,4},{6,5},{7,6},{8,15},{9,8},{10,9... | collective-permute-start | bytes 786440 | tf_op jit(solution)/shard_map/ppermute | solution.py:23
  40.6 3.4 %collective-permute-start.13 = (bf16[128,1024]{1,0:T(8,128)(2,1)S(1)}, bf16[128,1024]{1,0:T(8,128)(2,1)}, u32[]{:S(2)}, u32[]{:S(2)}) collective-permute-start(bf16[128,1024]{1,0:T(8,128)(2,1)S(1)} %collective-permute-done.11.refs_13_), channel_id=1, source_target_pairs={{0,7},{1,0},{2,1},{3,2},{4,3},{5,4},{6,5},{7,6},{8,15},{9,8},{10,9... | collective-permute-start | bytes 786440 | tf_op jit(solution)/shard_map/ppermute | solution.py:28
  44.0 0.0 collective-permute-done.8.refs_10_
  44.0 2.0 %collective-permute-start.12 = (bf16[128,1024]{1,0:T(8,128)(2,1)S(1)}, bf16[128,1024]{1,0:T(8,128)(2,1)}, u32[]{:S(2)}, u32[]{:S(2)}) collective-permute-start(bf16[128,1024]{1,0:T(8,128)(2,1)S(1)} %collective-permute-done.8.refs_10_), channel_id=1, source_target_pairs={{0,1},{1,2},{2,3},{3,4},{4,5},{5,6},{6,7},{7,0},{8,9},{9,10},{10,1... | collective-permute-start | bytes 786440 | tf_op jit(solution)/shard_map/ppermute | solution.py:28
  46.0 1.3 pad_add_fusion.route_ref
  47.3 0.0 collective-permute-done.9.refs_11_
  47.3 0.0 collective-permute-done.10.refs_12_
  47.3 1.5 %collective-permute-done.13.refs_15_ = bf16[128,1024]{1,0:T(8,128)(2,1)} collective-permute-done((bf16[128,1024]{1,0:T(8,128)(2,1)S(1)}, bf16[128,1024]{1,0:T(8,128)(2,1)}, u32[]{:S(2)}, u32[]{:S(2)}) %collective-permute-start.13) | collective-permute-done | bytes 262176 | tf_op jit(solution)/shard_map/ppermute | solution.py:28
  48.8 5.1 %collective-permute-done.12.refs_14_ = bf16[128,1024]{1,0:T(8,128)(2,1)} collective-permute-done((bf16[128,1024]{1,0:T(8,128)(2,1)S(1)}, bf16[128,1024]{1,0:T(8,128)(2,1)}, u32[]{:S(2)}, u32[]{:S(2)}) %collective-permute-start.12) | collective-permute-done | bytes 262176 | tf_op jit(solution)/shard_map/ppermute | solution.py:28
  54.0 5.8 %project_pack.1 = bf16[32,40,128]{2,1,0:T(8,128)(2,1)} custom-call(s32[1]{0:T(128)} %bitcast.me_ref, s32[3,32]{1,0:T(4,128)} %pad_add_fusion.route_ref, bf16[128,1024]{1,0:T(8,128)(2,1)} %copy-done.1, bf16[128,1024]{1,0:T(8,128)(2,1)} %copy-done, bf16[128,1024]{1,0:T(8,128)(2,1)} %copy-done.3, bf16[128,1024]{1,0:T(8,128)(2,1)} %copy-done.4, ...), custom_call_target="tpu_custom_call" | custom-call | flops 1073741824 | bytes 8388608 | tf_op jit(solution)/shard_map/project_pack/pallas_call | solution.py:135
  59.9 72.6 %all_to_all.5.arrived_ref = bf16[32,40,128]{2,1,0:T(8,128)(2,1)} all-to-all(bf16[32,40,128]{2,1,0:T(8,128)(2,1)} %project_pack.1), channel_id=1, replica_groups=mesh['grp'=2,'seq'=32,'head'=8] {'seq'}, dimensions={0} | all-to-all | bytes 655360 | tf_op jit(solution)/shard_map/all_to_all | solution.py:147
  132.5 2.2 %place.1 = (bf16[64,8,128]{2,1,0:T(8,128)(2,1)}, bf16[64,8,128]{2,1,0:T(8,128)(2,1)}) custom-call(bf16[32,40,128]{2,1,0:T(8,128)(2,1)} %all_to_all.5.arrived_ref), custom_call_target="tpu_custom_call" | custom-call | tf_op jit(solution)/shard_map/place/pallas_call | solution.py:149
  (27 shorter events, 0.1 us)
Async XLA Ops:
  1.7 52.2 %copy-start = (bf16[128,1024]{1,0:T(8,128)(2,1)}, bf16[128,1024]{1,0:T(8,128)(2,1)S(1)}, u32[]{:S(2)}) copy-start(bf16[128,1024]{1,0:T(8,128)(2,1)S(1)} %get-tuple-element.2.refs_1_) | copy-start | bytes 786436
  1.7 52.2 %copy-start.1 = (bf16[128,1024]{1,0:T(8,128)(2,1)}, bf16[128,1024]{1,0:T(8,128)(2,1)S(1)}, u32[]{:S(2)}) copy-start(bf16[128,1024]{1,0:T(8,128)(2,1)S(1)} %get-tuple-element.3.refs_0_) | copy-start | bytes 786436
  1.7 14.8 %collective-permute-start.3 = (bf16[128,1024]{1,0:T(8,128)(2,1)S(1)}, bf16[128,1024]{1,0:T(8,128)(2,1)S(1)}, u32[]{:S(2)}, u32[]{:S(2)}) collective-permute-start(bf16[128,1024]{1,0:T(8,128)(2,1)S(1)} %get-tuple-element.2.refs_1_), channel_id=1, source_target_pairs={{0,7},{1,0},{2,1},{3,2},{4,3},{5,4},{6,5},{7,6},{8,15},{9,8},{10,9... | collective-permute-start | bytes 786440 | tf_op jit(solution)/shard_map/ppermute | solution.py:23
  8.0 12.0 %collective-permute-start = (bf16[128,1024]{1,0:T(8,128)(2,1)S(1)}, bf16[128,1024]{1,0:T(8,128)(2,1)S(1)}, u32[]{:S(2)}, u32[]{:S(2)}) collective-permute-start(bf16[128,1024]{1,0:T(8,128)(2,1)S(1)} %get-tuple-element.3.refs_0_), channel_id=1, source_target_pairs={{0,1},{1,2},{2,3},{3,4},{4,5},{5,6},{6,7},{7,0},{8,9},{9,10},{10,1... | collective-permute-start | bytes 786440 | tf_op jit(solution)/shard_map/ppermute | solution.py:22
  10.0 12.0 %collective-permute-start.1 = (bf16[128,1024]{1,0:T(8,128)(2,1)S(1)}, bf16[128,1024]{1,0:T(8,128)(2,1)S(1)}, u32[]{:S(2)}, u32[]{:S(2)}) collective-permute-start(bf16[128,1024]{1,0:T(8,128)(2,1)S(1)} %get-tuple-element.2.refs_1_), channel_id=1, source_target_pairs={{0,1},{1,2},{2,3},{3,4},{4,5},{5,6},{6,7},{7,0},{8,9},{9,10},{10,1... | collective-permute-start | bytes 786440 | tf_op jit(solution)/shard_map/ppermute | solution.py:22
  11.9 12.0 %collective-permute-start.2 = (bf16[128,1024]{1,0:T(8,128)(2,1)S(1)}, bf16[128,1024]{1,0:T(8,128)(2,1)S(1)}, u32[]{:S(2)}, u32[]{:S(2)}) collective-permute-start(bf16[128,1024]{1,0:T(8,128)(2,1)S(1)} %get-tuple-element.3.refs_0_), channel_id=1, source_target_pairs={{0,7},{1,0},{2,1},{3,2},{4,3},{5,4},{6,5},{7,6},{8,15},{9,8},{10,9... | collective-permute-start | bytes 786440 | tf_op jit(solution)/shard_map/ppermute | solution.py:23
  16.6 37.4 %copy-start.2 = (bf16[128,1024]{1,0:T(8,128)(2,1)}, bf16[128,1024]{1,0:T(8,128)(2,1)S(1)}, u32[]{:S(2)}) copy-start(bf16[128,1024]{1,0:T(8,128)(2,1)S(1)} %collective-permute-done.3.refs_5_) | copy-start | bytes 786436
  16.6 12.0 %collective-permute-start.7 = (bf16[128,1024]{1,0:T(8,128)(2,1)S(1)}, bf16[128,1024]{1,0:T(8,128)(2,1)S(1)}, u32[]{:S(2)}, u32[]{:S(2)}) collective-permute-start(bf16[128,1024]{1,0:T(8,128)(2,1)S(1)} %collective-permute-done.3.refs_5_), channel_id=1, source_target_pairs={{0,7},{1,0},{2,1},{3,2},{4,3},{5,4},{6,5},{7,6},{8,15},{9,8},{10,9... | collective-permute-start | bytes 786440 | tf_op jit(solution)/shard_map/ppermute | solution.py:23
  20.0 34.0 %copy-start.3 = (bf16[128,1024]{1,0:T(8,128)(2,1)}, bf16[128,1024]{1,0:T(8,128)(2,1)S(1)}, u32[]{:S(2)}) copy-start(bf16[128,1024]{1,0:T(8,128)(2,1)S(1)} %collective-permute-done.refs_2_) | copy-start | bytes 786436
  20.0 12.0 %collective-permute-start.4 = (bf16[128,1024]{1,0:T(8,128)(2,1)S(1)}, bf16[128,1024]{1,0:T(8,128)(2,1)S(1)}, u32[]{:S(2)}, u32[]{:S(2)}) collective-permute-start(bf16[128,1024]{1,0:T(8,128)(2,1)S(1)} %collective-permute-done.refs_2_), channel_id=1, source_target_pairs={{0,1},{1,2},{2,3},{3,4},{4,5},{5,6},{6,7},{7,0},{8,9},{9,10},{10,1... | collective-permute-start | bytes 786440 | tf_op jit(solution)/shard_map/ppermute | solution.py:22
  22.0 32.0 %copy-start.4 = (bf16[128,1024]{1,0:T(8,128)(2,1)}, bf16[128,1024]{1,0:T(8,128)(2,1)S(1)}, u32[]{:S(2)}) copy-start(bf16[128,1024]{1,0:T(8,128)(2,1)S(1)} %collective-permute-done.1.refs_3_) | copy-start | bytes 786436
  22.0 12.0 %collective-permute-start.5 = (bf16[128,1024]{1,0:T(8,128)(2,1)S(1)}, bf16[128,1024]{1,0:T(8,128)(2,1)S(1)}, u32[]{:S(2)}, u32[]{:S(2)}) collective-permute-start(bf16[128,1024]{1,0:T(8,128)(2,1)S(1)} %collective-permute-done.1.refs_3_), channel_id=1, source_target_pairs={{0,1},{1,2},{2,3},{3,4},{4,5},{5,6},{6,7},{7,0},{8,9},{9,10},{10,1... | collective-permute-start | bytes 786440 | tf_op jit(solution)/shard_map/ppermute | solution.py:22
  23.9 30.0 %copy-start.5 = (bf16[128,1024]{1,0:T(8,128)(2,1)}, bf16[128,1024]{1,0:T(8,128)(2,1)S(1)}, u32[]{:S(2)}) copy-start(bf16[128,1024]{1,0:T(8,128)(2,1)S(1)} %collective-permute-done.2.refs_4_) | copy-start | bytes 786436
  24.0 12.0 %collective-permute-start.6 = (bf16[128,1024]{1,0:T(8,128)(2,1)S(1)}, bf16[128,1024]{1,0:T(8,128)(2,1)S(1)}, u32[]{:S(2)}, u32[]{:S(2)}) collective-permute-start(bf16[128,1024]{1,0:T(8,128)(2,1)S(1)} %collective-permute-done.2.refs_4_), channel_id=1, source_target_pairs={{0,7},{1,0},{2,1},{3,2},{4,3},{5,4},{6,5},{7,6},{8,15},{9,8},{10,9... | collective-permute-start | bytes 786440 | tf_op jit(solution)/shard_map/ppermute | solution.py:23
  28.6 25.4 %copy-start.6 = (bf16[128,1024]{1,0:T(8,128)(2,1)}, bf16[128,1024]{1,0:T(8,128)(2,1)S(1)}, u32[]{:S(2)}) copy-start(bf16[128,1024]{1,0:T(8,128)(2,1)S(1)} %collective-permute-done.7.refs_9_) | copy-start | bytes 786436
  28.6 12.0 %collective-permute-start.11 = (bf16[128,1024]{1,0:T(8,128)(2,1)S(1)}, bf16[128,1024]{1,0:T(8,128)(2,1)S(1)}, u32[]{:S(2)}, u32[]{:S(2)}) collective-permute-start(bf16[128,1024]{1,0:T(8,128)(2,1)S(1)} %collective-permute-done.7.refs_9_), channel_id=1, source_target_pairs={{0,7},{1,0},{2,1},{3,2},{4,3},{5,4},{6,5},{7,6},{8,15},{9,8},{10,9... | collective-permute-start | bytes 786440 | tf_op jit(solution)/shard_map/ppermute | solution.py:23
  32.0 22.0 %copy-start.7 = (bf16[128,1024]{1,0:T(8,128)(2,1)}, bf16[128,1024]{1,0:T(8,128)(2,1)S(1)}, u32[]{:S(2)}) copy-start(bf16[128,1024]{1,0:T(8,128)(2,1)S(1)} %collective-permute-done.4.refs_6_) | copy-start | bytes 786436
  32.0 12.0 %collective-permute-start.8 = (bf16[128,1024]{1,0:T(8,128)(2,1)S(1)}, bf16[128,1024]{1,0:T(8,128)(2,1)S(1)}, u32[]{:S(2)}, u32[]{:S(2)}) collective-permute-start(bf16[128,1024]{1,0:T(8,128)(2,1)S(1)} %collective-permute-done.4.refs_6_), channel_id=1, source_target_pairs={{0,1},{1,2},{2,3},{3,4},{4,5},{5,6},{6,7},{7,0},{8,9},{9,10},{10,1... | collective-permute-start | bytes 786440 | tf_op jit(solution)/shard_map/ppermute | solution.py:22
  34.0 20.0 %copy-start.8 = (bf16[128,1024]{1,0:T(8,128)(2,1)}, bf16[128,1024]{1,0:T(8,128)(2,1)S(1)}, u32[]{:S(2)}) copy-start(bf16[128,1024]{1,0:T(8,128)(2,1)S(1)} %collective-permute-done.5.refs_7_) | copy-start | bytes 786436
  34.0 13.3 %collective-permute-start.9 = (bf16[128,1024]{1,0:T(8,128)(2,1)S(1)}, bf16[128,1024]{1,0:T(8,128)(2,1)S(1)}, u32[]{:S(2)}, u32[]{:S(2)}) collective-permute-start(bf16[128,1024]{1,0:T(8,128)(2,1)S(1)} %collective-permute-done.5.refs_7_), channel_id=1, source_target_pairs={{0,1},{1,2},{2,3},{3,4},{4,5},{5,6},{6,7},{7,0},{8,9},{9,10},{10,1... | collective-permute-start | bytes 786440 | tf_op jit(solution)/shard_map/ppermute | solution.py:22
  36.0 18.1 %copy-start.9 = (bf16[128,1024]{1,0:T(8,128)(2,1)}, bf16[128,1024]{1,0:T(8,128)(2,1)S(1)}, u32[]{:S(2)}) copy-start(bf16[128,1024]{1,0:T(8,128)(2,1)S(1)} %collective-permute-done.6.refs_8_) | copy-start | bytes 786436
  36.0 11.3 %collective-permute-start.10 = (bf16[128,1024]{1,0:T(8,128)(2,1)S(1)}, bf16[128,1024]{1,0:T(8,128)(2,1)}, u32[]{:S(2)}, u32[]{:S(2)}) collective-permute-start(bf16[128,1024]{1,0:T(8,128)(2,1)S(1)} %collective-permute-done.6.refs_8_), channel_id=1, source_target_pairs={{0,7},{1,0},{2,1},{3,2},{4,3},{5,4},{6,5},{7,6},{8,15},{9,8},{10,9... | collective-permute-start | bytes 786440 | tf_op jit(solution)/shard_map/ppermute | solution.py:23
  40.6 13.4 %copy-start.10 = (bf16[128,1024]{1,0:T(8,128)(2,1)}, bf16[128,1024]{1,0:T(8,128)(2,1)S(1)}, u32[]{:S(2)}) copy-start(bf16[128,1024]{1,0:T(8,128)(2,1)S(1)} %collective-permute-done.11.refs_13_) | copy-start | bytes 786436
  40.6 8.2 %collective-permute-start.13 = (bf16[128,1024]{1,0:T(8,128)(2,1)S(1)}, bf16[128,1024]{1,0:T(8,128)(2,1)}, u32[]{:S(2)}, u32[]{:S(2)}) collective-permute-start(bf16[128,1024]{1,0:T(8,128)(2,1)S(1)} %collective-permute-done.11.refs_13_), channel_id=1, source_target_pairs={{0,7},{1,0},{2,1},{3,2},{4,3},{5,4},{6,5},{7,6},{8,15},{9,8},{10,9... | collective-permute-start | bytes 786440 | tf_op jit(solution)/shard_map/ppermute | solution.py:28
  44.0 10.0 %copy-start.11 = (bf16[128,1024]{1,0:T(8,128)(2,1)}, bf16[128,1024]{1,0:T(8,128)(2,1)S(1)}, u32[]{:S(2)}) copy-start(bf16[128,1024]{1,0:T(8,128)(2,1)S(1)} %collective-permute-done.8.refs_10_) | copy-start | bytes 786436
  44.0 9.9 %collective-permute-start.12 = (bf16[128,1024]{1,0:T(8,128)(2,1)S(1)}, bf16[128,1024]{1,0:T(8,128)(2,1)}, u32[]{:S(2)}, u32[]{:S(2)}) collective-permute-start(bf16[128,1024]{1,0:T(8,128)(2,1)S(1)} %collective-permute-done.8.refs_10_), channel_id=1, source_target_pairs={{0,1},{1,2},{2,3},{3,4},{4,5},{5,6},{6,7},{7,0},{8,9},{9,10},{10,1... | collective-permute-start | bytes 786440 | tf_op jit(solution)/shard_map/ppermute | solution.py:28
  47.3 6.8 %copy-start.12 = (bf16[128,1024]{1,0:T(8,128)(2,1)}, bf16[128,1024]{1,0:T(8,128)(2,1)S(1)}, u32[]{:S(2)}) copy-start(bf16[128,1024]{1,0:T(8,128)(2,1)S(1)} %collective-permute-done.9.refs_11_) | copy-start | bytes 786436

commit v2 on v1

--- a/solution.py
+++ b/solution.py
@@ -8,6 +8,8 @@
 from jax.sharding import PartitionSpec as P
 
 CHUNKS = 2
+PROJECT_VMEM = 50 * 2**20
+OTHER_VMEM = 12 * 2**20
 
 
 def gather_ring(block):
@@ -36,24 +38,29 @@
     return lax.broadcasted_iota(jnp.int32, shape, dim)
 
 
-def project_pack_kernel(offsets, slot_cap, draft, me_ref, route_ref, *refs):
-    blocks = refs[: len(offsets) * CHUNKS]
-    wk_ref, wv_ref, out_ref = refs[len(offsets) * CHUNKS :]
-    depth = blocks[0].shape[1]
+def project_kernel(offsets, slot_cap, draft, me_ref, accepted_ref, owner_ref, page_ref, wk_ref, wv_ref, *refs):
+    count = len(offsets) - 1
+    blocks = refs[: count * CHUNKS]
+    total_ref, lastk_ref, lastv_ref, select_ref, notes_ref, weights, routes, sems = refs[count * CHUNKS :]
+    depth, head_cols = blocks[0].shape[1], wk_ref.shape[1]
     heads = len(offsets)
-    total = None
+    fetches = []
+    for i, ref in enumerate((accepted_ref, owner_ref, page_ref)):
+        fetches.append(pltpu.make_async_copy(ref, routes.at[i], sems.at[2 * heads + i]))
     for i, offset in enumerate(offsets):
-        rows = jnp.concatenate([b[...] for b in blocks[i * CHUNKS : (i + 1) * CHUNKS]], axis=0)
         origin = lax.rem(me_ref[0] + offset, heads)
         at = pl.ds(pl.multiple_of(origin * depth, depth), depth)
-        weights = jnp.concatenate([wk_ref[at, :], wv_ref[at, :]], axis=1)
-        part = jnp.dot(rows, weights, preferred_element_type=jnp.float32)
-        total = part if total is None else total + part
-    projected = total.astype(jnp.bfloat16)
-    req = route_ref.shape[1]
-    accepted = route_ref[0:1, :].astype(jnp.float32)
-    owner = route_ref[1:2, :].astype(jnp.float32)
-    page = route_ref[2:3, :].astype(jnp.float32)
+        to = (weights.at[i, 0], weights.at[i, 1]) if i < count else (lastk_ref, lastv_ref)
+        for j, w in enumerate((wk_ref, wv_ref)):
+            fetches.append(pltpu.make_async_copy(w.at[at, :], to[j], sems.at[2 * i + j]))
+    for fetch in fetches:
+        fetch.start()
+    for fetch in fetches[:3]:
+        fetch.wait()
+    req = owner_ref.shape[1]
+    accepted = routes[0].astype(jnp.float32)
+    owner = routes[1].astype(jnp.float32)
+    page = routes[2].astype(jnp.float32)
     diagonal = iota((req, req), 0) == iota((req, req), 1)
     owner_col = jnp.sum(jnp.where(diagonal, owner, 0.0), axis=1, keepdims=True)
     earlier = (owner_col == owner) & (iota((req, req), 0) < iota((req, req), 1))
@@ -69,26 +76,44 @@
         mine & (draft_row < accepted_col), slot_col * draft + draft_row + 1.0, 0.0
     )
     target = jnp.sum(wanted, axis=0, keepdims=True) - 1.0
-    owners = out_ref.shape[0]
-    slots = owners * slot_cap
-    select = jnp.where(
-        iota((slots * draft, row_count), 0).astype(jnp.float32) == target, 1.0, 0.0
-    ).astype(jnp.bfloat16)
-    packed = jnp.dot(select, projected, preferred_element_type=jnp.float32).astype(jnp.bfloat16)
-    head_cols = wk_ref.shape[1]
-    span = slot_cap * draft
-    out_ref[:, 0:span, :] = packed[:, :head_cols].reshape(owners, span, head_cols)
-    out_ref[:, span : 2 * span, :] = packed[:, head_cols:].reshape(owners, span, head_cols)
+    place = iota(select_ref.shape, 0).astype(jnp.float32)
+    select_ref[...] = jnp.where(place == target, 1.0, 0.0).astype(jnp.bfloat16)
     part_lanes = head_cols // slot_cap
-    dest = lax.div(iota((owners * draft, req), 0), draft).astype(jnp.float32)
-    note_lane = iota((owners * draft, head_cols), 1)
-    notes = jnp.full((owners * draft, head_cols), -1.0, jnp.float32)
+    dest = lax.div(iota((notes_ref.shape[0], req), 0), draft).astype(jnp.float32)
+    note_lane = iota(notes_ref.shape, 1)
+    notes = jnp.full(notes_ref.shape, -1.0, jnp.float32)
     for s in range(slot_cap):
         found = jnp.sum(
             jnp.where(dest * slot_cap + s == slot, page + 1.0, 0.0), axis=1, keepdims=True
         ) - 1.0
         notes = jnp.where(note_lane >= s * part_lanes, found, notes)
-    out_ref[:, 2 * span :, :] = notes.astype(jnp.bfloat16).reshape(owners, draft, head_cols)
+    notes_ref[...] = notes.astype(jnp.bfloat16)
+    total = None
+    for i in range(count):
+        rows = jnp.concatenate([b[...] for b in blocks[i * CHUNKS : (i + 1) * CHUNKS]], axis=0)
+        fetches[3 + 2 * i].wait()
+        fetches[4 + 2 * i].wait()
+        both = jnp.concatenate([weights[i, 0], weights[i, 1]], axis=1)
+        part = jnp.dot(rows, both, preferred_element_type=jnp.float32)
+        total = part if total is None else total + part
+    total_ref[...] = total
+    fetches[3 + 2 * count].wait()
+    fetches[4 + 2 * count].wait()
+
+
+def pack_kernel(slot_cap, draft, total_ref, lastk_ref, lastv_ref, select_ref, notes_ref, *refs):
+    out_ref = refs[-1]
+    rows = jnp.concatenate([b[...] for b in refs[:-1]], axis=0)
+    both = jnp.concatenate([lastk_ref[...], lastv_ref[...]], axis=1)
+    total = total_ref[...] + jnp.dot(rows, both, preferred_element_type=jnp.float32)
+    packed = jnp.dot(
+        select_ref[...], total.astype(jnp.bfloat16), preferred_element_type=jnp.float32
+    ).astype(jnp.bfloat16)
+    owners, _, head_cols = out_ref.shape
+    span = slot_cap * draft
+    out_ref[:, 0:span, :] = packed[:, :head_cols].reshape(owners, span, head_cols)
+    out_ref[:, span : 2 * span, :] = packed[:, head_cols:].reshape(owners, span, head_cols)
+    out_ref[:, 2 * span :, :] = notes_ref[...].reshape(owners, draft, head_cols)
 
 
 def place_kernel(slot_cap, arrived_ref, key_ref, value_ref):
@@ -125,25 +150,49 @@
     seq_count = lax.axis_size("seq")
     slot_cap = max(2, 2 * req_dev // seq_count)
     slot_total = slot_cap * seq_count
-    route = jnp.stack([accepted, owner_group, page_slot])
+    routes = [a.reshape(1, req_dev) for a in (accepted, owner_group, page_slot)]
     me = lax.axis_index("head").astype(jnp.int32).reshape(1)
     held = gather_ring(draft_features)
     offsets = tuple(offset for offset, _ in held)
     blocks = [b for _, chunks in held for b in chunks]
     vmem = pl.BlockSpec(memory_space=pltpu.VMEM)
-    note_rows = 2 * slot_cap * draft + draft
-    packed = pl.pallas_call(
-        functools.partial(project_pack_kernel, offsets, slot_cap, draft),
-        out_shape=jax.ShapeDtypeStruct((seq_count, note_rows, head_cols), jnp.bfloat16),
-        in_specs=[pl.BlockSpec(memory_space=pltpu.SMEM), vmem] + [vmem] * (len(blocks) + 2),
-        out_specs=vmem,
+    hbm = pl.BlockSpec(memory_space=pltpu.HBM)
+    early, late = blocks[:-CHUNKS], blocks[-CHUNKS:]
+    row_count, heads = req_dev * draft, len(offsets)
+    total, last_key, last_value, select, notes = pl.pallas_call(
+        functools.partial(project_kernel, offsets, slot_cap, draft),
+        out_shape=(
+            jax.ShapeDtypeStruct((row_count, 2 * head_cols), jnp.float32),
+            jax.ShapeDtypeStruct((depth, head_cols), jnp.bfloat16),
+            jax.ShapeDtypeStruct((depth, head_cols), jnp.bfloat16),
+            jax.ShapeDtypeStruct((slot_total * draft, row_count), jnp.bfloat16),
+            jax.ShapeDtypeStruct((seq_count * draft, head_cols), jnp.bfloat16),
+        ),
+        in_specs=[pl.BlockSpec(memory_space=pltpu.SMEM)] + [hbm] * 5 + [vmem] * len(early),
+        out_specs=(vmem,) * 5,
+        scratch_shapes=[
+            pltpu.VMEM((heads - 1, 2, depth, head_cols), jnp.bfloat16),
+            pltpu.VMEM((3, 1, req_dev), jnp.int32),
+            pltpu.SemaphoreType.DMA((2 * heads + 3,)),
+        ],
         cost_estimate=pl.CostEstimate(
-            flops=4 * req_dev * draft * depth * len(offsets) * head_cols,
-            bytes_accessed=2 * (req_dev * draft + 2 * head_cols) * depth * len(offsets),
+            flops=4 * row_count * depth * heads * head_cols,
+            bytes_accessed=2 * (row_count + 2 * head_cols) * depth * heads,
             transcendentals=0,
         ),
-        name="project_pack",
-    )(me, route, *blocks, w_key, w_value)
+        compiler_params=pltpu.CompilerParams(vmem_limit_bytes=PROJECT_VMEM),
+        name="project",
+    )(me, *routes, w_key, w_value, *early)
+    packed = pl.pallas_call(
+        functools.partial(pack_kernel, slot_cap, draft),
+        out_shape=jax.ShapeDtypeStruct(
+            (seq_count, 2 * slot_cap * draft + draft, head_cols), jnp.bfloat16
+        ),
+        in_specs=[vmem] * (5 + len(late)),
+        out_specs=vmem,
+        compiler_params=pltpu.CompilerParams(vmem_limit_bytes=OTHER_VMEM),
+        name="pack",
+    )(total, last_key, last_value, select, notes, *late)
     arrived = lax.all_to_all(packed, "seq", split_axis=0, concat_axis=0, tiled=True)
     cache = jax.ShapeDtypeStruct((slot_total, draft, head_cols), jnp.bfloat16)
     return pl.pallas_call(
@@ -151,6 +200,7 @@
         out_shape=(cache, cache),
         in_specs=[vmem],
         out_specs=(vmem, vmem),
+        compiler_params=pltpu.CompilerParams(vmem_limit_bytes=OTHER_VMEM),
         name="place",
     )(arrived)
 

time: 135 us -> 130 us (0.963)
  waiting for transfers between devices: 6.69 us -> 0.04 us
  blocking collectives: 72.6 us -> 75.2 us
  local copies, waits for them, and re-layouts: 1.12 us -> 3.03 us
    ppermute x1, waiting for transfers between devices: 5.12 us -> 0.01 us  [gather_ring(): lax.ppermute(rising[c], 'head', up)]
    ppermute x6, starting transfers between devices: 26.9 us -> 22.5 us  [gather_ring(): falling[c] = lax.ppermute(falling[c], 'head', down)]
    ppermute x6, starting transfers between devices: 11.7 us -> 14.9 us  [gather_ring(): rising[c] = lax.ppermute(rising[c], 'head', up)]
    all_to_all x1, blocking collectives: 72.6 us -> 75.2 us  [local(): lax.all_to_all(packed, 'seq', split_axis=0, concat_axis=0, tiled=True)]
    ppermute x1, starting transfers between devices: 1.95 us -> 3.89 us  [gather_ring(): lax.ppermute(rising[c], 'head', up)]
    unnamed x26 -> x6, local copies, waits for them, and re-layouts: 0.05 us -> 1.96 us
    ppermute x1, waiting for transfers between devices: 1.54 us -> 0.01 us  [gather_ring(): lax.ppermute(falling[c], 'head', down)]
    pallas_call x1 -> x2, Pallas kernels: 5.82 us -> 5.5 us  [the longest x1 4.88 us: local(): pl.pallas_call(functools.partial(project_kernel, offsets, slot_cap, draft...]
  transfers between devices with their start and end apart: 14 -> 14, of which waited for: 2 -> 0; matrix products, arithmetic and copies ran while one was open for 1% -> 0% of each run, Pallas kernels for 0% -> 4%
where the time goes in v2:
time: 130 us
  blocking collectives  75.2 us (58%)
  starting transfers between devices  43.9 us (34%)
  Pallas kernels  6.69 us (5%)
  local copies, waits for them, and re-layouts  3.03 us (2%)
    all_to_all x1, blocking collectives, local(): lax.all_to_all(packed, 'seq', split_axis=0, concat_axis=0, tiled=True)  75.2 us
    ppermute x6, starting transfers between devices, gather_ring(): falling[c] = lax.ppermute(falling[c], 'head', down)  22.5 us
    ppermute x6, starting transfers between devices, gather_ring(): rising[c] = lax.ppermute(rising[c], 'head', up)  14.9 us
    pallas_call x1, Pallas kernels, local(): pl.pallas_call(functools.partial(project_kernel, offsets, slot_cap, draft...  4.88 us
    ppermute x1, starting transfers between devices, gather_ring(): lax.ppermute(rising[c], 'head', up)  3.89 us
    ppermute x1, starting transfers between devices, gather_ring(): lax.ppermute(falling[c], 'head', down)  2.67 us
  transfers between devices with their start and end apart: 14, of which 0 were waited for; matrix products, arithmetic and copies ran while one was open for 0% of the time, Pallas kernels for 4%

profile of v2, /device:TPU:65, one launch (start us, length us, event | category | flops | bytes accessed | tf_op | source)
XLA Modules:
  0.0 129.7 jit_solution(15557620438350120241)
XLA Ops:
  0.6 1.1 fusion
  1.7 4.1 %collective-permute-start = (bf16[128,1024]{1,0:T(8,128)(2,1)S(1)}, bf16[128,1024]{1,0:T(8,128)(2,1)S(1)}, u32[]{:S(2)}, u32[]{:S(2)}) collective-permute-start(bf16[128,1024]{1,0:T(8,128)(2,1)S(1)} %get-tuple-element.13.refs_0_), channel_id=1, source_target_pairs={{0,1},{1,2},{2,3},{3,4},{4,5},{5,6},{6,7},{7,0},{8,9},{9,10},{10,1... | collective-permute-start | bytes 786440 | tf_op jit(solution)/shard_map/ppermute | solution.py:24
  5.8 4.1 %collective-permute-start.3 = (bf16[128,1024]{1,0:T(8,128)(2,1)S(1)}, bf16[128,1024]{1,0:T(8,128)(2,1)S(1)}, u32[]{:S(2)}, u32[]{:S(2)}) collective-permute-start(bf16[128,1024]{1,0:T(8,128)(2,1)S(1)} %get-tuple-element.12.refs_1_), channel_id=1, source_target_pairs={{0,7},{1,0},{2,1},{3,2},{4,3},{5,4},{6,5},{7,6},{8,15},{9,8},{10,9... | collective-permute-start | bytes 786440 | tf_op jit(solution)/shard_map/ppermute | solution.py:25
  10.0 3.4 %collective-permute-start.2 = (bf16[128,1024]{1,0:T(8,128)(2,1)S(1)}, bf16[128,1024]{1,0:T(8,128)(2,1)S(1)}, u32[]{:S(2)}, u32[]{:S(2)}) collective-permute-start(bf16[128,1024]{1,0:T(8,128)(2,1)S(1)} %get-tuple-element.13.refs_0_), channel_id=1, source_target_pairs={{0,7},{1,0},{2,1},{3,2},{4,3},{5,4},{6,5},{7,6},{8,15},{9,8},{10,9... | collective-permute-start | bytes 786440 | tf_op jit(solution)/shard_map/ppermute | solution.py:25
  13.4 2.0 %collective-permute-start.1 = (bf16[128,1024]{1,0:T(8,128)(2,1)S(1)}, bf16[128,1024]{1,0:T(8,128)(2,1)S(1)}, u32[]{:S(2)}, u32[]{:S(2)}) collective-permute-start(bf16[128,1024]{1,0:T(8,128)(2,1)S(1)} %get-tuple-element.12.refs_1_), channel_id=1, source_target_pairs={{0,1},{1,2},{2,3},{3,4},{4,5},{5,6},{6,7},{7,0},{8,9},{9,10},{10,1... | collective-permute-start | bytes 786440 | tf_op jit(solution)/shard_map/ppermute | solution.py:24
  15.3 0.0 collective-permute-done.refs_2_
  15.3 2.0 %collective-permute-start.4 = (bf16[128,1024]{1,0:T(8,128)(2,1)S(1)}, bf16[128,1024]{1,0:T(8,128)(2,1)S(1)}, u32[]{:S(2)}, u32[]{:S(2)}) collective-permute-start(bf16[128,1024]{1,0:T(8,128)(2,1)S(1)} %collective-permute-done.refs_2_), channel_id=1, source_target_pairs={{0,1},{1,2},{2,3},{3,4},{4,5},{5,6},{6,7},{7,0},{8,9},{9,10},{10,1... | collective-permute-start | bytes 786440 | tf_op jit(solution)/shard_map/ppermute | solution.py:24
  17.3 0.0 collective-permute-done.3.refs_5_
  17.3 4.6 %collective-permute-start.7 = (bf16[128,1024]{1,0:T(8,128)(2,1)S(1)}, bf16[128,1024]{1,0:T(8,128)(2,1)S(1)}, u32[]{:S(2)}, u32[]{:S(2)}) collective-permute-start(bf16[128,1024]{1,0:T(8,128)(2,1)S(1)} %collective-permute-done.3.refs_5_), channel_id=1, source_target_pairs={{0,7},{1,0},{2,1},{3,2},{4,3},{5,4},{6,5},{7,6},{8,15},{9,8},{10,9... | collective-permute-start | bytes 786440 | tf_op jit(solution)/shard_map/ppermute | solution.py:25
  21.9 0.0 collective-permute-done.2.refs_4_
  21.9 3.4 %collective-permute-start.6 = (bf16[128,1024]{1,0:T(8,128)(2,1)S(1)}, bf16[128,1024]{1,0:T(8,128)(2,1)S(1)}, u32[]{:S(2)}, u32[]{:S(2)}) collective-permute-start(bf16[128,1024]{1,0:T(8,128)(2,1)S(1)} %collective-permute-done.2.refs_4_), channel_id=1, source_target_pairs={{0,7},{1,0},{2,1},{3,2},{4,3},{5,4},{6,5},{7,6},{8,15},{9,8},{10,9... | collective-permute-start | bytes 786440 | tf_op jit(solution)/shard_map/ppermute | solution.py:25
  25.3 0.0 collective-permute-done.1.refs_3_
  25.3 2.0 %collective-permute-start.5 = (bf16[128,1024]{1,0:T(8,128)(2,1)S(1)}, bf16[128,1024]{1,0:T(8,128)(2,1)S(1)}, u32[]{:S(2)}, u32[]{:S(2)}) collective-permute-start(bf16[128,1024]{1,0:T(8,128)(2,1)S(1)} %collective-permute-done.1.refs_3_), channel_id=1, source_target_pairs={{0,1},{1,2},{2,3},{3,4},{4,5},{5,6},{6,7},{7,0},{8,9},{9,10},{10,1... | collective-permute-start | bytes 786440 | tf_op jit(solution)/shard_map/ppermute | solution.py:24
  27.3 0.0 collective-permute-done.4.refs_6_
  27.3 3.0 %collective-permute-start.8 = (bf16[128,1024]{1,0:T(8,128)(2,1)S(1)}, bf16[128,1024]{1,0:T(8,128)(2,1)S(1)}, u32[]{:S(2)}, u32[]{:S(2)}) collective-permute-start(bf16[128,1024]{1,0:T(8,128)(2,1)S(1)} %collective-permute-done.4.refs_6_), channel_id=1, source_target_pairs={{0,1},{1,2},{2,3},{3,4},{4,5},{5,6},{6,7},{7,0},{8,9},{9,10},{10,1... | collective-permute-start | bytes 786440 | tf_op jit(solution)/shard_map/ppermute | solution.py:24
  30.3 0.0 collective-permute-done.7.refs_9_
  30.3 3.6 %collective-permute-start.11 = (bf16[128,1024]{1,0:T(8,128)(2,1)S(1)}, bf16[128,1024]{1,0:T(8,128)(2,1)}, u32[]{:S(2)}, u32[]{:S(2)}) collective-permute-start(bf16[128,1024]{1,0:T(8,128)(2,1)S(1)} %collective-permute-done.7.refs_9_), channel_id=1, source_target_pairs={{0,7},{1,0},{2,1},{3,2},{4,3},{5,4},{6,5},{7,6},{8,15},{9,8},{10,9... | collective-permute-start | bytes 786440 | tf_op jit(solution)/shard_map/ppermute | solution.py:25
  33.9 3.4 %collective-permute-start.10 = (bf16[128,1024]{1,0:T(8,128)(2,1)S(1)}, bf16[128,1024]{1,0:T(8,128)(2,1)}, u32[]{:S(2)}, u32[]{:S(2)}) collective-permute-start(bf16[128,1024]{1,0:T(8,128)(2,1)S(1)} %collective-permute-done.6.refs_8_), channel_id=1, source_target_pairs={{0,7},{1,0},{2,1},{3,2},{4,3},{5,4},{6,5},{7,6},{8,15},{9,8},{10,9... | collective-permute-start | bytes 786440 | tf_op jit(solution)/shard_map/ppermute | solution.py:25
  37.3 2.0 %collective-permute-start.9 = (bf16[128,1024]{1,0:T(8,128)(2,1)S(1)}, bf16[128,1024]{1,0:T(8,128)(2,1)}, u32[]{:S(2)}, u32[]{:S(2)}) collective-permute-start(bf16[128,1024]{1,0:T(8,128)(2,1)S(1)} %collective-permute-done.5.refs_7_), channel_id=1, source_target_pairs={{0,1},{1,2},{2,3},{3,4},{4,5},{5,6},{6,7},{7,0},{8,9},{9,10},{10,1... | collective-permute-start | bytes 786440 | tf_op jit(solution)/shard_map/ppermute | solution.py:24
  39.3 0.0 collective-permute-done.8.refs_10_
  39.3 3.9 %collective-permute-start.12 = (bf16[128,1024]{1,0:T(8,128)(2,1)S(1)}, bf16[128,1024]{1,0:T(8,128)(2,1)S(1)}, u32[]{:S(2)}, u32[]{:S(2)}) collective-permute-start(bf16[128,1024]{1,0:T(8,128)(2,1)S(1)} %collective-permute-done.8.refs_10_), channel_id=1, source_target_pairs={{0,1},{1,2},{2,3},{3,4},{4,5},{5,6},{6,7},{7,0},{8,9},{9,10},{10,1... | collective-permute-start | bytes 786440 | tf_op jit(solution)/shard_map/ppermute | solution.py:30
  43.2 0.0 collective-permute-done.11.refs_13_
  43.2 2.7 %collective-permute-start.13 = (bf16[128,1024]{1,0:T(8,128)(2,1)}, bf16[128,1024]{1,0:T(8,128)(2,1)S(1)}, u32[]{:S(2)}, u32[]{:S(2)}) collective-permute-start(bf16[128,1024]{1,0:T(8,128)(2,1)} %collective-permute-done.11.refs_13_), channel_id=1, source_target_pairs={{0,7},{1,0},{2,1},{3,2},{4,3},{5,4},{6,5},{7,6},{8,15},{9,8},{10,9... | collective-permute-start | bytes 786440 | tf_op jit(solution)/shard_map/ppermute | solution.py:30
  45.9 0.0 collective-permute-done.9.refs_11_
  45.9 0.0 copy-start
  45.9 0.6 copy-done
  46.5 0.7 copy-done.1
  47.2 0.7 copy-done.2
  47.9 4.9 %project.1 = (f32[256,256]{1,0:T(8,128)S(1)}, bf16[1024,128]{1,0:T(8,128)(2,1)S(1)}, bf16[1024,128]{1,0:T(8,128)(2,1)S(1)}, bf16[512,256]{1,0:T(8,128)(2,1)S(1)}, bf16[256,128]{1,0:T(8,128)(2,1)S(1)}) custom-call(s32[1]{0:T(128)} %bitcast.me_ref, s32[1,32]{1,0:T(1,128)S(1)} %bitcast.4, s32[1,32]{1,0:T(1,128)S(1)} %bitcast.5, s32[1,32]{1,0:T(1,128)S(1)} %bitcast.6, ...), custom_call_target="tpu_custom_call" | custom-call | flops 1073741824 | bytes 8388608 | tf_op jit(solution)/shard_map/project/pallas_call | solution.py:162
  52.8 0.6 pack.1
  53.4 75.2 %all_to_all.5.arrived_ref = bf16[32,40,128]{2,1,0:T(8,128)(2,1)S(1)} all-to-all(bf16[32,40,128]{2,1,0:T(8,128)(2,1)S(1)} %pack.1), channel_id=1, replica_groups=mesh['grp'=2,'seq'=32,'head'=8] {'seq'}, dimensions={0} | all-to-all | bytes 655360 | tf_op jit(solution)/shard_map/all_to_all | solution.py:196
  128.5 1.2 place.1
  (7 shorter events, 0.0 us)
Async XLA Ops:
  1.7 13.6 %collective-permute-start = (bf16[128,1024]{1,0:T(8,128)(2,1)S(1)}, bf16[128,1024]{1,0:T(8,128)(2,1)S(1)}, u32[]{:S(2)}, u32[]{:S(2)}) collective-permute-start(bf16[128,1024]{1,0:T(8,128)(2,1)S(1)} %get-tuple-element.13.refs_0_), channel_id=1, source_target_pairs={{0,1},{1,2},{2,3},{3,4},{4,5},{5,6},{6,7},{7,0},{8,9},{9,10},{10,1... | collective-permute-start | bytes 786440 | tf_op jit(solution)/shard_map/ppermute | solution.py:24
  5.8 11.5 %collective-permute-start.3 = (bf16[128,1024]{1,0:T(8,128)(2,1)S(1)}, bf16[128,1024]{1,0:T(8,128)(2,1)S(1)}, u32[]{:S(2)}, u32[]{:S(2)}) collective-permute-start(bf16[128,1024]{1,0:T(8,128)(2,1)S(1)} %get-tuple-element.12.refs_1_), channel_id=1, source_target_pairs={{0,7},{1,0},{2,1},{3,2},{4,3},{5,4},{6,5},{7,6},{8,15},{9,8},{10,9... | collective-permute-start | bytes 786440 | tf_op jit(solution)/shard_map/ppermute | solution.py:25
  10.0 12.0 %collective-permute-start.2 = (bf16[128,1024]{1,0:T(8,128)(2,1)S(1)}, bf16[128,1024]{1,0:T(8,128)(2,1)S(1)}, u32[]{:S(2)}, u32[]{:S(2)}) collective-permute-start(bf16[128,1024]{1,0:T(8,128)(2,1)S(1)} %get-tuple-element.13.refs_0_), channel_id=1, source_target_pairs={{0,7},{1,0},{2,1},{3,2},{4,3},{5,4},{6,5},{7,6},{8,15},{9,8},{10,9... | collective-permute-start | bytes 786440 | tf_op jit(solution)/shard_map/ppermute | solution.py:25
  13.4 12.0 %collective-permute-start.1 = (bf16[128,1024]{1,0:T(8,128)(2,1)S(1)}, bf16[128,1024]{1,0:T(8,128)(2,1)S(1)}, u32[]{:S(2)}, u32[]{:S(2)}) collective-permute-start(bf16[128,1024]{1,0:T(8,128)(2,1)S(1)} %get-tuple-element.12.refs_1_), channel_id=1, source_target_pairs={{0,1},{1,2},{2,3},{3,4},{4,5},{5,6},{6,7},{7,0},{8,9},{9,10},{10,1... | collective-permute-start | bytes 786440 | tf_op jit(solution)/shard_map/ppermute | solution.py:24
  15.3 12.0 %collective-permute-start.4 = (bf16[128,1024]{1,0:T(8,128)(2,1)S(1)}, bf16[128,1024]{1,0:T(8,128)(2,1)S(1)}, u32[]{:S(2)}, u32[]{:S(2)}) collective-permute-start(bf16[128,1024]{1,0:T(8,128)(2,1)S(1)} %collective-permute-done.refs_2_), channel_id=1, source_target_pairs={{0,1},{1,2},{2,3},{3,4},{4,5},{5,6},{6,7},{7,0},{8,9},{9,10},{10,1... | collective-permute-start | bytes 786440 | tf_op jit(solution)/shard_map/ppermute | solution.py:24
  17.3 13.0 %collective-permute-start.7 = (bf16[128,1024]{1,0:T(8,128)(2,1)S(1)}, bf16[128,1024]{1,0:T(8,128)(2,1)S(1)}, u32[]{:S(2)}, u32[]{:S(2)}) collective-permute-start(bf16[128,1024]{1,0:T(8,128)(2,1)S(1)} %collective-permute-done.3.refs_5_), channel_id=1, source_target_pairs={{0,7},{1,0},{2,1},{3,2},{4,3},{5,4},{6,5},{7,6},{8,15},{9,8},{10,9... | collective-permute-start | bytes 786440 | tf_op jit(solution)/shard_map/ppermute | solution.py:25
  21.9 12.0 %collective-permute-start.6 = (bf16[128,1024]{1,0:T(8,128)(2,1)S(1)}, bf16[128,1024]{1,0:T(8,128)(2,1)S(1)}, u32[]{:S(2)}, u32[]{:S(2)}) collective-permute-start(bf16[128,1024]{1,0:T(8,128)(2,1)S(1)} %collective-permute-done.2.refs_4_), channel_id=1, source_target_pairs={{0,7},{1,0},{2,1},{3,2},{4,3},{5,4},{6,5},{7,6},{8,15},{9,8},{10,9... | collective-permute-start | bytes 786440 | tf_op jit(solution)/shard_map/ppermute | solution.py:25
  25.3 12.0 %collective-permute-start.5 = (bf16[128,1024]{1,0:T(8,128)(2,1)S(1)}, bf16[128,1024]{1,0:T(8,128)(2,1)S(1)}, u32[]{:S(2)}, u32[]{:S(2)}) collective-permute-start(bf16[128,1024]{1,0:T(8,128)(2,1)S(1)} %collective-permute-done.1.refs_3_), channel_id=1, source_target_pairs={{0,1},{1,2},{2,3},{3,4},{4,5},{5,6},{6,7},{7,0},{8,9},{9,10},{10,1... | collective-permute-start | bytes 786440 | tf_op jit(solution)/shard_map/ppermute | solution.py:24
  27.3 12.0 %collective-permute-start.8 = (bf16[128,1024]{1,0:T(8,128)(2,1)S(1)}, bf16[128,1024]{1,0:T(8,128)(2,1)S(1)}, u32[]{:S(2)}, u32[]{:S(2)}) collective-permute-start(bf16[128,1024]{1,0:T(8,128)(2,1)S(1)} %collective-permute-done.4.refs_6_), channel_id=1, source_target_pairs={{0,1},{1,2},{2,3},{3,4},{4,5},{5,6},{6,7},{7,0},{8,9},{9,10},{10,1... | collective-permute-start | bytes 786440 | tf_op jit(solution)/shard_map/ppermute | solution.py:24
  30.3 12.9 %collective-permute-start.11 = (bf16[128,1024]{1,0:T(8,128)(2,1)S(1)}, bf16[128,1024]{1,0:T(8,128)(2,1)}, u32[]{:S(2)}, u32[]{:S(2)}) collective-permute-start(bf16[128,1024]{1,0:T(8,128)(2,1)S(1)} %collective-permute-done.7.refs_9_), channel_id=1, source_target_pairs={{0,7},{1,0},{2,1},{3,2},{4,3},{5,4},{6,5},{7,6},{8,15},{9,8},{10,9... | collective-permute-start | bytes 786440 | tf_op jit(solution)/shard_map/ppermute | solution.py:25
  33.9 12.0 %collective-permute-start.10 = (bf16[128,1024]{1,0:T(8,128)(2,1)S(1)}, bf16[128,1024]{1,0:T(8,128)(2,1)}, u32[]{:S(2)}, u32[]{:S(2)}) collective-permute-start(bf16[128,1024]{1,0:T(8,128)(2,1)S(1)} %collective-permute-done.6.refs_8_), channel_id=1, source_target_pairs={{0,7},{1,0},{2,1},{3,2},{4,3},{5,4},{6,5},{7,6},{8,15},{9,8},{10,9... | collective-permute-start | bytes 786440 | tf_op jit(solution)/shard_map/ppermute | solution.py:25
  37.3 8.6 %collective-permute-start.9 = (bf16[128,1024]{1,0:T(8,128)(2,1)S(1)}, bf16[128,1024]{1,0:T(8,128)(2,1)}, u32[]{:S(2)}, u32[]{:S(2)}) collective-permute-start(bf16[128,1024]{1,0:T(8,128)(2,1)S(1)} %collective-permute-done.5.refs_7_), channel_id=1, source_target_pairs={{0,1},{1,2},{2,3},{3,4},{4,5},{5,6},{6,7},{7,0},{8,9},{9,10},{10,1... | collective-permute-start | bytes 786440 | tf_op jit(solution)/shard_map/ppermute | solution.py:24
  39.3 13.5 %collective-permute-start.12 = (bf16[128,1024]{1,0:T(8,128)(2,1)S(1)}, bf16[128,1024]{1,0:T(8,128)(2,1)S(1)}, u32[]{:S(2)}, u32[]{:S(2)}) collective-permute-start(bf16[128,1024]{1,0:T(8,128)(2,1)S(1)} %collective-permute-done.8.refs_10_), channel_id=1, source_target_pairs={{0,1},{1,2},{2,3},{3,4},{4,5},{5,6},{6,7},{7,0},{8,9},{9,10},{10,1... | collective-permute-start | bytes 786440 | tf_op jit(solution)/shard_map/ppermute | solution.py:30
  43.2 9.6 %collective-permute-start.13 = (bf16[128,1024]{1,0:T(8,128)(2,1)}, bf16[128,1024]{1,0:T(8,128)(2,1)S(1)}, u32[]{:S(2)}, u32[]{:S(2)}) collective-permute-start(bf16[128,1024]{1,0:T(8,128)(2,1)} %collective-permute-done.11.refs_13_), channel_id=1, source_target_pairs={{0,7},{1,0},{2,1},{3,2},{4,3},{5,4},{6,5},{7,6},{8,15},{9,8},{10,9... | collective-permute-start | bytes 786440 | tf_op jit(solution)/shard_map/ppermute | solution.py:30
  45.9 0.7 copy-start
  46.5 0.7 copy-start.1
  47.2 0.7 copy-start.2

commit v3 on v2

v3 whole, which is shorter than its diff:
```python
import functools

import jax
import jax.numpy as jnp
from jax import lax
from jax.experimental import pallas as pl
from jax.experimental.pallas import tpu as pltpu
from jax.sharding import PartitionSpec as P

CHUNKS = 2
PROJECT_VMEM = 50 * 2**20
OTHER_VMEM = 12 * 2**20


def gather_ring(block):
    heads, lines = lax.axis_size("head"), lax.axis_size("seq")

    def turn(step):
        return [
            (line * heads + i, line * heads + (i + (step if line % 2 == 0 else -step)) % heads)
            for line in range(lines)
            for i in range(heads)
        ]

    axes, up, down = ("seq", "head"), turn(1), turn(-1)
    own = jnp.split(block, CHUNKS, axis=0)
    held = [(0, own)]
    rising, falling = list(own), list(own)
    for step in range(1, (heads + 1) // 2):
        for c in range(CHUNKS):
            rising[c] = lax.ppermute(rising[c], axes, up)
            falling[c] = lax.ppermute(falling[c], axes, down)
        held.append((-step, list(rising)))
        held.append((step, list(falling)))
    if heads % 2 == 0:
        last = [
            lax.ppermute(rising[c], axes, up) if c % 2 == 0 else lax.ppermute(falling[c], axes, down)
            for c in range(CHUNKS)
        ]
        held.append((heads // 2, last))
    return held


def iota(shape, dim):
    return lax.broadcasted_iota(jnp.int32, shape, dim)


def project_kernel(offsets, slot_cap, draft, me_ref, accepted_ref, owner_ref, page_ref, wk_ref, wv_ref, *refs):
    count = len(offsets) - 1
    blocks = refs[: count * CHUNKS]
    total_ref, lastk_ref, lastv_ref, select_ref, notes_ref, weights, sems = refs[count * CHUNKS :]
    depth, head_cols = blocks[0].shape[1], wk_ref.shape[1]
    heads = len(offsets)
    fetches = []
    for i, offset in enumerate(offsets):
        origin = lax.rem(me_ref[0] + me_ref[1] * offset + heads, heads)
        at = pl.ds(pl.multiple_of(origin * depth, depth), depth)
        to = (weights.at[i, 0], weights.at[i, 1]) if i < count else (lastk_ref, lastv_ref)
        for j, w in enumerate((wk_ref, wv_ref)):
            fetches.append(pltpu.make_async_copy(w.at[at, :], to[j], sems.at[2 * i + j]))
    for fetch in fetches:
        fetch.start()
    req = owner_ref.shape[0]
    spot = iota((1, req), 1)
    accepted = owner = page = jnp.zeros((1, req), jnp.int32)
    for r in range(req):
        accepted = jnp.where(spot == r, accepted_ref[r], accepted)
        owner = jnp.where(spot == r, owner_ref[r], owner)
        page = jnp.where(spot == r, page_ref[r], page)
    accepted, owner, page = (a.astype(jnp.float32) for a in (accepted, owner, page))
    diagonal = iota((req, req), 0) == iota((req, req), 1)
    owner_col = jnp.sum(jnp.where(diagonal, owner, 0.0), axis=1, keepdims=True)
    earlier = (owner_col == owner) & (iota((req, req), 0) < iota((req, req), 1))
    within = jnp.sum(jnp.where(earlier, 1.0, 0.0), axis=0, keepdims=True)
    slot = owner * slot_cap + within
    row_count = req * draft
    lane, sub = iota((req, row_count), 1), iota((req, row_count), 0)
    mine = (lane >= sub * draft) & (lane < sub * draft + draft)
    slot_col = jnp.sum(jnp.where(diagonal, slot, 0.0), axis=1, keepdims=True)
    accepted_col = jnp.sum(jnp.where(diagonal, accepted, 0.0), axis=1, keepdims=True)
    draft_row = (lane - sub * draft).astype(jnp.float32)
    wanted = jnp.where(
        mine & (draft_row < accepted_col), slot_col * draft + draft_row + 1.0, 0.0
    )
    target = jnp.sum(wanted, axis=0, keepdims=True) - 1.0
    row = iota(select_ref.shape, 0).astype(jnp.float32)
    select_ref[...] = jnp.where(row == target, 1.0, 0.0).astype(jnp.bfloat16)
    taken = iota((notes_ref.shape[0], req), 0).astype(jnp.float32) == slot
    found = jnp.sum(jnp.where(taken, page + 1.0, 0.0), axis=1, keepdims=True)
    notes_ref[...] = jnp.broadcast_to(found, notes_ref.shape).astype(jnp.bfloat16)
    total = None
    for i in range(count):
        rows = jnp.concatenate([b[...] for b in blocks[i * CHUNKS : (i + 1) * CHUNKS]], axis=0)
        fetches[2 * i].wait()
        fetches[2 * i + 1].wait()
        both = jnp.concatenate([weights[i, 0], weights[i, 1]], axis=1)
        part = jnp.dot(rows, both, preferred_element_type=jnp.float32)
        total = part if total is None else total + part
    total_ref[...] = total
    fetches[2 * count].wait()
    fetches[2 * count + 1].wait()


def pack_kernel(slot_cap, draft, total_ref, lastk_ref, lastv_ref, select_ref, notes_ref, *refs):
    out_ref = refs[-1]
    rows = jnp.concatenate([b[...] for b in refs[:-1]], axis=0)
    both = jnp.concatenate([lastk_ref[...], lastv_ref[...]], axis=1)
    total = total_ref[...] + jnp.dot(rows, both, preferred_element_type=jnp.float32)
    packed = jnp.dot(
        select_ref[...], total.astype(jnp.bfloat16), preferred_element_type=jnp.float32
    ).astype(jnp.bfloat16)
    head_cols = out_ref.shape[1]
    span = slot_cap * draft
    stride = 2 * span + slot_cap
    for d in range(out_ref.shape[0] // stride):
        at = d * stride
        out_ref[at : at + span, :] = packed[d * span : (d + 1) * span, :head_cols]
        out_ref[at + span : at + 2 * span, :] = packed[d * span : (d + 1) * span, head_cols:]
        out_ref[at + 2 * span : at + stride, :] = notes_ref[d * slot_cap : (d + 1) * slot_cap, :]


def place_kernel(slot_cap, arrived_ref, key_ref, value_ref, rows_ref, notes_ref):
    pages, draft, head_cols = key_ref.shape
    span = slot_cap * draft
    stride = 2 * span + slot_cap
    sources = arrived_ref.shape[0] // stride
    rows = sources * draft
    for d in range(sources):
        rows_ref[d] = arrived_ref[d * stride : d * stride + 2 * span, :]
        notes = arrived_ref[d * stride + 2 * span : (d + 1) * stride, :].astype(jnp.float32)
        for s in range(slot_cap):
            notes_ref[s, d * draft : (d + 1) * draft, :] = jnp.broadcast_to(
                notes[s : s + 1, :], (draft, head_cols)
            )
    draft_row = lax.rem(iota((rows, head_cols), 0), draft).astype(jnp.float32)
    total = None
    for s in range(slot_cap):
        page = notes_ref[s]
        goes = jnp.where(page > 0.0, (page - 1.0) * draft + draft_row, -1.0)
        select = jnp.concatenate(
            [
                jnp.where(goes == (iota(goes.shape, 1) + at).astype(jnp.float32), 1.0, 0.0)
                for at in range(0, pages * draft, head_cols)
            ],
            axis=1,
        ).astype(jnp.bfloat16)
        keys = rows_ref[:, s * draft : (s + 1) * draft, :].reshape(rows, head_cols)
        values = rows_ref[:, span + s * draft : span + (s + 1) * draft, :].reshape(rows, head_cols)
        both = jnp.concatenate([keys, values], axis=1)
        part = lax.dot_general(
            select, both, (((0,), (0,)), ((), ())), preferred_element_type=jnp.float32
        )
        total = part if total is None else total + part
    placed = total.astype(jnp.bfloat16)
    key_ref[...] = placed[:, :head_cols].reshape(pages, draft, head_cols)
    value_ref[...] = placed[:, head_cols:].reshape(pages, draft, head_cols)


def local(draft_features, w_key, w_value, accepted, owner_group, page_slot):
    req_dev = accepted.shape[0]
    draft = draft_features.shape[0] // req_dev
    depth = draft_features.shape[1]
    head_cols = w_key.shape[1]
    seq_count = lax.axis_size("seq")
    slot_cap = max(2, 2 * req_dev // seq_count)
    slot_total = slot_cap * seq_count
    turn = 1 - 2 * lax.rem(lax.axis_index("seq"), 2)
    me = jnp.stack([lax.axis_index("head"), turn]).astype(jnp.int32)
    held = gather_ring(draft_features)
    offsets = tuple(offset for offset, _ in held)
    blocks = [b for _, chunks in held for b in chunks]
    vmem = pl.BlockSpec(memory_space=pltpu.VMEM)
    hbm = pl.BlockSpec(memory_space=pltpu.HBM)
    smem = pl.BlockSpec(memory_space=pltpu.SMEM)
    early, late = blocks[:-CHUNKS], blocks[-CHUNKS:]
    row_count, heads = req_dev * draft, len(offsets)
    stride = 2 * slot_cap * draft + slot_cap
    total, last_key, last_value, select, notes = pl.pallas_call(
        functools.partial(project_kernel, offsets, slot_cap, draft),
        out_shape=(
            jax.ShapeDtypeStruct((row_count, 2 * head_cols), jnp.float32),
            jax.ShapeDtypeStruct((depth, head_cols), jnp.bfloat16),
            jax.ShapeDtypeStruct((depth, head_cols), jnp.bfloat16),
            jax.ShapeDtypeStruct((slot_total * draft, row_count), jnp.bfloat16),
            jax.ShapeDtypeStruct((slot_total, head_cols), jnp.bfloat16),
        ),
        in_specs=[smem] * 4 + [hbm] * 2 + [vmem] * len(early),
        out_specs=(vmem,) * 5,
        scratch_shapes=[
            pltpu.VMEM((heads - 1, 2, depth, head_cols), jnp.bfloat16),
            pltpu.SemaphoreType.DMA((2 * heads,)),
        ],
        cost_estimate=pl.CostEstimate(
            flops=4 * row_count * depth * heads * head_cols,
            bytes_accessed=2 * (row_count + 2 * head_cols) * depth * heads,
            transcendentals=0,
        ),
        compiler_params=pltpu.CompilerParams(vmem_limit_bytes=PROJECT_VMEM),
        name="project",
    )(me, accepted, owner_group, page_slot, w_key, w_value, *early)
    packed = pl.pallas_call(
        functools.partial(pack_kernel, slot_cap, draft),
        out_shape=jax.ShapeDtypeStruct((seq_count * stride, head_cols), jnp.bfloat16),
        in_specs=[vmem] * (5 + len(late)),
        out_specs=vmem,
        compiler_params=pltpu.CompilerParams(vmem_limit_bytes=OTHER_VMEM),
        name="pack",
    )(total, last_key, last_value, select, notes, *late)
    paired = packed.reshape(seq_count, stride // 2, 2, head_cols)
    arrived = lax.all_to_all(paired, "seq", split_axis=0, concat_axis=0, tiled=True).reshape(packed.shape)
    cache = jax.ShapeDtypeStruct((slot_total, draft, head_cols), jnp.bfloat16)
    return pl.pallas_call(
        functools.partial(place_kernel, slot_cap),
        out_shape=(cache, cache),
        in_specs=[vmem],
        out_specs=(vmem, vmem),
        scratch_shapes=[
            pltpu.VMEM((seq_count, 2 * slot_cap * draft, head_cols), jnp.bfloat16),
            pltpu.VMEM((slot_cap, seq_count * draft, head_cols), jnp.float32),
        ],
        compiler_params=pltpu.CompilerParams(vmem_limit_bytes=OTHER_VMEM),
        name="place",
    )(arrived)


def solution(mesh):
    placed = (
        P(("grp", "seq"), "head"),
        P(None, "head"),
        P(None, "head"),
        P(("grp", "seq")),
        P(("grp", "seq")),
        P(("grp", "seq")),
    )
    return jax.shard_map(
        local,
        mesh=mesh,
        in_specs=placed,
        out_specs=(P(("grp", "seq"), None, "head"), P(("grp", "seq"), None, "head")),
        check_vma=False,
    )
```

time: 130 us -> 126 us (0.969)
  blocking collectives: 75.2 us -> 68.8 us
  waiting for transfers between devices: 0.04 us -> 1.96 us
    all_to_all x1, blocking collectives: 75.2 us -> 68.8 us  [local(): lax.all_to_all(paired, 'seq', split_axis=0, concat_axis=0, tiled=True)]
    ppermute x14, waiting for transfers between devices: 0.04 us -> 1.96 us  [the longest x1 1.93 us: gather_ring(): lax.ppermute(falling[c], axes, down)]
  transfers between devices with their start and end apart: 14 -> 14, of which waited for: 0 -> 1; matrix products, arithmetic and copies ran while one was open for 0% -> 0% of each run, Pallas kernels for 4% -> 4%
where the time goes in v3:
time: 126 us; the launch traced here: 125 us
  blocking collectives  68.8 us (55%)
  starting transfers between devices  43.9 us (35%)
  Pallas kernels  6.68 us (5%)
  local copies, waits for them, and re-layouts  3.03 us (2%)
  waiting for transfers between devices  1.96 us (2%)
    all_to_all x1, blocking collectives, local(): lax.all_to_all(paired, 'seq', split_axis=0, concat_axis=0, tiled=True)  68.8 us
    ppermute x6, starting transfers between devices, gather_ring(): rising[c] = lax.ppermute(rising[c], axes, up)  26.9 us
    ppermute x6, starting transfers between devices, gather_ring(): falling[c] = lax.ppermute(falling[c], axes, down)  11.7 us
    pallas_call x1, Pallas kernels, local(): pl.pallas_call(functools.partial(project_kernel, offsets, slot_cap, draft...  4.89 us
    ppermute x1, starting transfers between devices, gather_ring(): lax.ppermute(rising[c], axes, up)  3.39 us
  transfers between devices with their start and end apart: 14, of which 1 were waited for; matrix products, arithmetic and copies ran while one was open for 0% of the time, Pallas kernels for 4%

profile of v3, /device:TPU:65, one launch (start us, length us, event | category | flops | bytes accessed | tf_op | source)
XLA Modules:
  0.0 125.4 jit_solution(13976648009339889782)
XLA Ops:
  0.6 1.1 fusion
  1.7 6.3 %collective-permute-start = (bf16[128,1024]{1,0:T(8,128)(2,1)S(1)}, bf16[128,1024]{1,0:T(8,128)(2,1)S(1)}, u32[]{:S(2)}, u32[]{:S(2)}) collective-permute-start(bf16[128,1024]{1,0:T(8,128)(2,1)S(1)} %get-tuple-element.13.refs_0_), channel_id=1, source_target_pairs={{0,1},{1,2},{2,3},{3,4},{4,5},{5,6},{6,7},{7,0},{8,15},{9,8},{10,9... | collective-permute-start | bytes 786440 | tf_op jit(solution)/shard_map/ppermute | solution.py:31
  8.0 2.0 %collective-permute-start.3 = (bf16[128,1024]{1,0:T(8,128)(2,1)S(1)}, bf16[128,1024]{1,0:T(8,128)(2,1)S(1)}, u32[]{:S(2)}, u32[]{:S(2)}) collective-permute-start(bf16[128,1024]{1,0:T(8,128)(2,1)S(1)} %get-tuple-element.12.refs_1_), channel_id=1, source_target_pairs={{0,7},{1,0},{2,1},{3,2},{4,3},{5,4},{6,5},{7,6},{8,9},{9,10},{10,1... | collective-permute-start | bytes 786440 | tf_op jit(solution)/shard_map/ppermute | solution.py:32
  10.0 2.0 %collective-permute-start.2 = (bf16[128,1024]{1,0:T(8,128)(2,1)S(1)}, bf16[128,1024]{1,0:T(8,128)(2,1)S(1)}, u32[]{:S(2)}, u32[]{:S(2)}) collective-permute-start(bf16[128,1024]{1,0:T(8,128)(2,1)S(1)} %get-tuple-element.13.refs_0_), channel_id=1, source_target_pairs={{0,7},{1,0},{2,1},{3,2},{4,3},{5,4},{6,5},{7,6},{8,9},{9,10},{10,1... | collective-permute-start | bytes 786440 | tf_op jit(solution)/shard_map/ppermute | solution.py:32
  11.9 4.6 %collective-permute-start.1 = (bf16[128,1024]{1,0:T(8,128)(2,1)S(1)}, bf16[128,1024]{1,0:T(8,128)(2,1)S(1)}, u32[]{:S(2)}, u32[]{:S(2)}) collective-permute-start(bf16[128,1024]{1,0:T(8,128)(2,1)S(1)} %get-tuple-element.12.refs_1_), channel_id=1, source_target_pairs={{0,1},{1,2},{2,3},{3,4},{4,5},{5,6},{6,7},{7,0},{8,15},{9,8},{10,9... | collective-permute-start | bytes 786440 | tf_op jit(solution)/shard_map/ppermute | solution.py:31
  16.5 0.0 collective-permute-done.refs_2_
  16.5 3.4 %collective-permute-start.4 = (bf16[128,1024]{1,0:T(8,128)(2,1)S(1)}, bf16[128,1024]{1,0:T(8,128)(2,1)S(1)}, u32[]{:S(2)}, u32[]{:S(2)}) collective-permute-start(bf16[128,1024]{1,0:T(8,128)(2,1)S(1)} %collective-permute-done.refs_2_), channel_id=1, source_target_pairs={{0,1},{1,2},{2,3},{3,4},{4,5},{5,6},{6,7},{7,0},{8,15},{9,8},{10,9... | collective-permute-start | bytes 786440 | tf_op jit(solution)/shard_map/ppermute | solution.py:31
  19.9 0.0 collective-permute-done.3.refs_5_
  20.0 2.0 %collective-permute-start.7 = (bf16[128,1024]{1,0:T(8,128)(2,1)S(1)}, bf16[128,1024]{1,0:T(8,128)(2,1)S(1)}, u32[]{:S(2)}, u32[]{:S(2)}) collective-permute-start(bf16[128,1024]{1,0:T(8,128)(2,1)S(1)} %collective-permute-done.3.refs_5_), channel_id=1, source_target_pairs={{0,7},{1,0},{2,1},{3,2},{4,3},{5,4},{6,5},{7,6},{8,9},{9,10},{10,1... | collective-permute-start | bytes 786440 | tf_op jit(solution)/shard_map/ppermute | solution.py:32
  21.9 0.0 collective-permute-done.2.refs_4_
  21.9 2.0 %collective-permute-start.6 = (bf16[128,1024]{1,0:T(8,128)(2,1)S(1)}, bf16[128,1024]{1,0:T(8,128)(2,1)S(1)}, u32[]{:S(2)}, u32[]{:S(2)}) collective-permute-start(bf16[128,1024]{1,0:T(8,128)(2,1)S(1)} %collective-permute-done.2.refs_4_), channel_id=1, source_target_pairs={{0,7},{1,0},{2,1},{3,2},{4,3},{5,4},{6,5},{7,6},{8,9},{9,10},{10,1... | collective-permute-start | bytes 786440 | tf_op jit(solution)/shard_map/ppermute | solution.py:32
  23.9 0.0 collective-permute-done.1.refs_3_
  23.9 4.6 %collective-permute-start.5 = (bf16[128,1024]{1,0:T(8,128)(2,1)S(1)}, bf16[128,1024]{1,0:T(8,128)(2,1)S(1)}, u32[]{:S(2)}, u32[]{:S(2)}) collective-permute-start(bf16[128,1024]{1,0:T(8,128)(2,1)S(1)} %collective-permute-done.1.refs_3_), channel_id=1, source_target_pairs={{0,1},{1,2},{2,3},{3,4},{4,5},{5,6},{6,7},{7,0},{8,15},{9,8},{10,9... | collective-permute-start | bytes 786440 | tf_op jit(solution)/shard_map/ppermute | solution.py:31
  28.5 3.4 %collective-permute-start.8 = (bf16[128,1024]{1,0:T(8,128)(2,1)S(1)}, bf16[128,1024]{1,0:T(8,128)(2,1)S(1)}, u32[]{:S(2)}, u32[]{:S(2)}) collective-permute-start(bf16[128,1024]{1,0:T(8,128)(2,1)S(1)} %collective-permute-done.4.refs_6_), channel_id=1, source_target_pairs={{0,1},{1,2},{2,3},{3,4},{4,5},{5,6},{6,7},{7,0},{8,15},{9,8},{10,9... | collective-permute-start | bytes 786440 | tf_op jit(solution)/shard_map/ppermute | solution.py:31
  31.9 2.0 %collective-permute-start.11 = (bf16[128,1024]{1,0:T(8,128)(2,1)S(1)}, bf16[128,1024]{1,0:T(8,128)(2,1)}, u32[]{:S(2)}, u32[]{:S(2)}) collective-permute-start(bf16[128,1024]{1,0:T(8,128)(2,1)S(1)} %collective-permute-done.7.refs_9_), channel_id=1, source_target_pairs={{0,7},{1,0},{2,1},{3,2},{4,3},{5,4},{6,5},{7,6},{8,9},{9,10},{10,1... | collective-permute-start | bytes 786440 | tf_op jit(solution)/shard_map/ppermute | solution.py:32
  33.9 2.0 %collective-permute-start.10 = (bf16[128,1024]{1,0:T(8,128)(2,1)S(1)}, bf16[128,1024]{1,0:T(8,128)(2,1)}, u32[]{:S(2)}, u32[]{:S(2)}) collective-permute-start(bf16[128,1024]{1,0:T(8,128)(2,1)S(1)} %collective-permute-done.6.refs_8_), channel_id=1, source_target_pairs={{0,7},{1,0},{2,1},{3,2},{4,3},{5,4},{6,5},{7,6},{8,9},{9,10},{10,1... | collective-permute-start | bytes 786440 | tf_op jit(solution)/shard_map/ppermute | solution.py:32
  35.9 0.0 collective-permute-done.5.refs_7_
  35.9 4.6 %collective-permute-start.9 = (bf16[128,1024]{1,0:T(8,128)(2,1)S(1)}, bf16[128,1024]{1,0:T(8,128)(2,1)}, u32[]{:S(2)}, u32[]{:S(2)}) collective-permute-start(bf16[128,1024]{1,0:T(8,128)(2,1)S(1)} %collective-permute-done.5.refs_7_), channel_id=1, source_target_pairs={{0,1},{1,2},{2,3},{3,4},{4,5},{5,6},{6,7},{7,0},{8,15},{9,8},{10,9... | collective-permute-start | bytes 786440 | tf_op jit(solution)/shard_map/ppermute | solution.py:31
  40.5 3.4 %collective-permute-start.12 = (bf16[128,1024]{1,0:T(8,128)(2,1)S(1)}, bf16[128,1024]{1,0:T(8,128)(2,1)S(1)}, u32[]{:S(2)}, u32[]{:S(2)}) collective-permute-start(bf16[128,1024]{1,0:T(8,128)(2,1)S(1)} %collective-permute-done.8.refs_10_), channel_id=1, source_target_pairs={{0,1},{1,2},{2,3},{3,4},{4,5},{5,6},{6,7},{7,0},{8,15},{9,8},{10,9... | collective-permute-start | bytes 786440 | tf_op jit(solution)/shard_map/ppermute | solution.py:37
  43.9 0.0 collective-permute-done.11.refs_13_
  43.9 2.0 %collective-permute-start.13 = (bf16[128,1024]{1,0:T(8,128)(2,1)}, bf16[128,1024]{1,0:T(8,128)(2,1)S(1)}, u32[]{:S(2)}, u32[]{:S(2)}) collective-permute-start(bf16[128,1024]{1,0:T(8,128)(2,1)} %collective-permute-done.11.refs_13_), channel_id=1, source_target_pairs={{0,7},{1,0},{2,1},{3,2},{4,3},{5,4},{6,5},{7,6},{8,9},{9,10},{10,1... | collective-permute-start | bytes 786440 | tf_op jit(solution)/shard_map/ppermute | solution.py:37
  45.9 0.1 pad_add_fusion.me_ref
  45.9 0.0 collective-permute-done.10.refs_12_
  46.0 0.7 copy-done
  46.6 0.7 copy-done.1
  47.3 0.7 copy-done.2
  47.9 4.9 %project.1 = (f32[256,256]{1,0:T(8,128)S(1)}, bf16[1024,128]{1,0:T(8,128)(2,1)S(1)}, bf16[1024,128]{1,0:T(8,128)(2,1)S(1)}, bf16[512,256]{1,0:T(8,128)(2,1)S(1)}, bf16[64,128]{1,0:T(8,128)(2,1)S(1)}) custom-call(s32[2]{0:T(128)S(1)} %pad_add_fusion.me_ref, s32[32]{0:T(128)S(1)} %copy-done, s32[32]{0:T(128)S(1)} %copy-done.1, s32[32]{0:T(128)S(1)} %copy-done.2, ...), custom_call_target="tpu_custom_call" | custom-call | flops 1073741824 | bytes 8388608 | tf_op jit(solution)/shard_map/project/pallas_call | solution.py:178
  52.8 0.0 collective-permute-done.12.refs_0_
  52.8 1.9 %collective-permute-done.13.refs_1_ = bf16[128,1024]{1,0:T(8,128)(2,1)S(1)} collective-permute-done((bf16[128,1024]{1,0:T(8,128)(2,1)}, bf16[128,1024]{1,0:T(8,128)(2,1)S(1)}, u32[]{:S(2)}, u32[]{:S(2)}) %collective-permute-start.13) | collective-permute-done | bytes 262176 | tf_op jit(solution)/shard_map/ppermute | solution.py:37
  54.8 0.6 pack.1
  55.4 68.8 %all_to_all.5 = bf16[32,17,2,128]{3,2,1,0:T(2,128)(2,1)S(1)} all-to-all(bf16[32,17,2,128]{3,2,1,0:T(2,128)(2,1)S(1)} %bitcast.4), channel_id=1, replica_groups=mesh['grp'=2,'seq'=32,'head'=8] {'seq'}, dimensions={0} | all-to-all | bytes 557056 | tf_op jit(solution)/shard_map/all_to_all | solution.py:210
  124.2 1.2 place.1
  (8 shorter events, 0.0 us)
Async XLA Ops:
  1.7 14.8 %collective-permute-start = (bf16[128,1024]{1,0:T(8,128)(2,1)S(1)}, bf16[128,1024]{1,0:T(8,128)(2,1)S(1)}, u32[]{:S(2)}, u32[]{:S(2)}) collective-permute-start(bf16[128,1024]{1,0:T(8,128)(2,1)S(1)} %get-tuple-element.13.refs_0_), channel_id=1, source_target_pairs={{0,1},{1,2},{2,3},{3,4},{4,5},{5,6},{6,7},{7,0},{8,15},{9,8},{10,9... | collective-permute-start | bytes 786440 | tf_op jit(solution)/shard_map/ppermute | solution.py:31
  8.0 11.9 %collective-permute-start.3 = (bf16[128,1024]{1,0:T(8,128)(2,1)S(1)}, bf16[128,1024]{1,0:T(8,128)(2,1)S(1)}, u32[]{:S(2)}, u32[]{:S(2)}) collective-permute-start(bf16[128,1024]{1,0:T(8,128)(2,1)S(1)} %get-tuple-element.12.refs_1_), channel_id=1, source_target_pairs={{0,7},{1,0},{2,1},{3,2},{4,3},{5,4},{6,5},{7,6},{8,9},{9,10},{10,1... | collective-permute-start | bytes 786440 | tf_op jit(solution)/shard_map/ppermute | solution.py:32
  10.0 12.0 %collective-permute-start.2 = (bf16[128,1024]{1,0:T(8,128)(2,1)S(1)}, bf16[128,1024]{1,0:T(8,128)(2,1)S(1)}, u32[]{:S(2)}, u32[]{:S(2)}) collective-permute-start(bf16[128,1024]{1,0:T(8,128)(2,1)S(1)} %get-tuple-element.13.refs_0_), channel_id=1, source_target_pairs={{0,7},{1,0},{2,1},{3,2},{4,3},{5,4},{6,5},{7,6},{8,9},{9,10},{10,1... | collective-permute-start | bytes 786440 | tf_op jit(solution)/shard_map/ppermute | solution.py:32
  11.9 12.0 %collective-permute-start.1 = (bf16[128,1024]{1,0:T(8,128)(2,1)S(1)}, bf16[128,1024]{1,0:T(8,128)(2,1)S(1)}, u32[]{:S(2)}, u32[]{:S(2)}) collective-permute-start(bf16[128,1024]{1,0:T(8,128)(2,1)S(1)} %get-tuple-element.12.refs_1_), channel_id=1, source_target_pairs={{0,1},{1,2},{2,3},{3,4},{4,5},{5,6},{6,7},{7,0},{8,15},{9,8},{10,9... | collective-permute-start | bytes 786440 | tf_op jit(solution)/shard_map/ppermute | solution.py:31
  16.5 12.0 %collective-permute-start.4 = (bf16[128,1024]{1,0:T(8,128)(2,1)S(1)}, bf16[128,1024]{1,0:T(8,128)(2,1)S(1)}, u32[]{:S(2)}, u32[]{:S(2)}) collective-permute-start(bf16[128,1024]{1,0:T(8,128)(2,1)S(1)} %collective-permute-done.refs_2_), channel_id=1, source_target_pairs={{0,1},{1,2},{2,3},{3,4},{4,5},{5,6},{6,7},{7,0},{8,15},{9,8},{10,9... | collective-permute-start | bytes 786440 | tf_op jit(solution)/shard_map/ppermute | solution.py:31
  20.0 12.0 %collective-permute-start.7 = (bf16[128,1024]{1,0:T(8,128)(2,1)S(1)}, bf16[128,1024]{1,0:T(8,128)(2,1)S(1)}, u32[]{:S(2)}, u32[]{:S(2)}) collective-permute-start(bf16[128,1024]{1,0:T(8,128)(2,1)S(1)} %collective-permute-done.3.refs_5_), channel_id=1, source_target_pairs={{0,7},{1,0},{2,1},{3,2},{4,3},{5,4},{6,5},{7,6},{8,9},{9,10},{10,1... | collective-permute-start | bytes 786440 | tf_op jit(solution)/shard_map/ppermute | solution.py:32
  21.9 12.0 %collective-permute-start.6 = (bf16[128,1024]{1,0:T(8,128)(2,1)S(1)}, bf16[128,1024]{1,0:T(8,128)(2,1)S(1)}, u32[]{:S(2)}, u32[]{:S(2)}) collective-permute-start(bf16[128,1024]{1,0:T(8,128)(2,1)S(1)} %collective-permute-done.2.refs_4_), channel_id=1, source_target_pairs={{0,7},{1,0},{2,1},{3,2},{4,3},{5,4},{6,5},{7,6},{8,9},{9,10},{10,1... | collective-permute-start | bytes 786440 | tf_op jit(solution)/shard_map/ppermute | solution.py:32
  23.9 12.0 %collective-permute-start.5 = (bf16[128,1024]{1,0:T(8,128)(2,1)S(1)}, bf16[128,1024]{1,0:T(8,128)(2,1)S(1)}, u32[]{:S(2)}, u32[]{:S(2)}) collective-permute-start(bf16[128,1024]{1,0:T(8,128)(2,1)S(1)} %collective-permute-done.1.refs_3_), channel_id=1, source_target_pairs={{0,1},{1,2},{2,3},{3,4},{4,5},{5,6},{6,7},{7,0},{8,15},{9,8},{10,9... | collective-permute-start | bytes 786440 | tf_op jit(solution)/shard_map/ppermute | solution.py:31
  28.5 12.0 %collective-permute-start.8 = (bf16[128,1024]{1,0:T(8,128)(2,1)S(1)}, bf16[128,1024]{1,0:T(8,128)(2,1)S(1)}, u32[]{:S(2)}, u32[]{:S(2)}) collective-permute-start(bf16[128,1024]{1,0:T(8,128)(2,1)S(1)} %collective-permute-done.4.refs_6_), channel_id=1, source_target_pairs={{0,1},{1,2},{2,3},{3,4},{4,5},{5,6},{6,7},{7,0},{8,15},{9,8},{10,9... | collective-permute-start | bytes 786440 | tf_op jit(solution)/shard_map/ppermute | solution.py:31
  31.9 12.0 %collective-permute-start.11 = (bf16[128,1024]{1,0:T(8,128)(2,1)S(1)}, bf16[128,1024]{1,0:T(8,128)(2,1)}, u32[]{:S(2)}, u32[]{:S(2)}) collective-permute-start(bf16[128,1024]{1,0:T(8,128)(2,1)S(1)} %collective-permute-done.7.refs_9_), channel_id=1, source_target_pairs={{0,7},{1,0},{2,1},{3,2},{4,3},{5,4},{6,5},{7,6},{8,9},{9,10},{10,1... | collective-permute-start | bytes 786440 | tf_op jit(solution)/shard_map/ppermute | solution.py:32
  33.9 12.0 %collective-permute-start.10 = (bf16[128,1024]{1,0:T(8,128)(2,1)S(1)}, bf16[128,1024]{1,0:T(8,128)(2,1)}, u32[]{:S(2)}, u32[]{:S(2)}) collective-permute-start(bf16[128,1024]{1,0:T(8,128)(2,1)S(1)} %collective-permute-done.6.refs_8_), channel_id=1, source_target_pairs={{0,7},{1,0},{2,1},{3,2},{4,3},{5,4},{6,5},{7,6},{8,9},{9,10},{10,1... | collective-permute-start | bytes 786440 | tf_op jit(solution)/shard_map/ppermute | solution.py:32
  35.9 10.1 %collective-permute-start.9 = (bf16[128,1024]{1,0:T(8,128)(2,1)S(1)}, bf16[128,1024]{1,0:T(8,128)(2,1)}, u32[]{:S(2)}, u32[]{:S(2)}) collective-permute-start(bf16[128,1024]{1,0:T(8,128)(2,1)S(1)} %collective-permute-done.5.refs_7_), channel_id=1, source_target_pairs={{0,1},{1,2},{2,3},{3,4},{4,5},{5,6},{6,7},{7,0},{8,15},{9,8},{10,9... | collective-permute-start | bytes 786440 | tf_op jit(solution)/shard_map/ppermute | solution.py:31
  40.5 12.3 %collective-permute-start.12 = (bf16[128,1024]{1,0:T(8,128)(2,1)S(1)}, bf16[128,1024]{1,0:T(8,128)(2,1)S(1)}, u32[]{:S(2)}, u32[]{:S(2)}) collective-permute-start(bf16[128,1024]{1,0:T(8,128)(2,1)S(1)} %collective-permute-done.8.refs_10_), channel_id=1, source_target_pairs={{0,1},{1,2},{2,3},{3,4},{4,5},{5,6},{6,7},{7,0},{8,15},{9,8},{10,9... | collective-permute-start | bytes 786440 | tf_op jit(solution)/shard_map/ppermute | solution.py:37
  43.9 10.9 %collective-permute-start.13 = (bf16[128,1024]{1,0:T(8,128)(2,1)}, bf16[128,1024]{1,0:T(8,128)(2,1)S(1)}, u32[]{:S(2)}, u32[]{:S(2)}) collective-permute-start(bf16[128,1024]{1,0:T(8,128)(2,1)} %collective-permute-done.11.refs_13_), channel_id=1, source_target_pairs={{0,7},{1,0},{2,1},{3,2},{4,3},{5,4},{6,5},{7,6},{8,9},{9,10},{10,1... | collective-permute-start | bytes 786440 | tf_op jit(solution)/shard_map/ppermute | solution.py:37
  45.9 0.7 copy-start
  46.6 0.7 copy-start.1
  47.3 0.7 copy-start.2

commit v4 on v3

--- a/solution.py
+++ b/solution.py
@@ -8,7 +8,7 @@
 from jax.sharding import PartitionSpec as P
 
 CHUNKS = 2
-PROJECT_VMEM = 50 * 2**20
+PROJECT_VMEM = 49 * 2**20
 OTHER_VMEM = 12 * 2**20
 
 
@@ -45,7 +45,7 @@
     return lax.broadcasted_iota(jnp.int32, shape, dim)
 
 
-def project_kernel(offsets, slot_cap, draft, me_ref, accepted_ref, owner_ref, page_ref, wk_ref, wv_ref, *refs):
+def project_kernel(offsets, slot_cap, draft, owners, me_ref, turn_ref, route_ref, wk_ref, wv_ref, *refs):
     count = len(offsets) - 1
     blocks = refs[: count * CHUNKS]
     total_ref, lastk_ref, lastv_ref, select_ref, notes_ref, weights, sems = refs[count * CHUNKS :]
@@ -53,21 +53,19 @@
     heads = len(offsets)
     fetches = []
     for i, offset in enumerate(offsets):
-        origin = lax.rem(me_ref[0] + me_ref[1] * offset + heads, heads)
+        origin = lax.rem(me_ref[0] + turn_ref[0] * offset + heads, heads)
         at = pl.ds(pl.multiple_of(origin * depth, depth), depth)
         to = (weights.at[i, 0], weights.at[i, 1]) if i < count else (lastk_ref, lastv_ref)
         for j, w in enumerate((wk_ref, wv_ref)):
             fetches.append(pltpu.make_async_copy(w.at[at, :], to[j], sems.at[2 * i + j]))
     for fetch in fetches:
         fetch.start()
-    req = owner_ref.shape[0]
-    spot = iota((1, req), 1)
-    accepted = owner = page = jnp.zeros((1, req), jnp.int32)
-    for r in range(req):
-        accepted = jnp.where(spot == r, accepted_ref[r], accepted)
-        owner = jnp.where(spot == r, owner_ref[r], owner)
-        page = jnp.where(spot == r, page_ref[r], page)
-    accepted, owner, page = (a.astype(jnp.float32) for a in (accepted, owner, page))
+    req = route_ref.shape[1]
+    slots = owners * slot_cap
+    route = route_ref[...]
+    page = lax.rem(route, slots).astype(jnp.float32)
+    owner = lax.rem(lax.div(route, slots), owners).astype(jnp.float32)
+    accepted = lax.div(route, slots * owners).astype(jnp.float32)
     diagonal = iota((req, req), 0) == iota((req, req), 1)
     owner_col = jnp.sum(jnp.where(diagonal, owner, 0.0), axis=1, keepdims=True)
     earlier = (owner_col == owner) & (iota((req, req), 0) < iota((req, req), 1))
@@ -164,8 +162,9 @@
     seq_count = lax.axis_size("seq")
     slot_cap = max(2, 2 * req_dev // seq_count)
     slot_total = slot_cap * seq_count
-    turn = 1 - 2 * lax.rem(lax.axis_index("seq"), 2)
-    me = jnp.stack([lax.axis_index("head"), turn]).astype(jnp.int32)
+    me = lax.axis_index("head").astype(jnp.int32).reshape(1)
+    turn = (1 - 2 * (lax.axis_index("seq") & 1)).astype(jnp.int32).reshape(1)
+    route = ((accepted * seq_count + owner_group) * slot_total + page_slot).reshape(1, req_dev)
     held = gather_ring(draft_features)
     offsets = tuple(offset for offset, _ in held)
     blocks = [b for _, chunks in held for b in chunks]
@@ -176,7 +175,7 @@
     row_count, heads = req_dev * draft, len(offsets)
     stride = 2 * slot_cap * draft + slot_cap
     total, last_key, last_value, select, notes = pl.pallas_call(
-        functools.partial(project_kernel, offsets, slot_cap, draft),
+        functools.partial(project_kernel, offsets, slot_cap, draft, seq_count),
         out_shape=(
             jax.ShapeDtypeStruct((row_count, 2 * head_cols), jnp.float32),
             jax.ShapeDtypeStruct((depth, head_cols), jnp.bfloat16),
@@ -184,7 +183,7 @@
             jax.ShapeDtypeStruct((slot_total * draft, row_count), jnp.bfloat16),
             jax.ShapeDtypeStruct((slot_total, head_cols), jnp.bfloat16),
         ),
-        in_specs=[smem] * 4 + [hbm] * 2 + [vmem] * len(early),
+        in_specs=[smem, smem, vmem] + [hbm] * 2 + [vmem] * len(early),
         out_specs=(vmem,) * 5,
         scratch_shapes=[
             pltpu.VMEM((heads - 1, 2, depth, head_cols), jnp.bfloat16),
@@ -197,7 +196,7 @@
         ),
         compiler_params=pltpu.CompilerParams(vmem_limit_bytes=PROJECT_VMEM),
         name="project",
-    )(me, accepted, owner_group, page_slot, w_key, w_value, *early)
+    )(me, turn, route, w_key, w_value, *early)
     packed = pl.pallas_call(
         functools.partial(pack_kernel, slot_cap, draft),
         out_shape=jax.ShapeDtypeStruct((seq_count * stride, head_cols), jnp.bfloat16),

time: 126 us -> 125 us (level)
  local copies, waits for them, and re-layouts: 3.03 us -> 1.07 us
  waiting for transfers between devices: 1.96 us -> 3.48 us
  blocking collectives: 68.8 us -> 67.3 us
    unnamed x6 -> x0, local copies, waits for them, and re-layouts: 1.96 us -> none
    all_to_all x1, blocking collectives: 68.8 us -> 67.3 us  [local(): lax.all_to_all(paired, 'seq', split_axis=0, concat_axis=0, tiled=True)]
    ppermute x1, waiting for transfers between devices: 1.93 us -> 3.44 us  [gather_ring(): lax.ppermute(falling[c], axes, down)]
  transfers between devices with their start and end apart: 14 -> 14, of which waited for: 1 -> 1; matrix products, arithmetic and copies ran while one was open for 0% -> 1% of each run, Pallas kernels for 4% -> 4%
where the time goes in v4:
time: 125 us; the launch traced here: 124 us
  blocking collectives  67.3 us (54%)
  starting transfers between devices  43.9 us (35%)
  Pallas kernels  6.52 us (5%)
  waiting for transfers between devices  3.48 us (3%)
    all_to_all x1, blocking collectives, local(): lax.all_to_all(paired, 'seq', split_axis=0, concat_axis=0, tiled=True)  67.3 us
    ppermute x6, starting transfers between devices, gather_ring(): rising[c] = lax.ppermute(rising[c], axes, up)  26.9 us
    ppermute x6, starting transfers between devices, gather_ring(): falling[c] = lax.ppermute(falling[c], axes, down)  11.7 us
    pallas_call x1, Pallas kernels, local(): pl.pallas_call(functools.partial(project_kernel, offsets, slot_cap, draft...  4.72 us
    ppermute x1, waiting for transfers between devices, gather_ring(): lax.ppermute(falling[c], axes, down)  3.44 us
    ppermute x1, starting transfers between devices, gather_ring(): lax.ppermute(rising[c], axes, up)  3.39 us
  transfers between devices with their start and end apart: 14, of which 1 were waited for; matrix products, arithmetic and copies ran while one was open for 1% of the time, Pallas kernels for 4%

profile of v4, /device:TPU:65, one launch (start us, length us, event | category | flops | bytes accessed | tf_op | source)
XLA Modules:
  0.0 123.9 jit_solution(3527265768530013485)
XLA Ops:
  0.6 1.1 fusion
  1.7 6.3 %collective-permute-start = (bf16[128,1024]{1,0:T(8,128)(2,1)S(1)}, bf16[128,1024]{1,0:T(8,128)(2,1)S(1)}, u32[]{:S(2)}, u32[]{:S(2)}) collective-permute-start(bf16[128,1024]{1,0:T(8,128)(2,1)S(1)} %get-tuple-element.13.refs_0_), channel_id=1, source_target_pairs={{0,1},{1,2},{2,3},{3,4},{4,5},{5,6},{6,7},{7,0},{8,15},{9,8},{10,9... | collective-permute-start | bytes 786440 | tf_op jit(solution)/shard_map/ppermute | solution.py:31
  8.0 2.0 %collective-permute-start.3 = (bf16[128,1024]{1,0:T(8,128)(2,1)S(1)}, bf16[128,1024]{1,0:T(8,128)(2,1)S(1)}, u32[]{:S(2)}, u32[]{:S(2)}) collective-permute-start(bf16[128,1024]{1,0:T(8,128)(2,1)S(1)} %get-tuple-element.12.refs_1_), channel_id=1, source_target_pairs={{0,7},{1,0},{2,1},{3,2},{4,3},{5,4},{6,5},{7,6},{8,9},{9,10},{10,1... | collective-permute-start | bytes 786440 | tf_op jit(solution)/shard_map/ppermute | solution.py:32
  10.0 2.0 %collective-permute-start.2 = (bf16[128,1024]{1,0:T(8,128)(2,1)S(1)}, bf16[128,1024]{1,0:T(8,128)(2,1)S(1)}, u32[]{:S(2)}, u32[]{:S(2)}) collective-permute-start(bf16[128,1024]{1,0:T(8,128)(2,1)S(1)} %get-tuple-element.13.refs_0_), channel_id=1, source_target_pairs={{0,7},{1,0},{2,1},{3,2},{4,3},{5,4},{6,5},{7,6},{8,9},{9,10},{10,1... | collective-permute-start | bytes 786440 | tf_op jit(solution)/shard_map/ppermute | solution.py:32
  11.9 4.6 %collective-permute-start.1 = (bf16[128,1024]{1,0:T(8,128)(2,1)S(1)}, bf16[128,1024]{1,0:T(8,128)(2,1)S(1)}, u32[]{:S(2)}, u32[]{:S(2)}) collective-permute-start(bf16[128,1024]{1,0:T(8,128)(2,1)S(1)} %get-tuple-element.12.refs_1_), channel_id=1, source_target_pairs={{0,1},{1,2},{2,3},{3,4},{4,5},{5,6},{6,7},{7,0},{8,15},{9,8},{10,9... | collective-permute-start | bytes 786440 | tf_op jit(solution)/shard_map/ppermute | solution.py:31
  16.5 0.0 collective-permute-done.refs_2_
  16.5 3.4 %collective-permute-start.4 = (bf16[128,1024]{1,0:T(8,128)(2,1)S(1)}, bf16[128,1024]{1,0:T(8,128)(2,1)S(1)}, u32[]{:S(2)}, u32[]{:S(2)}) collective-permute-start(bf16[128,1024]{1,0:T(8,128)(2,1)S(1)} %collective-permute-done.refs_2_), channel_id=1, source_target_pairs={{0,1},{1,2},{2,3},{3,4},{4,5},{5,6},{6,7},{7,0},{8,15},{9,8},{10,9... | collective-permute-start | bytes 786440 | tf_op jit(solution)/shard_map/ppermute | solution.py:31
  19.9 0.0 collective-permute-done.3.refs_5_
  20.0 2.0 %collective-permute-start.7 = (bf16[128,1024]{1,0:T(8,128)(2,1)S(1)}, bf16[128,1024]{1,0:T(8,128)(2,1)S(1)}, u32[]{:S(2)}, u32[]{:S(2)}) collective-permute-start(bf16[128,1024]{1,0:T(8,128)(2,1)S(1)} %collective-permute-done.3.refs_5_), channel_id=1, source_target_pairs={{0,7},{1,0},{2,1},{3,2},{4,3},{5,4},{6,5},{7,6},{8,9},{9,10},{10,1... | collective-permute-start | bytes 786440 | tf_op jit(solution)/shard_map/ppermute | solution.py:32
  21.9 2.0 %collective-permute-start.6 = (bf16[128,1024]{1,0:T(8,128)(2,1)S(1)}, bf16[128,1024]{1,0:T(8,128)(2,1)S(1)}, u32[]{:S(2)}, u32[]{:S(2)}) collective-permute-start(bf16[128,1024]{1,0:T(8,128)(2,1)S(1)} %collective-permute-done.2.refs_4_), channel_id=1, source_target_pairs={{0,7},{1,0},{2,1},{3,2},{4,3},{5,4},{6,5},{7,6},{8,9},{9,10},{10,1... | collective-permute-start | bytes 786440 | tf_op jit(solution)/shard_map/ppermute | solution.py:32
  23.9 0.0 collective-permute-done.1.refs_3_
  23.9 4.6 %collective-permute-start.5 = (bf16[128,1024]{1,0:T(8,128)(2,1)S(1)}, bf16[128,1024]{1,0:T(8,128)(2,1)S(1)}, u32[]{:S(2)}, u32[]{:S(2)}) collective-permute-start(bf16[128,1024]{1,0:T(8,128)(2,1)S(1)} %collective-permute-done.1.refs_3_), channel_id=1, source_target_pairs={{0,1},{1,2},{2,3},{3,4},{4,5},{5,6},{6,7},{7,0},{8,15},{9,8},{10,9... | collective-permute-start | bytes 786440 | tf_op jit(solution)/shard_map/ppermute | solution.py:31
  28.5 0.0 collective-permute-done.4.refs_6_
  28.5 3.4 %collective-permute-start.8 = (bf16[128,1024]{1,0:T(8,128)(2,1)S(1)}, bf16[128,1024]{1,0:T(8,128)(2,1)S(1)}, u32[]{:S(2)}, u32[]{:S(2)}) collective-permute-start(bf16[128,1024]{1,0:T(8,128)(2,1)S(1)} %collective-permute-done.4.refs_6_), channel_id=1, source_target_pairs={{0,1},{1,2},{2,3},{3,4},{4,5},{5,6},{6,7},{7,0},{8,15},{9,8},{10,9... | collective-permute-start | bytes 786440 | tf_op jit(solution)/shard_map/ppermute | solution.py:31
  31.9 0.0 collective-permute-done.7.refs_9_
  31.9 2.0 %collective-permute-start.11 = (bf16[128,1024]{1,0:T(8,128)(2,1)S(1)}, bf16[128,1024]{1,0:T(8,128)(2,1)S(1)}, u32[]{:S(2)}, u32[]{:S(2)}) collective-permute-start(bf16[128,1024]{1,0:T(8,128)(2,1)S(1)} %collective-permute-done.7.refs_9_), channel_id=1, source_target_pairs={{0,7},{1,0},{2,1},{3,2},{4,3},{5,4},{6,5},{7,6},{8,9},{9,10},{10,1... | collective-permute-start | bytes 786440 | tf_op jit(solution)/shard_map/ppermute | solution.py:32
  33.9 2.0 %collective-permute-start.10 = (bf16[128,1024]{1,0:T(8,128)(2,1)S(1)}, bf16[128,1024]{1,0:T(8,128)(2,1)S(1)}, u32[]{:S(2)}, u32[]{:S(2)}) collective-permute-start(bf16[128,1024]{1,0:T(8,128)(2,1)S(1)} %collective-permute-done.6.refs_8_), channel_id=1, source_target_pairs={{0,7},{1,0},{2,1},{3,2},{4,3},{5,4},{6,5},{7,6},{8,9},{9,10},{10,1... | collective-permute-start | bytes 786440 | tf_op jit(solution)/shard_map/ppermute | solution.py:32
  35.9 0.0 collective-permute-done.5.refs_7_
  35.9 4.6 %collective-permute-start.9 = (bf16[128,1024]{1,0:T(8,128)(2,1)S(1)}, bf16[128,1024]{1,0:T(8,128)(2,1)}, u32[]{:S(2)}, u32[]{:S(2)}) collective-permute-start(bf16[128,1024]{1,0:T(8,128)(2,1)S(1)} %collective-permute-done.5.refs_7_), channel_id=1, source_target_pairs={{0,1},{1,2},{2,3},{3,4},{4,5},{5,6},{6,7},{7,0},{8,15},{9,8},{10,9... | collective-permute-start | bytes 786440 | tf_op jit(solution)/shard_map/ppermute | solution.py:31
  40.5 0.0 collective-permute-done.8.refs_10_
  40.5 3.4 %collective-permute-start.12 = (bf16[128,1024]{1,0:T(8,128)(2,1)S(1)}, bf16[128,1024]{1,0:T(8,128)(2,1)S(1)}, u32[]{:S(2)}, u32[]{:S(2)}) collective-permute-start(bf16[128,1024]{1,0:T(8,128)(2,1)S(1)} %collective-permute-done.8.refs_10_), channel_id=1, source_target_pairs={{0,1},{1,2},{2,3},{3,4},{4,5},{5,6},{6,7},{7,0},{8,15},{9,8},{10,9... | collective-permute-start | bytes 786440 | tf_op jit(solution)/shard_map/ppermute | solution.py:37
  43.9 0.0 collective-permute-done.11.refs_13_
  43.9 2.0 %collective-permute-start.13 = (bf16[128,1024]{1,0:T(8,128)(2,1)S(1)}, bf16[128,1024]{1,0:T(8,128)(2,1)S(1)}, u32[]{:S(2)}, u32[]{:S(2)}) collective-permute-start(bf16[128,1024]{1,0:T(8,128)(2,1)S(1)} %collective-permute-done.11.refs_13_), channel_id=1, source_target_pairs={{0,7},{1,0},{2,1},{3,2},{4,3},{5,4},{6,5},{7,6},{8,9},{9,10},{10,1... | collective-permute-start | bytes 786440 | tf_op jit(solution)/shard_map/ppermute | solution.py:37
  45.9 0.7 add_bitcast_fusion.route_ref
  46.6 0.0 collective-permute-done.10.refs_12_
  46.6 0.0 collective-permute-done.9.refs_11_
  46.6 4.7 %project.1 = (f32[256,256]{1,0:T(8,128)S(1)}, bf16[1024,128]{1,0:T(8,128)(2,1)S(1)}, bf16[1024,128]{1,0:T(8,128)(2,1)S(1)}, bf16[512,256]{1,0:T(8,128)(2,1)S(1)}, bf16[64,128]{1,0:T(8,128)(2,1)S(1)}) custom-call(s32[1]{0:T(128)} %bitcast.me_ref, s32[1]{0:T(128)} %bitcast.1.turn_ref, s32[1,32]{1,0:T(1,128)S(1)} %add_bitcast_fusion.route_ref, ...), custom_call_target="tpu_custom_call" | custom-call | flops 1073741824 | bytes 8388608 | tf_op jit(solution)/shard_map/project/pallas_call | solution.py:177
  51.3 0.0 collective-permute-done.12.refs_0_
  51.3 3.4 %collective-permute-done.13.refs_1_ = bf16[128,1024]{1,0:T(8,128)(2,1)S(1)} collective-permute-done((bf16[128,1024]{1,0:T(8,128)(2,1)S(1)}, bf16[128,1024]{1,0:T(8,128)(2,1)S(1)}, u32[]{:S(2)}, u32[]{:S(2)}) %collective-permute-start.13) | collective-permute-done | bytes 262176 | tf_op jit(solution)/shard_map/ppermute | solution.py:37
  54.8 0.6 pack.1
  55.4 67.3 %all_to_all.5 = bf16[32,17,2,128]{3,2,1,0:T(2,128)(2,1)S(1)} all-to-all(bf16[32,17,2,128]{3,2,1,0:T(2,128)(2,1)S(1)} %bitcast.6), channel_id=1, replica_groups=mesh['grp'=2,'seq'=32,'head'=8] {'seq'}, dimensions={0} | all-to-all | bytes 557056 | tf_op jit(solution)/shard_map/all_to_all | solution.py:209
  122.7 1.2 place.1
  (2 shorter events, 0.0 us)
Async XLA Ops:
  1.7 14.8 %collective-permute-start = (bf16[128,1024]{1,0:T(8,128)(2,1)S(1)}, bf16[128,1024]{1,0:T(8,128)(2,1)S(1)}, u32[]{:S(2)}, u32[]{:S(2)}) collective-permute-start(bf16[128,1024]{1,0:T(8,128)(2,1)S(1)} %get-tuple-element.13.refs_0_), channel_id=1, source_target_pairs={{0,1},{1,2},{2,3},{3,4},{4,5},{5,6},{6,7},{7,0},{8,15},{9,8},{10,9... | collective-permute-start | bytes 786440 | tf_op jit(solution)/shard_map/ppermute | solution.py:31
  8.0 11.9 %collective-permute-start.3 = (bf16[128,1024]{1,0:T(8,128)(2,1)S(1)}, bf16[128,1024]{1,0:T(8,128)(2,1)S(1)}, u32[]{:S(2)}, u32[]{:S(2)}) collective-permute-start(bf16[128,1024]{1,0:T(8,128)(2,1)S(1)} %get-tuple-element.12.refs_1_), channel_id=1, source_target_pairs={{0,7},{1,0},{2,1},{3,2},{4,3},{5,4},{6,5},{7,6},{8,9},{9,10},{10,1... | collective-permute-start | bytes 786440 | tf_op jit(solution)/shard_map/ppermute | solution.py:32
  10.0 12.0 %collective-permute-start.2 = (bf16[128,1024]{1,0:T(8,128)(2,1)S(1)}, bf16[128,1024]{1,0:T(8,128)(2,1)S(1)}, u32[]{:S(2)}, u32[]{:S(2)}) collective-permute-start(bf16[128,1024]{1,0:T(8,128)(2,1)S(1)} %get-tuple-element.13.refs_0_), channel_id=1, source_target_pairs={{0,7},{1,0},{2,1},{3,2},{4,3},{5,4},{6,5},{7,6},{8,9},{9,10},{10,1... | collective-permute-start | bytes 786440 | tf_op jit(solution)/shard_map/ppermute | solution.py:32
  11.9 12.0 %collective-permute-start.1 = (bf16[128,1024]{1,0:T(8,128)(2,1)S(1)}, bf16[128,1024]{1,0:T(8,128)(2,1)S(1)}, u32[]{:S(2)}, u32[]{:S(2)}) collective-permute-start(bf16[128,1024]{1,0:T(8,128)(2,1)S(1)} %get-tuple-element.12.refs_1_), channel_id=1, source_target_pairs={{0,1},{1,2},{2,3},{3,4},{4,5},{5,6},{6,7},{7,0},{8,15},{9,8},{10,9... | collective-permute-start | bytes 786440 | tf_op jit(solution)/shard_map/ppermute | solution.py:31
  16.5 12.0 %collective-permute-start.4 = (bf16[128,1024]{1,0:T(8,128)(2,1)S(1)}, bf16[128,1024]{1,0:T(8,128)(2,1)S(1)}, u32[]{:S(2)}, u32[]{:S(2)}) collective-permute-start(bf16[128,1024]{1,0:T(8,128)(2,1)S(1)} %collective-permute-done.refs_2_), channel_id=1, source_target_pairs={{0,1},{1,2},{2,3},{3,4},{4,5},{5,6},{6,7},{7,0},{8,15},{9,8},{10,9... | collective-permute-start | bytes 786440 | tf_op jit(solution)/shard_map/ppermute | solution.py:31
  20.0 12.0 %collective-permute-start.7 = (bf16[128,1024]{1,0:T(8,128)(2,1)S(1)}, bf16[128,1024]{1,0:T(8,128)(2,1)S(1)}, u32[]{:S(2)}, u32[]{:S(2)}) collective-permute-start(bf16[128,1024]{1,0:T(8,128)(2,1)S(1)} %collective-permute-done.3.refs_5_), channel_id=1, source_target_pairs={{0,7},{1,0},{2,1},{3,2},{4,3},{5,4},{6,5},{7,6},{8,9},{9,10},{10,1... | collective-permute-start | bytes 786440 | tf_op jit(solution)/shard_map/ppermute | solution.py:32
  21.9 12.0 %collective-permute-start.6 = (bf16[128,1024]{1,0:T(8,128)(2,1)S(1)}, bf16[128,1024]{1,0:T(8,128)(2,1)S(1)}, u32[]{:S(2)}, u32[]{:S(2)}) collective-permute-start(bf16[128,1024]{1,0:T(8,128)(2,1)S(1)} %collective-permute-done.2.refs_4_), channel_id=1, source_target_pairs={{0,7},{1,0},{2,1},{3,2},{4,3},{5,4},{6,5},{7,6},{8,9},{9,10},{10,1... | collective-permute-start | bytes 786440 | tf_op jit(solution)/shard_map/ppermute | solution.py:32
  23.9 12.0 %collective-permute-start.5 = (bf16[128,1024]{1,0:T(8,128)(2,1)S(1)}, bf16[128,1024]{1,0:T(8,128)(2,1)S(1)}, u32[]{:S(2)}, u32[]{:S(2)}) collective-permute-start(bf16[128,1024]{1,0:T(8,128)(2,1)S(1)} %collective-permute-done.1.refs_3_), channel_id=1, source_target_pairs={{0,1},{1,2},{2,3},{3,4},{4,5},{5,6},{6,7},{7,0},{8,15},{9,8},{10,9... | collective-permute-start | bytes 786440 | tf_op jit(solution)/shard_map/ppermute | solution.py:31
  28.5 12.0 %collective-permute-start.8 = (bf16[128,1024]{1,0:T(8,128)(2,1)S(1)}, bf16[128,1024]{1,0:T(8,128)(2,1)S(1)}, u32[]{:S(2)}, u32[]{:S(2)}) collective-permute-start(bf16[128,1024]{1,0:T(8,128)(2,1)S(1)} %collective-permute-done.4.refs_6_), channel_id=1, source_target_pairs={{0,1},{1,2},{2,3},{3,4},{4,5},{5,6},{6,7},{7,0},{8,15},{9,8},{10,9... | collective-permute-start | bytes 786440 | tf_op jit(solution)/shard_map/ppermute | solution.py:31
  31.9 12.0 %collective-permute-start.11 = (bf16[128,1024]{1,0:T(8,128)(2,1)S(1)}, bf16[128,1024]{1,0:T(8,128)(2,1)S(1)}, u32[]{:S(2)}, u32[]{:S(2)}) collective-permute-start(bf16[128,1024]{1,0:T(8,128)(2,1)S(1)} %collective-permute-done.7.refs_9_), channel_id=1, source_target_pairs={{0,7},{1,0},{2,1},{3,2},{4,3},{5,4},{6,5},{7,6},{8,9},{9,10},{10,1... | collective-permute-start | bytes 786440 | tf_op jit(solution)/shard_map/ppermute | solution.py:32
  33.9 12.7 %collective-permute-start.10 = (bf16[128,1024]{1,0:T(8,128)(2,1)S(1)}, bf16[128,1024]{1,0:T(8,128)(2,1)S(1)}, u32[]{:S(2)}, u32[]{:S(2)}) collective-permute-start(bf16[128,1024]{1,0:T(8,128)(2,1)S(1)} %collective-permute-done.6.refs_8_), channel_id=1, source_target_pairs={{0,7},{1,0},{2,1},{3,2},{4,3},{5,4},{6,5},{7,6},{8,9},{9,10},{10,1... | collective-permute-start | bytes 786440 | tf_op jit(solution)/shard_map/ppermute | solution.py:32
  35.9 10.7 %collective-permute-start.9 = (bf16[128,1024]{1,0:T(8,128)(2,1)S(1)}, bf16[128,1024]{1,0:T(8,128)(2,1)}, u32[]{:S(2)}, u32[]{:S(2)}) collective-permute-start(bf16[128,1024]{1,0:T(8,128)(2,1)S(1)} %collective-permute-done.5.refs_7_), channel_id=1, source_target_pairs={{0,1},{1,2},{2,3},{3,4},{4,5},{5,6},{6,7},{7,0},{8,15},{9,8},{10,9... | collective-permute-start | bytes 786440 | tf_op jit(solution)/shard_map/ppermute | solution.py:31
  40.5 10.8 %collective-permute-start.12 = (bf16[128,1024]{1,0:T(8,128)(2,1)S(1)}, bf16[128,1024]{1,0:T(8,128)(2,1)S(1)}, u32[]{:S(2)}, u32[]{:S(2)}) collective-permute-start(bf16[128,1024]{1,0:T(8,128)(2,1)S(1)} %collective-permute-done.8.refs_10_), channel_id=1, source_target_pairs={{0,1},{1,2},{2,3},{3,4},{4,5},{5,6},{6,7},{7,0},{8,15},{9,8},{10,9... | collective-permute-start | bytes 786440 | tf_op jit(solution)/shard_map/ppermute | solution.py:37
  43.9 10.8 %collective-permute-start.13 = (bf16[128,1024]{1,0:T(8,128)(2,1)S(1)}, bf16[128,1024]{1,0:T(8,128)(2,1)S(1)}, u32[]{:S(2)}, u32[]{:S(2)}) collective-permute-start(bf16[128,1024]{1,0:T(8,128)(2,1)S(1)} %collective-permute-done.11.refs_13_), channel_id=1, source_target_pairs={{0,7},{1,0},{2,1},{3,2},{4,3},{5,4},{6,5},{7,6},{8,9},{9,10},{10,1... | collective-permute-start | bytes 786440 | tf_op jit(solution)/shard_map/ppermute | solution.py:37

commit v5 on v4

--- a/solution.py
+++ b/solution.py
@@ -117,19 +117,26 @@
         out_ref[at + 2 * span : at + stride, :] = notes_ref[d * slot_cap : (d + 1) * slot_cap, :]
 
 
-def place_kernel(slot_cap, arrived_ref, key_ref, value_ref, rows_ref, notes_ref):
+def place_kernel(slot_cap, side_ref, own_ref, other_ref, key_ref, value_ref, rows_ref, notes_ref):
     pages, draft, head_cols = key_ref.shape
     span = slot_cap * draft
     stride = 2 * span + slot_cap
-    sources = arrived_ref.shape[0] // stride
+    sources = rows_ref.shape[0]
     rows = sources * draft
-    for d in range(sources):
-        rows_ref[d] = arrived_ref[d * stride : d * stride + 2 * span, :]
-        notes = arrived_ref[d * stride + 2 * span : (d + 1) * stride, :].astype(jnp.float32)
-        for s in range(slot_cap):
-            notes_ref[s, d * draft : (d + 1) * draft, :] = jnp.broadcast_to(
-                notes[s : s + 1, :], (draft, head_cols)
-            )
+
+    def take(side):
+        for d in range(sources):
+            from_ref = own_ref if 2 * d < sources else other_ref
+            at = (2 * (d % (sources // 2)) + side) * stride
+            rows_ref[d] = from_ref[at : at + 2 * span, :]
+            notes = from_ref[at + 2 * span : at + stride, :].astype(jnp.float32)
+            for s in range(slot_cap):
+                notes_ref[s, d * draft : (d + 1) * draft, :] = jnp.broadcast_to(
+                    notes[s : s + 1, :], (draft, head_cols)
+                )
+
+    for side in range(2):
+        pl.when(side_ref[0] == side)(functools.partial(take, side))
     draft_row = lax.rem(iota((rows, head_cols), 0), draft).astype(jnp.float32)
     total = None
     for s in range(slot_cap):
@@ -163,7 +170,8 @@
     slot_cap = max(2, 2 * req_dev // seq_count)
     slot_total = slot_cap * seq_count
     me = lax.axis_index("head").astype(jnp.int32).reshape(1)
-    turn = (1 - 2 * (lax.axis_index("seq") & 1)).astype(jnp.int32).reshape(1)
+    side = (lax.axis_index("seq") & 1).astype(jnp.int32).reshape(1)
+    turn = 1 - 2 * side
     route = ((accepted * seq_count + owner_group) * slot_total + page_slot).reshape(1, req_dev)
     held = gather_ring(draft_features)
     offsets = tuple(offset for offset, _ in held)
@@ -205,13 +213,17 @@
         compiler_params=pltpu.CompilerParams(vmem_limit_bytes=OTHER_VMEM),
         name="pack",
     )(total, last_key, last_value, select, notes, *late)
-    paired = packed.reshape(seq_count, stride // 2, 2, head_cols)
-    arrived = lax.all_to_all(paired, "seq", split_axis=0, concat_axis=0, tiled=True).reshape(packed.shape)
+    paired = packed.reshape(seq_count // 2, stride, 2, head_cols)
+    sides = [list(range(side, seq_count, 2)) for side in range(2)]
+    arrived = lax.all_to_all(
+        paired, "seq", split_axis=0, concat_axis=0, tiled=True, axis_index_groups=sides
+    ).reshape(packed.shape)
+    shared = lax.ppermute(arrived, "seq", [(i, i ^ 1) for i in range(seq_count)])
     cache = jax.ShapeDtypeStruct((slot_total, draft, head_cols), jnp.bfloat16)
     return pl.pallas_call(
         functools.partial(place_kernel, slot_cap),
         out_shape=(cache, cache),
-        in_specs=[vmem],
+        in_specs=[smem, vmem, vmem],
         out_specs=(vmem, vmem),
         scratch_shapes=[
             pltpu.VMEM((seq_count, 2 * slot_cap * draft, head_cols), jnp.bfloat16),
@@ -219,7 +231,7 @@
         ],
         compiler_params=pltpu.CompilerParams(vmem_limit_bytes=OTHER_VMEM),
         name="place",
-    )(arrived)
+    )(side, arrived, shared)
 
 
 def solution(mesh):

time: 125 us -> 124 us (level)
  blocking collectives: 67.3 us -> 57.6 us
  starting transfers between devices: 43.9 us -> 51.9 us
    all_to_all x1, blocking collectives: 67.3 us -> 57.6 us  [local(): lax.all_to_all(paired, 'seq', split_axis=0, concat_axis=0, tiled=True, ax...]
    ppermute x0 -> x1, starting transfers between devices: none -> 7.92 us  [local(): lax.ppermute(arrived, 'seq', [(i, i ^ 1) for i in range(seq_count)])]
  transfers between devices with their start and end apart: 14 -> 15, of which waited for: 1 -> 2; matrix products, arithmetic and copies ran while one was open for 1% -> 1% of each run, Pallas kernels for 4% -> 4%
where the time goes in v5:
time: 124 us; the launch traced here: 123 us
  blocking collectives  57.6 us (46%)
  starting transfers between devices  51.9 us (42%)
  Pallas kernels  6.53 us (5%)
  waiting for transfers between devices  4.64 us (4%)
    all_to_all x1, blocking collectives, local(): lax.all_to_all(paired, 'seq', split_axis=0, concat_axis=0, tiled=True, ax...  57.6 us
    ppermute x6, starting transfers between devices, gather_ring(): rising[c] = lax.ppermute(rising[c], axes, up)  26.9 us
    ppermute x6, starting transfers between devices, gather_ring(): falling[c] = lax.ppermute(falling[c], axes, down)  11.7 us
    ppermute x1, starting transfers between devices, local(): lax.ppermute(arrived, 'seq', [(i, i ^ 1) for i in range(seq_count)])  7.92 us
    pallas_call x1, Pallas kernels, local(): pl.pallas_call(functools.partial(project_kernel, offsets, slot_cap, draft...  4.72 us
    ppermute x1, waiting for transfers between devices, gather_ring(): lax.ppermute(falling[c], axes, down)  3.44 us
    ppermute x1, starting transfers between devices, gather_ring(): lax.ppermute(rising[c], axes, up)  3.39 us
  transfers between devices with their start and end apart: 15, of which 2 were waited for; matrix products, arithmetic and copies ran while one was open for 1% of the time, Pallas kernels for 4%

profile of v5, /device:TPU:65, one launch (start us, length us, event | category | flops | bytes accessed | tf_op | source)
XLA Modules:
  0.0 123.2 jit_solution(11885026156634758775)
XLA Ops:
  0.6 1.1 fusion
  1.7 6.3 %collective-permute-start = (bf16[128,1024]{1,0:T(8,128)(2,1)S(1)}, bf16[128,1024]{1,0:T(8,128)(2,1)S(1)}, u32[]{:S(2)}, u32[]{:S(2)}) collective-permute-start(bf16[128,1024]{1,0:T(8,128)(2,1)S(1)} %get-tuple-element.13.refs_0_), channel_id=1, source_target_pairs={{0,1},{1,2},{2,3},{3,4},{4,5},{5,6},{6,7},{7,0},{8,15},{9,8},{10,9... | collective-permute-start | bytes 786440 | tf_op jit(solution)/shard_map/ppermute | solution.py:31
  8.0 2.0 %collective-permute-start.3 = (bf16[128,1024]{1,0:T(8,128)(2,1)S(1)}, bf16[128,1024]{1,0:T(8,128)(2,1)S(1)}, u32[]{:S(2)}, u32[]{:S(2)}) collective-permute-start(bf16[128,1024]{1,0:T(8,128)(2,1)S(1)} %get-tuple-element.12.refs_1_), channel_id=1, source_target_pairs={{0,7},{1,0},{2,1},{3,2},{4,3},{5,4},{6,5},{7,6},{8,9},{9,10},{10,1... | collective-permute-start | bytes 786440 | tf_op jit(solution)/shard_map/ppermute | solution.py:32
  10.0 2.0 %collective-permute-start.2 = (bf16[128,1024]{1,0:T(8,128)(2,1)S(1)}, bf16[128,1024]{1,0:T(8,128)(2,1)S(1)}, u32[]{:S(2)}, u32[]{:S(2)}) collective-permute-start(bf16[128,1024]{1,0:T(8,128)(2,1)S(1)} %get-tuple-element.13.refs_0_), channel_id=1, source_target_pairs={{0,7},{1,0},{2,1},{3,2},{4,3},{5,4},{6,5},{7,6},{8,9},{9,10},{10,1... | collective-permute-start | bytes 786440 | tf_op jit(solution)/shard_map/ppermute | solution.py:32
  11.9 4.6 %collective-permute-start.1 = (bf16[128,1024]{1,0:T(8,128)(2,1)S(1)}, bf16[128,1024]{1,0:T(8,128)(2,1)S(1)}, u32[]{:S(2)}, u32[]{:S(2)}) collective-permute-start(bf16[128,1024]{1,0:T(8,128)(2,1)S(1)} %get-tuple-element.12.refs_1_), channel_id=1, source_target_pairs={{0,1},{1,2},{2,3},{3,4},{4,5},{5,6},{6,7},{7,0},{8,15},{9,8},{10,9... | collective-permute-start | bytes 786440 | tf_op jit(solution)/shard_map/ppermute | solution.py:31
  16.5 0.0 collective-permute-done.refs_2_
  16.5 3.4 %collective-permute-start.4 = (bf16[128,1024]{1,0:T(8,128)(2,1)S(1)}, bf16[128,1024]{1,0:T(8,128)(2,1)S(1)}, u32[]{:S(2)}, u32[]{:S(2)}) collective-permute-start(bf16[128,1024]{1,0:T(8,128)(2,1)S(1)} %collective-permute-done.refs_2_), channel_id=1, source_target_pairs={{0,1},{1,2},{2,3},{3,4},{4,5},{5,6},{6,7},{7,0},{8,15},{9,8},{10,9... | collective-permute-start | bytes 786440 | tf_op jit(solution)/shard_map/ppermute | solution.py:31
  19.9 0.0 collective-permute-done.3.refs_5_
  20.0 2.0 %collective-permute-start.7 = (bf16[128,1024]{1,0:T(8,128)(2,1)S(1)}, bf16[128,1024]{1,0:T(8,128)(2,1)S(1)}, u32[]{:S(2)}, u32[]{:S(2)}) collective-permute-start(bf16[128,1024]{1,0:T(8,128)(2,1)S(1)} %collective-permute-done.3.refs_5_), channel_id=1, source_target_pairs={{0,7},{1,0},{2,1},{3,2},{4,3},{5,4},{6,5},{7,6},{8,9},{9,10},{10,1... | collective-permute-start | bytes 786440 | tf_op jit(solution)/shard_map/ppermute | solution.py:32
  21.9 0.0 collective-permute-done.2.refs_4_
  21.9 2.0 %collective-permute-start.6 = (bf16[128,1024]{1,0:T(8,128)(2,1)S(1)}, bf16[128,1024]{1,0:T(8,128)(2,1)S(1)}, u32[]{:S(2)}, u32[]{:S(2)}) collective-permute-start(bf16[128,1024]{1,0:T(8,128)(2,1)S(1)} %collective-permute-done.2.refs_4_), channel_id=1, source_target_pairs={{0,7},{1,0},{2,1},{3,2},{4,3},{5,4},{6,5},{7,6},{8,9},{9,10},{10,1... | collective-permute-start | bytes 786440 | tf_op jit(solution)/shard_map/ppermute | solution.py:32
  23.9 0.0 collective-permute-done.1.refs_3_
  23.9 4.6 %collective-permute-start.5 = (bf16[128,1024]{1,0:T(8,128)(2,1)S(1)}, bf16[128,1024]{1,0:T(8,128)(2,1)S(1)}, u32[]{:S(2)}, u32[]{:S(2)}) collective-permute-start(bf16[128,1024]{1,0:T(8,128)(2,1)S(1)} %collective-permute-done.1.refs_3_), channel_id=1, source_target_pairs={{0,1},{1,2},{2,3},{3,4},{4,5},{5,6},{6,7},{7,0},{8,15},{9,8},{10,9... | collective-permute-start | bytes 786440 | tf_op jit(solution)/shard_map/ppermute | solution.py:31
  28.5 0.0 collective-permute-done.4.refs_6_
  28.5 3.4 %collective-permute-start.8 = (bf16[128,1024]{1,0:T(8,128)(2,1)S(1)}, bf16[128,1024]{1,0:T(8,128)(2,1)S(1)}, u32[]{:S(2)}, u32[]{:S(2)}) collective-permute-start(bf16[128,1024]{1,0:T(8,128)(2,1)S(1)} %collective-permute-done.4.refs_6_), channel_id=1, source_target_pairs={{0,1},{1,2},{2,3},{3,4},{4,5},{5,6},{6,7},{7,0},{8,15},{9,8},{10,9... | collective-permute-start | bytes 786440 | tf_op jit(solution)/shard_map/ppermute | solution.py:31
  31.9 0.0 collective-permute-done.7.refs_9_
  31.9 2.0 %collective-permute-start.11 = (bf16[128,1024]{1,0:T(8,128)(2,1)S(1)}, bf16[128,1024]{1,0:T(8,128)(2,1)S(1)}, u32[]{:S(2)}, u32[]{:S(2)}) collective-permute-start(bf16[128,1024]{1,0:T(8,128)(2,1)S(1)} %collective-permute-done.7.refs_9_), channel_id=1, source_target_pairs={{0,7},{1,0},{2,1},{3,2},{4,3},{5,4},{6,5},{7,6},{8,9},{9,10},{10,1... | collective-permute-start | bytes 786440 | tf_op jit(solution)/shard_map/ppermute | solution.py:32
  33.9 2.0 %collective-permute-start.10 = (bf16[128,1024]{1,0:T(8,128)(2,1)S(1)}, bf16[128,1024]{1,0:T(8,128)(2,1)S(1)}, u32[]{:S(2)}, u32[]{:S(2)}) collective-permute-start(bf16[128,1024]{1,0:T(8,128)(2,1)S(1)} %collective-permute-done.6.refs_8_), channel_id=1, source_target_pairs={{0,7},{1,0},{2,1},{3,2},{4,3},{5,4},{6,5},{7,6},{8,9},{9,10},{10,1... | collective-permute-start | bytes 786440 | tf_op jit(solution)/shard_map/ppermute | solution.py:32
  35.9 0.0 collective-permute-done.5.refs_7_
  35.9 4.6 %collective-permute-start.9 = (bf16[128,1024]{1,0:T(8,128)(2,1)S(1)}, bf16[128,1024]{1,0:T(8,128)(2,1)}, u32[]{:S(2)}, u32[]{:S(2)}) collective-permute-start(bf16[128,1024]{1,0:T(8,128)(2,1)S(1)} %collective-permute-done.5.refs_7_), channel_id=1, source_target_pairs={{0,1},{1,2},{2,3},{3,4},{4,5},{5,6},{6,7},{7,0},{8,15},{9,8},{10,9... | collective-permute-start | bytes 786440 | tf_op jit(solution)/shard_map/ppermute | solution.py:31
  40.5 3.4 %collective-permute-start.12 = (bf16[128,1024]{1,0:T(8,128)(2,1)S(1)}, bf16[128,1024]{1,0:T(8,128)(2,1)S(1)}, u32[]{:S(2)}, u32[]{:S(2)}) collective-permute-start(bf16[128,1024]{1,0:T(8,128)(2,1)S(1)} %collective-permute-done.8.refs_10_), channel_id=1, source_target_pairs={{0,1},{1,2},{2,3},{3,4},{4,5},{5,6},{6,7},{7,0},{8,15},{9,8},{10,9... | collective-permute-start | bytes 786440 | tf_op jit(solution)/shard_map/ppermute | solution.py:37
  43.9 2.0 %collective-permute-start.13 = (bf16[128,1024]{1,0:T(8,128)(2,1)S(1)}, bf16[128,1024]{1,0:T(8,128)(2,1)S(1)}, u32[]{:S(2)}, u32[]{:S(2)}) collective-permute-start(bf16[128,1024]{1,0:T(8,128)(2,1)S(1)} %collective-permute-done.11.refs_13_), channel_id=1, source_target_pairs={{0,7},{1,0},{2,1},{3,2},{4,3},{5,4},{6,5},{7,6},{8,9},{9,10},{10,1... | collective-permute-start | bytes 786440 | tf_op jit(solution)/shard_map/ppermute | solution.py:37
  45.9 0.7 add_bitcast_fusion.route_ref
  46.6 0.0 collective-permute-done.10.refs_12_
  46.6 4.7 %project.1 = (f32[256,256]{1,0:T(8,128)S(1)}, bf16[1024,128]{1,0:T(8,128)(2,1)S(1)}, bf16[1024,128]{1,0:T(8,128)(2,1)S(1)}, bf16[512,256]{1,0:T(8,128)(2,1)S(1)}, bf16[64,128]{1,0:T(8,128)(2,1)S(1)}) custom-call(s32[1]{0:T(128)} %bitcast.1.me_ref, s32[1]{0:T(128)S(6)} %sub.3.turn_ref, s32[1,32]{1,0:T(1,128)S(1)} %add_bitcast_fusion.route_ref, ...), custom_call_target="tpu_custom_call" | custom-call | flops 1073741824 | bytes 8388608 | tf_op jit(solution)/shard_map/project/pallas_call | solution.py:185
  51.3 0.0 collective-permute-done.12.refs_0_
  51.3 3.4 %collective-permute-done.13.refs_1_ = bf16[128,1024]{1,0:T(8,128)(2,1)S(1)} collective-permute-done((bf16[128,1024]{1,0:T(8,128)(2,1)S(1)}, bf16[128,1024]{1,0:T(8,128)(2,1)S(1)}, u32[]{:S(2)}, u32[]{:S(2)}) %collective-permute-start.13) | collective-permute-done | bytes 262176 | tf_op jit(solution)/shard_map/ppermute | solution.py:37
  54.8 0.6 pack.1
  55.4 57.6 %all_to_all.5 = bf16[16,34,2,128]{3,2,1,0:T(2,128)(2,1)S(1)} all-to-all(bf16[16,34,2,128]{3,2,1,0:T(2,128)(2,1)S(1)} %bitcast.6), channel_id=1, replica_groups={{0,16,32,48,64,80,96,112,128,144,160,176,192,208,224,240},{8,24,40,56,7..., dimensions={0} | all-to-all | bytes 557056 | tf_op jit(solution)/shard_map/all_to_all | solution.py:218
  113.0 7.9 %collective-permute-start.14 = (bf16[1088,128]{1,0:T(8,128)(2,1)S(1)}, bf16[1088,128]{1,0:T(8,128)(2,1)S(1)}, u32[]{:S(2)}, u32[]{:S(2)}) collective-permute-start(bf16[1088,128]{1,0:T(8,128)(2,1)S(1)} %bitcast.7), channel_id=1, source_target_pairs={{0,8},{8,0},{16,24},{24,16},{32,40},{40,32},{48,56},{56,48},{64,72... | collective-permute-start | bytes 835592 | tf_op jit(solution)/shard_map/ppermute | solution.py:221
  120.9 1.2 collective-permute-done.14.other_ref
  122.0 1.2 place.1
  (4 shorter events, 0.0 us)
Async XLA Ops:
  1.7 14.8 %collective-permute-start = (bf16[128,1024]{1,0:T(8,128)(2,1)S(1)}, bf16[128,1024]{1,0:T(8,128)(2,1)S(1)}, u32[]{:S(2)}, u32[]{:S(2)}) collective-permute-start(bf16[128,1024]{1,0:T(8,128)(2,1)S(1)} %get-tuple-element.13.refs_0_), channel_id=1, source_target_pairs={{0,1},{1,2},{2,3},{3,4},{4,5},{5,6},{6,7},{7,0},{8,15},{9,8},{10,9... | collective-permute-start | bytes 786440 | tf_op jit(solution)/shard_map/ppermute | solution.py:31
  8.0 11.9 %collective-permute-start.3 = (bf16[128,1024]{1,0:T(8,128)(2,1)S(1)}, bf16[128,1024]{1,0:T(8,128)(2,1)S(1)}, u32[]{:S(2)}, u32[]{:S(2)}) collective-permute-start(bf16[128,1024]{1,0:T(8,128)(2,1)S(1)} %get-tuple-element.12.refs_1_), channel_id=1, source_target_pairs={{0,7},{1,0},{2,1},{3,2},{4,3},{5,4},{6,5},{7,6},{8,9},{9,10},{10,1... | collective-permute-start | bytes 786440 | tf_op jit(solution)/shard_map/ppermute | solution.py:32
  10.0 12.0 %collective-permute-start.2 = (bf16[128,1024]{1,0:T(8,128)(2,1)S(1)}, bf16[128,1024]{1,0:T(8,128)(2,1)S(1)}, u32[]{:S(2)}, u32[]{:S(2)}) collective-permute-start(bf16[128,1024]{1,0:T(8,128)(2,1)S(1)} %get-tuple-element.13.refs_0_), channel_id=1, source_target_pairs={{0,7},{1,0},{2,1},{3,2},{4,3},{5,4},{6,5},{7,6},{8,9},{9,10},{10,1... | collective-permute-start | bytes 786440 | tf_op jit(solution)/shard_map/ppermute | solution.py:32
  11.9 12.0 %collective-permute-start.1 = (bf16[128,1024]{1,0:T(8,128)(2,1)S(1)}, bf16[128,1024]{1,0:T(8,128)(2,1)S(1)}, u32[]{:S(2)}, u32[]{:S(2)}) collective-permute-start(bf16[128,1024]{1,0:T(8,128)(2,1)S(1)} %get-tuple-element.12.refs_1_), channel_id=1, source_target_pairs={{0,1},{1,2},{2,3},{3,4},{4,5},{5,6},{6,7},{7,0},{8,15},{9,8},{10,9... | collective-permute-start | bytes 786440 | tf_op jit(solution)/shard_map/ppermute | solution.py:31
  16.5 12.0 %collective-permute-start.4 = (bf16[128,1024]{1,0:T(8,128)(2,1)S(1)}, bf16[128,1024]{1,0:T(8,128)(2,1)S(1)}, u32[]{:S(2)}, u32[]{:S(2)}) collective-permute-start(bf16[128,1024]{1,0:T(8,128)(2,1)S(1)} %collective-permute-done.refs_2_), channel_id=1, source_target_pairs={{0,1},{1,2},{2,3},{3,4},{4,5},{5,6},{6,7},{7,0},{8,15},{9,8},{10,9... | collective-permute-start | bytes 786440 | tf_op jit(solution)/shard_map/ppermute | solution.py:31
  20.0 12.0 %collective-permute-start.7 = (bf16[128,1024]{1,0:T(8,128)(2,1)S(1)}, bf16[128,1024]{1,0:T(8,128)(2,1)S(1)}, u32[]{:S(2)}, u32[]{:S(2)}) collective-permute-start(bf16[128,1024]{1,0:T(8,128)(2,1)S(1)} %collective-permute-done.3.refs_5_), channel_id=1, source_target_pairs={{0,7},{1,0},{2,1},{3,2},{4,3},{5,4},{6,5},{7,6},{8,9},{9,10},{10,1... | collective-permute-start | bytes 786440 | tf_op jit(solution)/shard_map/ppermute | solution.py:32
  21.9 12.0 %collective-permute-start.6 = (bf16[128,1024]{1,0:T(8,128)(2,1)S(1)}, bf16[128,1024]{1,0:T(8,128)(2,1)S(1)}, u32[]{:S(2)}, u32[]{:S(2)}) collective-permute-start(bf16[128,1024]{1,0:T(8,128)(2,1)S(1)} %collective-permute-done.2.refs_4_), channel_id=1, source_target_pairs={{0,7},{1,0},{2,1},{3,2},{4,3},{5,4},{6,5},{7,6},{8,9},{9,10},{10,1... | collective-permute-start | bytes 786440 | tf_op jit(solution)/shard_map/ppermute | solution.py:32
  23.9 12.0 %collective-permute-start.5 = (bf16[128,1024]{1,0:T(8,128)(2,1)S(1)}, bf16[128,1024]{1,0:T(8,128)(2,1)S(1)}, u32[]{:S(2)}, u32[]{:S(2)}) collective-permute-start(bf16[128,1024]{1,0:T(8,128)(2,1)S(1)} %collective-permute-done.1.refs_3_), channel_id=1, source_target_pairs={{0,1},{1,2},{2,3},{3,4},{4,5},{5,6},{6,7},{7,0},{8,15},{9,8},{10,9... | collective-permute-start | bytes 786440 | tf_op jit(solution)/shard_map/ppermute | solution.py:31
  28.5 12.0 %collective-permute-start.8 = (bf16[128,1024]{1,0:T(8,128)(2,1)S(1)}, bf16[128,1024]{1,0:T(8,128)(2,1)S(1)}, u32[]{:S(2)}, u32[]{:S(2)}) collective-permute-start(bf16[128,1024]{1,0:T(8,128)(2,1)S(1)} %collective-permute-done.4.refs_6_), channel_id=1, source_target_pairs={{0,1},{1,2},{2,3},{3,4},{4,5},{5,6},{6,7},{7,0},{8,15},{9,8},{10,9... | collective-permute-start | bytes 786440 | tf_op jit(solution)/shard_map/ppermute | solution.py:31
  31.9 12.0 %collective-permute-start.11 = (bf16[128,1024]{1,0:T(8,128)(2,1)S(1)}, bf16[128,1024]{1,0:T(8,128)(2,1)S(1)}, u32[]{:S(2)}, u32[]{:S(2)}) collective-permute-start(bf16[128,1024]{1,0:T(8,128)(2,1)S(1)} %collective-permute-done.7.refs_9_), channel_id=1, source_target_pairs={{0,7},{1,0},{2,1},{3,2},{4,3},{5,4},{6,5},{7,6},{8,9},{9,10},{10,1... | collective-permute-start | bytes 786440 | tf_op jit(solution)/shard_map/ppermute | solution.py:32
  33.9 12.7 %collective-permute-start.10 = (bf16[128,1024]{1,0:T(8,128)(2,1)S(1)}, bf16[128,1024]{1,0:T(8,128)(2,1)S(1)}, u32[]{:S(2)}, u32[]{:S(2)}) collective-permute-start(bf16[128,1024]{1,0:T(8,128)(2,1)S(1)} %collective-permute-done.6.refs_8_), channel_id=1, source_target_pairs={{0,7},{1,0},{2,1},{3,2},{4,3},{5,4},{6,5},{7,6},{8,9},{9,10},{10,1... | collective-permute-start | bytes 786440 | tf_op jit(solution)/shard_map/ppermute | solution.py:32
  35.9 10.7 %collective-permute-start.9 = (bf16[128,1024]{1,0:T(8,128)(2,1)S(1)}, bf16[128,1024]{1,0:T(8,128)(2,1)}, u32[]{:S(2)}, u32[]{:S(2)}) collective-permute-start(bf16[128,1024]{1,0:T(8,128)(2,1)S(1)} %collective-permute-done.5.refs_7_), channel_id=1, source_target_pairs={{0,1},{1,2},{2,3},{3,4},{4,5},{5,6},{6,7},{7,0},{8,15},{9,8},{10,9... | collective-permute-start | bytes 786440 | tf_op jit(solution)/shard_map/ppermute | solution.py:31
  40.5 10.8 %collective-permute-start.12 = (bf16[128,1024]{1,0:T(8,128)(2,1)S(1)}, bf16[128,1024]{1,0:T(8,128)(2,1)S(1)}, u32[]{:S(2)}, u32[]{:S(2)}) collective-permute-start(bf16[128,1024]{1,0:T(8,128)(2,1)S(1)} %collective-permute-done.8.refs_10_), channel_id=1, source_target_pairs={{0,1},{1,2},{2,3},{3,4},{4,5},{5,6},{6,7},{7,0},{8,15},{9,8},{10,9... | collective-permute-start | bytes 786440 | tf_op jit(solution)/shard_map/ppermute | solution.py:37
  43.9 10.8 %collective-permute-start.13 = (bf16[128,1024]{1,0:T(8,128)(2,1)S(1)}, bf16[128,1024]{1,0:T(8,128)(2,1)S(1)}, u32[]{:S(2)}, u32[]{:S(2)}) collective-permute-start(bf16[128,1024]{1,0:T(8,128)(2,1)S(1)} %collective-permute-done.11.refs_13_), channel_id=1, source_target_pairs={{0,7},{1,0},{2,1},{3,2},{4,3},{5,4},{6,5},{7,6},{8,9},{9,10},{10,1... | collective-permute-start | bytes 786440 | tf_op jit(solution)/shard_map/ppermute | solution.py:37
  113.0 9.1 %collective-permute-start.14 = (bf16[1088,128]{1,0:T(8,128)(2,1)S(1)}, bf16[1088,128]{1,0:T(8,128)(2,1)S(1)}, u32[]{:S(2)}, u32[]{:S(2)}) collective-permute-start(bf16[1088,128]{1,0:T(8,128)(2,1)S(1)} %bitcast.7), channel_id=1, source_target_pairs={{0,8},{8,0},{16,24},{24,16},{32,40},{40,32},{48,56},{56,48},{64,72... | collective-permute-start | bytes 835592 | tf_op jit(solution)/shard_map/ppermute | solution.py:221

commit v6 on v5

--- a/solution.py
+++ b/solution.py
@@ -87,12 +87,20 @@
     found = jnp.sum(jnp.where(taken, page + 1.0, 0.0), axis=1, keepdims=True)
     notes_ref[...] = jnp.broadcast_to(found, notes_ref.shape).astype(jnp.bfloat16)
     total = None
-    for i in range(count):
-        rows = jnp.concatenate([b[...] for b in blocks[i * CHUNKS : (i + 1) * CHUNKS]], axis=0)
-        fetches[2 * i].wait()
-        fetches[2 * i + 1].wait()
-        both = jnp.concatenate([weights[i, 0], weights[i, 1]], axis=1)
-        part = jnp.dot(rows, both, preferred_element_type=jnp.float32)
+    for group in (range(count // 2), range(count // 2, count)):
+        rows, both = [], []
+        for i in group:
+            fetches[2 * i].wait()
+            fetches[2 * i + 1].wait()
+            rows.append(
+                jnp.concatenate([b[...] for b in blocks[i * CHUNKS : (i + 1) * CHUNKS]], axis=0)
+            )
+            both.append(jnp.concatenate([weights[i, 0], weights[i, 1]], axis=1))
+        part = jnp.dot(
+            jnp.concatenate(rows, axis=1),
+            jnp.concatenate(both, axis=0),
+            preferred_element_type=jnp.float32,
+        )
         total = part if total is None else total + part
     total_ref[...] = total
     fetches[2 * count].wait()
@@ -117,8 +125,8 @@
         out_ref[at + 2 * span : at + stride, :] = notes_ref[d * slot_cap : (d + 1) * slot_cap, :]
 
 
-def place_kernel(slot_cap, side_ref, own_ref, other_ref, key_ref, value_ref, rows_ref, notes_ref):
-    pages, draft, head_cols = key_ref.shape
+def place_part(slot_cap, draft, pages, side_ref, from_ref, rows_ref, notes_ref):
+    head_cols = from_ref.shape[1]
     span = slot_cap * draft
     stride = 2 * span + slot_cap
     sources = rows_ref.shape[0]
@@ -126,8 +134,7 @@
 
     def take(side):
         for d in range(sources):
-            from_ref = own_ref if 2 * d < sources else other_ref
-            at = (2 * (d % (sources // 2)) + side) * stride
+            at = (2 * d + side) * stride
             rows_ref[d] = from_ref[at : at + 2 * span, :]
             notes = from_ref[at + 2 * span : at + stride, :].astype(jnp.float32)
             for s in range(slot_cap):
@@ -156,7 +163,17 @@
             select, both, (((0,), (0,)), ((), ())), preferred_element_type=jnp.float32
         )
         total = part if total is None else total + part
-    placed = total.astype(jnp.bfloat16)
+    return total
+
+
+def place_own_kernel(slot_cap, draft, pages, side_ref, own_ref, total_ref, rows_ref, notes_ref):
+    total_ref[...] = place_part(slot_cap, draft, pages, side_ref, own_ref, rows_ref, notes_ref)
+
+
+def place_kernel(slot_cap, side_ref, total_ref, other_ref, key_ref, value_ref, rows_ref, notes_ref):
+    pages, draft, head_cols = key_ref.shape
+    part = place_part(slot_cap, draft, pages, side_ref, other_ref, rows_ref, notes_ref)
+    placed = (total_ref[...] + part).astype(jnp.bfloat16)
     key_ref[...] = placed[:, :head_cols].reshape(pages, draft, head_cols)
     value_ref[...] = placed[:, head_cols:].reshape(pages, draft, head_cols)
 
@@ -220,18 +237,33 @@
     ).reshape(packed.shape)
     shared = lax.ppermute(arrived, "seq", [(i, i ^ 1) for i in range(seq_count)])
     cache = jax.ShapeDtypeStruct((slot_total, draft, head_cols), jnp.bfloat16)
+    half = [
+        pltpu.VMEM((seq_count // 2, 2 * slot_cap * draft, head_cols), jnp.bfloat16),
+        pltpu.VMEM((slot_cap, seq_count // 2 * draft, head_cols), jnp.float32),
+    ]
+    own = pl.pallas_call(
+        functools.partial(place_own_kernel, slot_cap, draft, slot_total),
+        out_shape=jax.ShapeDtypeStruct((slot_total * draft, 2 * head_cols), jnp.float32),
+        in_specs=[smem, vmem],
+        out_specs=vmem,
+        scratch_shapes=half,
+        cost_estimate=pl.CostEstimate(
+            flops=4 * slot_total * draft * slot_total * draft * head_cols,
+            bytes_accessed=4 * packed.size,
+            transcendentals=0,
+        ),
+        compiler_params=pltpu.CompilerParams(vmem_limit_bytes=OTHER_VMEM),
+        name="place_own",
+    )(side, arrived)
     return pl.pallas_call(
         functools.partial(place_kernel, slot_cap),
         out_shape=(cache, cache),
         in_specs=[smem, vmem, vmem],
         out_specs=(vmem, vmem),
-        scratch_shapes=[
-            pltpu.VMEM((seq_count, 2 * slot_cap * draft, head_cols), jnp.bfloat16),
-            pltpu.VMEM((slot_cap, seq_count * draft, head_cols), jnp.float32),
-        ],
+        scratch_shapes=half,
         compiler_params=pltpu.CompilerParams(vmem_limit_bytes=OTHER_VMEM),
         name="place",
-    )(side, arrived, shared)
+    )(side, own, shared)
 
 
 def solution(mesh):

time: 124 us -> 124 us (level)
  no operation moved by 1% of the time
where the time goes in v6:
time: 124 us; the launch traced here: 123 us
  blocking collectives  57.6 us (46%)
  starting transfers between devices  51.9 us (42%)
  Pallas kernels  6.34 us (5%)
  waiting for transfers between devices  4.73 us (4%)
    all_to_all x1, blocking collectives, local(): lax.all_to_all(paired, 'seq', split_axis=0, concat_axis=0, tiled=True, ax...  57.6 us
    ppermute x6, starting transfers between devices, gather_ring(): rising[c] = lax.ppermute(rising[c], axes, up)  26.9 us
    ppermute x6, starting transfers between devices, gather_ring(): falling[c] = lax.ppermute(falling[c], axes, down)  11.7 us
    ppermute x1, starting transfers between devices, local(): lax.ppermute(arrived, 'seq', [(i, i ^ 1) for i in range(seq_count)])  7.92 us
    pallas_call x1, Pallas kernels, local(): pl.pallas_call(functools.partial(project_kernel, offsets, slot_cap, draft...  4.21 us
    ppermute x1, waiting for transfers between devices, gather_ring(): lax.ppermute(falling[c], axes, down)  3.95 us
    ppermute x1, starting transfers between devices, gather_ring(): lax.ppermute(rising[c], axes, up)  3.39 us
  transfers between devices with their start and end apart: 15, of which 2 were waited for; matrix products, arithmetic and copies ran while one was open for 1% of the time, Pallas kernels for 4%

profile of v6, /device:TPU:65, one launch (start us, length us, event | category | flops | bytes accessed | tf_op | source)
XLA Modules:
  0.0 123.1 jit_solution(5506414381783572194)
XLA Ops:
  0.6 1.1 fusion
  1.7 6.3 %collective-permute-start = (bf16[128,1024]{1,0:T(8,128)(2,1)S(1)}, bf16[128,1024]{1,0:T(8,128)(2,1)S(1)}, u32[]{:S(2)}, u32[]{:S(2)}) collective-permute-start(bf16[128,1024]{1,0:T(8,128)(2,1)S(1)} %get-tuple-element.13.refs_0_), channel_id=1, source_target_pairs={{0,1},{1,2},{2,3},{3,4},{4,5},{5,6},{6,7},{7,0},{8,15},{9,8},{10,9... | collective-permute-start | bytes 786440 | tf_op jit(solution)/shard_map/ppermute | solution.py:31
  8.0 2.0 %collective-permute-start.3 = (bf16[128,1024]{1,0:T(8,128)(2,1)S(1)}, bf16[128,1024]{1,0:T(8,128)(2,1)S(1)}, u32[]{:S(2)}, u32[]{:S(2)}) collective-permute-start(bf16[128,1024]{1,0:T(8,128)(2,1)S(1)} %get-tuple-element.12.refs_1_), channel_id=1, source_target_pairs={{0,7},{1,0},{2,1},{3,2},{4,3},{5,4},{6,5},{7,6},{8,9},{9,10},{10,1... | collective-permute-start | bytes 786440 | tf_op jit(solution)/shard_map/ppermute | solution.py:32
  10.0 2.0 %collective-permute-start.2 = (bf16[128,1024]{1,0:T(8,128)(2,1)S(1)}, bf16[128,1024]{1,0:T(8,128)(2,1)S(1)}, u32[]{:S(2)}, u32[]{:S(2)}) collective-permute-start(bf16[128,1024]{1,0:T(8,128)(2,1)S(1)} %get-tuple-element.13.refs_0_), channel_id=1, source_target_pairs={{0,7},{1,0},{2,1},{3,2},{4,3},{5,4},{6,5},{7,6},{8,9},{9,10},{10,1... | collective-permute-start | bytes 786440 | tf_op jit(solution)/shard_map/ppermute | solution.py:32
  11.9 4.6 %collective-permute-start.1 = (bf16[128,1024]{1,0:T(8,128)(2,1)S(1)}, bf16[128,1024]{1,0:T(8,128)(2,1)S(1)}, u32[]{:S(2)}, u32[]{:S(2)}) collective-permute-start(bf16[128,1024]{1,0:T(8,128)(2,1)S(1)} %get-tuple-element.12.refs_1_), channel_id=1, source_target_pairs={{0,1},{1,2},{2,3},{3,4},{4,5},{5,6},{6,7},{7,0},{8,15},{9,8},{10,9... | collective-permute-start | bytes 786440 | tf_op jit(solution)/shard_map/ppermute | solution.py:31
  16.5 0.0 collective-permute-done.refs_2_
  16.5 3.4 %collective-permute-start.4 = (bf16[128,1024]{1,0:T(8,128)(2,1)S(1)}, bf16[128,1024]{1,0:T(8,128)(2,1)S(1)}, u32[]{:S(2)}, u32[]{:S(2)}) collective-permute-start(bf16[128,1024]{1,0:T(8,128)(2,1)S(1)} %collective-permute-done.refs_2_), channel_id=1, source_target_pairs={{0,1},{1,2},{2,3},{3,4},{4,5},{5,6},{6,7},{7,0},{8,15},{9,8},{10,9... | collective-permute-start | bytes 786440 | tf_op jit(solution)/shard_map/ppermute | solution.py:31
  19.9 0.0 collective-permute-done.3.refs_5_
  20.0 2.0 %collective-permute-start.7 = (bf16[128,1024]{1,0:T(8,128)(2,1)S(1)}, bf16[128,1024]{1,0:T(8,128)(2,1)S(1)}, u32[]{:S(2)}, u32[]{:S(2)}) collective-permute-start(bf16[128,1024]{1,0:T(8,128)(2,1)S(1)} %collective-permute-done.3.refs_5_), channel_id=1, source_target_pairs={{0,7},{1,0},{2,1},{3,2},{4,3},{5,4},{6,5},{7,6},{8,9},{9,10},{10,1... | collective-permute-start | bytes 786440 | tf_op jit(solution)/shard_map/ppermute | solution.py:32
  21.9 0.0 collective-permute-done.2.refs_4_
  21.9 2.0 %collective-permute-start.6 = (bf16[128,1024]{1,0:T(8,128)(2,1)S(1)}, bf16[128,1024]{1,0:T(8,128)(2,1)S(1)}, u32[]{:S(2)}, u32[]{:S(2)}) collective-permute-start(bf16[128,1024]{1,0:T(8,128)(2,1)S(1)} %collective-permute-done.2.refs_4_), channel_id=1, source_target_pairs={{0,7},{1,0},{2,1},{3,2},{4,3},{5,4},{6,5},{7,6},{8,9},{9,10},{10,1... | collective-permute-start | bytes 786440 | tf_op jit(solution)/shard_map/ppermute | solution.py:32
  23.9 0.0 collective-permute-done.1.refs_3_
  23.9 4.6 %collective-permute-start.5 = (bf16[128,1024]{1,0:T(8,128)(2,1)S(1)}, bf16[128,1024]{1,0:T(8,128)(2,1)S(1)}, u32[]{:S(2)}, u32[]{:S(2)}) collective-permute-start(bf16[128,1024]{1,0:T(8,128)(2,1)S(1)} %collective-permute-done.1.refs_3_), channel_id=1, source_target_pairs={{0,1},{1,2},{2,3},{3,4},{4,5},{5,6},{6,7},{7,0},{8,15},{9,8},{10,9... | collective-permute-start | bytes 786440 | tf_op jit(solution)/shard_map/ppermute | solution.py:31
  28.5 3.4 %collective-permute-start.8 = (bf16[128,1024]{1,0:T(8,128)(2,1)S(1)}, bf16[128,1024]{1,0:T(8,128)(2,1)S(1)}, u32[]{:S(2)}, u32[]{:S(2)}) collective-permute-start(bf16[128,1024]{1,0:T(8,128)(2,1)S(1)} %collective-permute-done.4.refs_6_), channel_id=1, source_target_pairs={{0,1},{1,2},{2,3},{3,4},{4,5},{5,6},{6,7},{7,0},{8,15},{9,8},{10,9... | collective-permute-start | bytes 786440 | tf_op jit(solution)/shard_map/ppermute | solution.py:31
  31.9 0.0 collective-permute-done.7.refs_9_
  31.9 2.0 %collective-permute-start.11 = (bf16[128,1024]{1,0:T(8,128)(2,1)S(1)}, bf16[128,1024]{1,0:T(8,128)(2,1)S(1)}, u32[]{:S(2)}, u32[]{:S(2)}) collective-permute-start(bf16[128,1024]{1,0:T(8,128)(2,1)S(1)} %collective-permute-done.7.refs_9_), channel_id=1, source_target_pairs={{0,7},{1,0},{2,1},{3,2},{4,3},{5,4},{6,5},{7,6},{8,9},{9,10},{10,1... | collective-permute-start | bytes 786440 | tf_op jit(solution)/shard_map/ppermute | solution.py:32
  33.9 2.0 %collective-permute-start.10 = (bf16[128,1024]{1,0:T(8,128)(2,1)S(1)}, bf16[128,1024]{1,0:T(8,128)(2,1)S(1)}, u32[]{:S(2)}, u32[]{:S(2)}) collective-permute-start(bf16[128,1024]{1,0:T(8,128)(2,1)S(1)} %collective-permute-done.6.refs_8_), channel_id=1, source_target_pairs={{0,7},{1,0},{2,1},{3,2},{4,3},{5,4},{6,5},{7,6},{8,9},{9,10},{10,1... | collective-permute-start | bytes 786440 | tf_op jit(solution)/shard_map/ppermute | solution.py:32
  35.9 4.6 %collective-permute-start.9 = (bf16[128,1024]{1,0:T(8,128)(2,1)S(1)}, bf16[128,1024]{1,0:T(8,128)(2,1)}, u32[]{:S(2)}, u32[]{:S(2)}) collective-permute-start(bf16[128,1024]{1,0:T(8,128)(2,1)S(1)} %collective-permute-done.5.refs_7_), channel_id=1, source_target_pairs={{0,1},{1,2},{2,3},{3,4},{4,5},{5,6},{6,7},{7,0},{8,15},{9,8},{10,9... | collective-permute-start | bytes 786440 | tf_op jit(solution)/shard_map/ppermute | solution.py:31
  40.5 0.0 collective-permute-done.8.refs_10_
  40.5 3.4 %collective-permute-start.12 = (bf16[128,1024]{1,0:T(8,128)(2,1)S(1)}, bf16[128,1024]{1,0:T(8,128)(2,1)S(1)}, u32[]{:S(2)}, u32[]{:S(2)}) collective-permute-start(bf16[128,1024]{1,0:T(8,128)(2,1)S(1)} %collective-permute-done.8.refs_10_), channel_id=1, source_target_pairs={{0,1},{1,2},{2,3},{3,4},{4,5},{5,6},{6,7},{7,0},{8,15},{9,8},{10,9... | collective-permute-start | bytes 786440 | tf_op jit(solution)/shard_map/ppermute | solution.py:37
  43.9 2.0 %collective-permute-start.13 = (bf16[128,1024]{1,0:T(8,128)(2,1)S(1)}, bf16[128,1024]{1,0:T(8,128)(2,1)S(1)}, u32[]{:S(2)}, u32[]{:S(2)}) collective-permute-start(bf16[128,1024]{1,0:T(8,128)(2,1)S(1)} %collective-permute-done.11.refs_13_), channel_id=1, source_target_pairs={{0,7},{1,0},{2,1},{3,2},{4,3},{5,4},{6,5},{7,6},{8,9},{9,10},{10,1... | collective-permute-start | bytes 786440 | tf_op jit(solution)/shard_map/ppermute | solution.py:37
  45.9 0.7 add_bitcast_fusion.route_ref
  46.6 0.0 collective-permute-done.10.refs_12_
  46.6 0.0 collective-permute-done.9.refs_11_
  46.6 4.2 %project.1 = (f32[256,256]{1,0:T(8,128)S(1)}, bf16[1024,128]{1,0:T(8,128)(2,1)S(1)}, bf16[1024,128]{1,0:T(8,128)(2,1)S(1)}, bf16[512,256]{1,0:T(8,128)(2,1)S(1)}, bf16[64,128]{1,0:T(8,128)(2,1)S(1)}) custom-call(s32[1]{0:T(128)} %bitcast.1.me_ref, s32[1]{0:T(128)S(6)} %sub.3.turn_ref, s32[1,32]{1,0:T(1,128)S(1)} %add_bitcast_fusion.route_ref, ...), custom_call_target="tpu_custom_call" | custom-call | flops 1073741824 | bytes 8388608 | tf_op jit(solution)/shard_map/project/pallas_call | solution.py:202
  50.8 4.0 %collective-permute-done.13.refs_1_ = bf16[128,1024]{1,0:T(8,128)(2,1)S(1)} collective-permute-done((bf16[128,1024]{1,0:T(8,128)(2,1)S(1)}, bf16[128,1024]{1,0:T(8,128)(2,1)S(1)}, u32[]{:S(2)}, u32[]{:S(2)}) %collective-permute-start.13) | collective-permute-done | bytes 262176 | tf_op jit(solution)/shard_map/ppermute | solution.py:37
  54.8 0.6 pack.1
  55.4 57.6 %all_to_all.5 = bf16[16,34,2,128]{3,2,1,0:T(2,128)(2,1)S(1)} all-to-all(bf16[16,34,2,128]{3,2,1,0:T(2,128)(2,1)S(1)} %bitcast.6), channel_id=1, replica_groups={{0,16,32,48,64,80,96,112,128,144,160,176,192,208,224,240},{8,24,40,56,7..., dimensions={0} | all-to-all | bytes 557056 | tf_op jit(solution)/shard_map/all_to_all | solution.py:235
  113.0 7.9 %collective-permute-start.14 = (bf16[1088,128]{1,0:T(8,128)(2,1)S(1)}, bf16[1088,128]{1,0:T(8,128)(2,1)S(1)}, u32[]{:S(2)}, u32[]{:S(2)}) collective-permute-start(bf16[1088,128]{1,0:T(8,128)(2,1)S(1)} %bitcast.7), channel_id=1, source_target_pairs={{0,8},{8,0},{16,24},{24,16},{32,40},{40,32},{48,56},{56,48},{64,72... | collective-permute-start | bytes 835592 | tf_op jit(solution)/shard_map/ppermute | solution.py:238
  120.9 0.4 place_own.1.total_ref
  121.3 0.7 collective-permute-done.14.other_ref
  122.0 1.1 place.1
  (5 shorter events, 0.0 us)
Async XLA Ops:
  1.7 14.8 %collective-permute-start = (bf16[128,1024]{1,0:T(8,128)(2,1)S(1)}, bf16[128,1024]{1,0:T(8,128)(2,1)S(1)}, u32[]{:S(2)}, u32[]{:S(2)}) collective-permute-start(bf16[128,1024]{1,0:T(8,128)(2,1)S(1)} %get-tuple-element.13.refs_0_), channel_id=1, source_target_pairs={{0,1},{1,2},{2,3},{3,4},{4,5},{5,6},{6,7},{7,0},{8,15},{9,8},{10,9... | collective-permute-start | bytes 786440 | tf_op jit(solution)/shard_map/ppermute | solution.py:31
  8.0 11.9 %collective-permute-start.3 = (bf16[128,1024]{1,0:T(8,128)(2,1)S(1)}, bf16[128,1024]{1,0:T(8,128)(2,1)S(1)}, u32[]{:S(2)}, u32[]{:S(2)}) collective-permute-start(bf16[128,1024]{1,0:T(8,128)(2,1)S(1)} %get-tuple-element.12.refs_1_), channel_id=1, source_target_pairs={{0,7},{1,0},{2,1},{3,2},{4,3},{5,4},{6,5},{7,6},{8,9},{9,10},{10,1... | collective-permute-start | bytes 786440 | tf_op jit(solution)/shard_map/ppermute | solution.py:32
  10.0 12.0 %collective-permute-start.2 = (bf16[128,1024]{1,0:T(8,128)(2,1)S(1)}, bf16[128,1024]{1,0:T(8,128)(2,1)S(1)}, u32[]{:S(2)}, u32[]{:S(2)}) collective-permute-start(bf16[128,1024]{1,0:T(8,128)(2,1)S(1)} %get-tuple-element.13.refs_0_), channel_id=1, source_target_pairs={{0,7},{1,0},{2,1},{3,2},{4,3},{5,4},{6,5},{7,6},{8,9},{9,10},{10,1... | collective-permute-start | bytes 786440 | tf_op jit(solution)/shard_map/ppermute | solution.py:32
  11.9 12.0 %collective-permute-start.1 = (bf16[128,1024]{1,0:T(8,128)(2,1)S(1)}, bf16[128,1024]{1,0:T(8,128)(2,1)S(1)}, u32[]{:S(2)}, u32[]{:S(2)}) collective-permute-start(bf16[128,1024]{1,0:T(8,128)(2,1)S(1)} %get-tuple-element.12.refs_1_), channel_id=1, source_target_pairs={{0,1},{1,2},{2,3},{3,4},{4,5},{5,6},{6,7},{7,0},{8,15},{9,8},{10,9... | collective-permute-start | bytes 786440 | tf_op jit(solution)/shard_map/ppermute | solution.py:31
  16.5 12.0 %collective-permute-start.4 = (bf16[128,1024]{1,0:T(8,128)(2,1)S(1)}, bf16[128,1024]{1,0:T(8,128)(2,1)S(1)}, u32[]{:S(2)}, u32[]{:S(2)}) collective-permute-start(bf16[128,1024]{1,0:T(8,128)(2,1)S(1)} %collective-permute-done.refs_2_), channel_id=1, source_target_pairs={{0,1},{1,2},{2,3},{3,4},{4,5},{5,6},{6,7},{7,0},{8,15},{9,8},{10,9... | collective-permute-start | bytes 786440 | tf_op jit(solution)/shard_map/ppermute | solution.py:31
  20.0 12.0 %collective-permute-start.7 = (bf16[128,1024]{1,0:T(8,128)(2,1)S(1)}, bf16[128,1024]{1,0:T(8,128)(2,1)S(1)}, u32[]{:S(2)}, u32[]{:S(2)}) collective-permute-start(bf16[128,1024]{1,0:T(8,128)(2,1)S(1)} %collective-permute-done.3.refs_5_), channel_id=1, source_target_pairs={{0,7},{1,0},{2,1},{3,2},{4,3},{5,4},{6,5},{7,6},{8,9},{9,10},{10,1... | collective-permute-start | bytes 786440 | tf_op jit(solution)/shard_map/ppermute | solution.py:32
  21.9 12.0 %collective-permute-start.6 = (bf16[128,1024]{1,0:T(8,128)(2,1)S(1)}, bf16[128,1024]{1,0:T(8,128)(2,1)S(1)}, u32[]{:S(2)}, u32[]{:S(2)}) collective-permute-start(bf16[128,1024]{1,0:T(8,128)(2,1)S(1)} %collective-permute-done.2.refs_4_), channel_id=1, source_target_pairs={{0,7},{1,0},{2,1},{3,2},{4,3},{5,4},{6,5},{7,6},{8,9},{9,10},{10,1... | collective-permute-start | bytes 786440 | tf_op jit(solution)/shard_map/ppermute | solution.py:32
  23.9 12.0 %collective-permute-start.5 = (bf16[128,1024]{1,0:T(8,128)(2,1)S(1)}, bf16[128,1024]{1,0:T(8,128)(2,1)S(1)}, u32[]{:S(2)}, u32[]{:S(2)}) collective-permute-start(bf16[128,1024]{1,0:T(8,128)(2,1)S(1)} %collective-permute-done.1.refs_3_), channel_id=1, source_target_pairs={{0,1},{1,2},{2,3},{3,4},{4,5},{5,6},{6,7},{7,0},{8,15},{9,8},{10,9... | collective-permute-start | bytes 786440 | tf_op jit(solution)/shard_map/ppermute | solution.py:31
  28.5 12.0 %collective-permute-start.8 = (bf16[128,1024]{1,0:T(8,128)(2,1)S(1)}, bf16[128,1024]{1,0:T(8,128)(2,1)S(1)}, u32[]{:S(2)}, u32[]{:S(2)}) collective-permute-start(bf16[128,1024]{1,0:T(8,128)(2,1)S(1)} %collective-permute-done.4.refs_6_), channel_id=1, source_target_pairs={{0,1},{1,2},{2,3},{3,4},{4,5},{5,6},{6,7},{7,0},{8,15},{9,8},{10,9... | collective-permute-start | bytes 786440 | tf_op jit(solution)/shard_map/ppermute | solution.py:31
  31.9 12.0 %collective-permute-start.11 = (bf16[128,1024]{1,0:T(8,128)(2,1)S(1)}, bf16[128,1024]{1,0:T(8,128)(2,1)S(1)}, u32[]{:S(2)}, u32[]{:S(2)}) collective-permute-start(bf16[128,1024]{1,0:T(8,128)(2,1)S(1)} %collective-permute-done.7.refs_9_), channel_id=1, source_target_pairs={{0,7},{1,0},{2,1},{3,2},{4,3},{5,4},{6,5},{7,6},{8,9},{9,10},{10,1... | collective-permute-start | bytes 786440 | tf_op jit(solution)/shard_map/ppermute | solution.py:32
  33.9 12.7 %collective-permute-start.10 = (bf16[128,1024]{1,0:T(8,128)(2,1)S(1)}, bf16[128,1024]{1,0:T(8,128)(2,1)S(1)}, u32[]{:S(2)}, u32[]{:S(2)}) collective-permute-start(bf16[128,1024]{1,0:T(8,128)(2,1)S(1)} %collective-permute-done.6.refs_8_), channel_id=1, source_target_pairs={{0,7},{1,0},{2,1},{3,2},{4,3},{5,4},{6,5},{7,6},{8,9},{9,10},{10,1... | collective-permute-start | bytes 786440 | tf_op jit(solution)/shard_map/ppermute | solution.py:32
  35.9 10.7 %collective-permute-start.9 = (bf16[128,1024]{1,0:T(8,128)(2,1)S(1)}, bf16[128,1024]{1,0:T(8,128)(2,1)}, u32[]{:S(2)}, u32[]{:S(2)}) collective-permute-start(bf16[128,1024]{1,0:T(8,128)(2,1)S(1)} %collective-permute-done.5.refs_7_), channel_id=1, source_target_pairs={{0,1},{1,2},{2,3},{3,4},{4,5},{5,6},{6,7},{7,0},{8,15},{9,8},{10,9... | collective-permute-start | bytes 786440 | tf_op jit(solution)/shard_map/ppermute | solution.py:31
  40.5 10.3 %collective-permute-start.12 = (bf16[128,1024]{1,0:T(8,128)(2,1)S(1)}, bf16[128,1024]{1,0:T(8,128)(2,1)S(1)}, u32[]{:S(2)}, u32[]{:S(2)}) collective-permute-start(bf16[128,1024]{1,0:T(8,128)(2,1)S(1)} %collective-permute-done.8.refs_10_), channel_id=1, source_target_pairs={{0,1},{1,2},{2,3},{3,4},{4,5},{5,6},{6,7},{7,0},{8,15},{9,8},{10,9... | collective-permute-start | bytes 786440 | tf_op jit(solution)/shard_map/ppermute | solution.py:37
  43.9 10.8 %collective-permute-start.13 = (bf16[128,1024]{1,0:T(8,128)(2,1)S(1)}, bf16[128,1024]{1,0:T(8,128)(2,1)S(1)}, u32[]{:S(2)}, u32[]{:S(2)}) collective-permute-start(bf16[128,1024]{1,0:T(8,128)(2,1)S(1)} %collective-permute-done.11.refs_13_), channel_id=1, source_target_pairs={{0,7},{1,0},{2,1},{3,2},{4,3},{5,4},{6,5},{7,6},{8,9},{9,10},{10,1... | collective-permute-start | bytes 786440 | tf_op jit(solution)/shard_map/ppermute | solution.py:37
  113.0 9.1 %collective-permute-start.14 = (bf16[1088,128]{1,0:T(8,128)(2,1)S(1)}, bf16[1088,128]{1,0:T(8,128)(2,1)S(1)}, u32[]{:S(2)}, u32[]{:S(2)}) collective-permute-start(bf16[1088,128]{1,0:T(8,128)(2,1)S(1)} %bitcast.7), channel_id=1, source_target_pairs={{0,8},{8,0},{16,24},{24,16},{32,40},{40,32},{48,56},{56,48},{64,72... | collective-permute-start | bytes 835592 | tf_op jit(solution)/shard_map/ppermute | solution.py:238

commit v7 on v6

--- a/solution.py
+++ b/solution.py
@@ -8,7 +8,7 @@
 from jax.sharding import PartitionSpec as P
 
 CHUNKS = 2
-PROJECT_VMEM = 49 * 2**20
+PROJECT_VMEM = 99 * 2**19
 OTHER_VMEM = 12 * 2**20
 
 

time: 124 us -> 124 us (level)
  no operation moved by 1% of the time
where the time goes in v7:
time: 124 us; the launch traced here: 123 us
  blocking collectives  57.9 us (47%)
  starting transfers between devices  51.5 us (42%)
  Pallas kernels  6.34 us (5%)
  waiting for transfers between devices  4.73 us (4%)
    all_to_all x1, blocking collectives, local(): lax.all_to_all(paired, 'seq', split_axis=0, concat_axis=0, tiled=True, ax...  57.9 us
    ppermute x6, starting transfers between devices, gather_ring(): rising[c] = lax.ppermute(rising[c], axes, up)  26.9 us
    ppermute x6, starting transfers between devices, gather_ring(): falling[c] = lax.ppermute(falling[c], axes, down)  11.7 us
    ppermute x1, starting transfers between devices, local(): lax.ppermute(arrived, 'seq', [(i, i ^ 1) for i in range(seq_count)])  7.51 us
    pallas_call x1, Pallas kernels, local(): pl.pallas_call(functools.partial(project_kernel, offsets, slot_cap, draft...  4.21 us
    ppermute x1, waiting for transfers between devices, gather_ring(): lax.ppermute(falling[c], axes, down)  3.95 us
    ppermute x1, starting transfers between devices, gather_ring(): lax.ppermute(rising[c], axes, up)  3.39 us
  transfers between devices with their start and end apart: 15, of which 2 were waited for; matrix products, arithmetic and copies ran while one was open for 1% of the time, Pallas kernels for 4%

profile of v7, /device:TPU:65, one launch (start us, length us, event | category | flops | bytes accessed | tf_op | source)
XLA Modules:
  0.0 123.1 jit_solution(2579965405096935013)
XLA Ops:
  0.6 1.1 fusion
  1.7 6.3 %collective-permute-start = (bf16[128,1024]{1,0:T(8,128)(2,1)S(1)}, bf16[128,1024]{1,0:T(8,128)(2,1)S(1)}, u32[]{:S(2)}, u32[]{:S(2)}) collective-permute-start(bf16[128,1024]{1,0:T(8,128)(2,1)S(1)} %get-tuple-element.13.refs_0_), channel_id=1, source_target_pairs={{0,1},{1,2},{2,3},{3,4},{4,5},{5,6},{6,7},{7,0},{8,15},{9,8},{10,9... | collective-permute-start | bytes 786440 | tf_op jit(solution)/shard_map/ppermute | solution.py:31
  8.0 2.0 %collective-permute-start.3 = (bf16[128,1024]{1,0:T(8,128)(2,1)S(1)}, bf16[128,1024]{1,0:T(8,128)(2,1)S(1)}, u32[]{:S(2)}, u32[]{:S(2)}) collective-permute-start(bf16[128,1024]{1,0:T(8,128)(2,1)S(1)} %get-tuple-element.12.refs_1_), channel_id=1, source_target_pairs={{0,7},{1,0},{2,1},{3,2},{4,3},{5,4},{6,5},{7,6},{8,9},{9,10},{10,1... | collective-permute-start | bytes 786440 | tf_op jit(solution)/shard_map/ppermute | solution.py:32
  10.0 2.0 %collective-permute-start.2 = (bf16[128,1024]{1,0:T(8,128)(2,1)S(1)}, bf16[128,1024]{1,0:T(8,128)(2,1)S(1)}, u32[]{:S(2)}, u32[]{:S(2)}) collective-permute-start(bf16[128,1024]{1,0:T(8,128)(2,1)S(1)} %get-tuple-element.13.refs_0_), channel_id=1, source_target_pairs={{0,7},{1,0},{2,1},{3,2},{4,3},{5,4},{6,5},{7,6},{8,9},{9,10},{10,1... | collective-permute-start | bytes 786440 | tf_op jit(solution)/shard_map/ppermute | solution.py:32
  11.9 4.6 %collective-permute-start.1 = (bf16[128,1024]{1,0:T(8,128)(2,1)S(1)}, bf16[128,1024]{1,0:T(8,128)(2,1)S(1)}, u32[]{:S(2)}, u32[]{:S(2)}) collective-permute-start(bf16[128,1024]{1,0:T(8,128)(2,1)S(1)} %get-tuple-element.12.refs_1_), channel_id=1, source_target_pairs={{0,1},{1,2},{2,3},{3,4},{4,5},{5,6},{6,7},{7,0},{8,15},{9,8},{10,9... | collective-permute-start | bytes 786440 | tf_op jit(solution)/shard_map/ppermute | solution.py:31
  16.5 0.0 collective-permute-done.refs_2_
  16.5 3.4 %collective-permute-start.4 = (bf16[128,1024]{1,0:T(8,128)(2,1)S(1)}, bf16[128,1024]{1,0:T(8,128)(2,1)S(1)}, u32[]{:S(2)}, u32[]{:S(2)}) collective-permute-start(bf16[128,1024]{1,0:T(8,128)(2,1)S(1)} %collective-permute-done.refs_2_), channel_id=1, source_target_pairs={{0,1},{1,2},{2,3},{3,4},{4,5},{5,6},{6,7},{7,0},{8,15},{9,8},{10,9... | collective-permute-start | bytes 786440 | tf_op jit(solution)/shard_map/ppermute | solution.py:31
  19.9 0.0 collective-permute-done.3.refs_5_
  20.0 2.0 %collective-permute-start.7 = (bf16[128,1024]{1,0:T(8,128)(2,1)S(1)}, bf16[128,1024]{1,0:T(8,128)(2,1)S(1)}, u32[]{:S(2)}, u32[]{:S(2)}) collective-permute-start(bf16[128,1024]{1,0:T(8,128)(2,1)S(1)} %collective-permute-done.3.refs_5_), channel_id=1, source_target_pairs={{0,7},{1,0},{2,1},{3,2},{4,3},{5,4},{6,5},{7,6},{8,9},{9,10},{10,1... | collective-permute-start | bytes 786440 | tf_op jit(solution)/shard_map/ppermute | solution.py:32
  21.9 0.0 collective-permute-done.2.refs_4_
  21.9 2.0 %collective-permute-start.6 = (bf16[128,1024]{1,0:T(8,128)(2,1)S(1)}, bf16[128,1024]{1,0:T(8,128)(2,1)S(1)}, u32[]{:S(2)}, u32[]{:S(2)}) collective-permute-start(bf16[128,1024]{1,0:T(8,128)(2,1)S(1)} %collective-permute-done.2.refs_4_), channel_id=1, source_target_pairs={{0,7},{1,0},{2,1},{3,2},{4,3},{5,4},{6,5},{7,6},{8,9},{9,10},{10,1... | collective-permute-start | bytes 786440 | tf_op jit(solution)/shard_map/ppermute | solution.py:32
  23.9 0.0 collective-permute-done.1.refs_3_
  23.9 4.6 %collective-permute-start.5 = (bf16[128,1024]{1,0:T(8,128)(2,1)S(1)}, bf16[128,1024]{1,0:T(8,128)(2,1)S(1)}, u32[]{:S(2)}, u32[]{:S(2)}) collective-permute-start(bf16[128,1024]{1,0:T(8,128)(2,1)S(1)} %collective-permute-done.1.refs_3_), channel_id=1, source_target_pairs={{0,1},{1,2},{2,3},{3,4},{4,5},{5,6},{6,7},{7,0},{8,15},{9,8},{10,9... | collective-permute-start | bytes 786440 | tf_op jit(solution)/shard_map/ppermute | solution.py:31
  28.5 0.0 collective-permute-done.4.refs_6_
  28.5 3.4 %collective-permute-start.8 = (bf16[128,1024]{1,0:T(8,128)(2,1)S(1)}, bf16[128,1024]{1,0:T(8,128)(2,1)S(1)}, u32[]{:S(2)}, u32[]{:S(2)}) collective-permute-start(bf16[128,1024]{1,0:T(8,128)(2,1)S(1)} %collective-permute-done.4.refs_6_), channel_id=1, source_target_pairs={{0,1},{1,2},{2,3},{3,4},{4,5},{5,6},{6,7},{7,0},{8,15},{9,8},{10,9... | collective-permute-start | bytes 786440 | tf_op jit(solution)/shard_map/ppermute | solution.py:31
  31.9 2.0 %collective-permute-start.11 = (bf16[128,1024]{1,0:T(8,128)(2,1)S(1)}, bf16[128,1024]{1,0:T(8,128)(2,1)}, u32[]{:S(2)}, u32[]{:S(2)}) collective-permute-start(bf16[128,1024]{1,0:T(8,128)(2,1)S(1)} %collective-permute-done.7.refs_9_), channel_id=1, source_target_pairs={{0,7},{1,0},{2,1},{3,2},{4,3},{5,4},{6,5},{7,6},{8,9},{9,10},{10,1... | collective-permute-start | bytes 786440 | tf_op jit(solution)/shard_map/ppermute | solution.py:32
  33.9 2.0 %collective-permute-start.10 = (bf16[128,1024]{1,0:T(8,128)(2,1)S(1)}, bf16[128,1024]{1,0:T(8,128)(2,1)S(1)}, u32[]{:S(2)}, u32[]{:S(2)}) collective-permute-start(bf16[128,1024]{1,0:T(8,128)(2,1)S(1)} %collective-permute-done.6.refs_8_), channel_id=1, source_target_pairs={{0,7},{1,0},{2,1},{3,2},{4,3},{5,4},{6,5},{7,6},{8,9},{9,10},{10,1... | collective-permute-start | bytes 786440 | tf_op jit(solution)/shard_map/ppermute | solution.py:32
  35.9 4.6 %collective-permute-start.9 = (bf16[128,1024]{1,0:T(8,128)(2,1)S(1)}, bf16[128,1024]{1,0:T(8,128)(2,1)S(1)}, u32[]{:S(2)}, u32[]{:S(2)}) collective-permute-start(bf16[128,1024]{1,0:T(8,128)(2,1)S(1)} %collective-permute-done.5.refs_7_), channel_id=1, source_target_pairs={{0,1},{1,2},{2,3},{3,4},{4,5},{5,6},{6,7},{7,0},{8,15},{9,8},{10,9... | collective-permute-start | bytes 786440 | tf_op jit(solution)/shard_map/ppermute | solution.py:31
  40.5 3.4 %collective-permute-start.12 = (bf16[128,1024]{1,0:T(8,128)(2,1)S(1)}, bf16[128,1024]{1,0:T(8,128)(2,1)S(1)}, u32[]{:S(2)}, u32[]{:S(2)}) collective-permute-start(bf16[128,1024]{1,0:T(8,128)(2,1)S(1)} %collective-permute-done.8.refs_10_), channel_id=1, source_target_pairs={{0,1},{1,2},{2,3},{3,4},{4,5},{5,6},{6,7},{7,0},{8,15},{9,8},{10,9... | collective-permute-start | bytes 786440 | tf_op jit(solution)/shard_map/ppermute | solution.py:37
  43.9 0.0 collective-permute-done.11.refs_13_
  43.9 2.0 %collective-permute-start.13 = (bf16[128,1024]{1,0:T(8,128)(2,1)}, bf16[128,1024]{1,0:T(8,128)(2,1)S(1)}, u32[]{:S(2)}, u32[]{:S(2)}) collective-permute-start(bf16[128,1024]{1,0:T(8,128)(2,1)} %collective-permute-done.11.refs_13_), channel_id=1, source_target_pairs={{0,7},{1,0},{2,1},{3,2},{4,3},{5,4},{6,5},{7,6},{8,9},{9,10},{10,1... | collective-permute-start | bytes 786440 | tf_op jit(solution)/shard_map/ppermute | solution.py:37
  45.9 0.7 add_bitcast_fusion.route_ref
  46.6 0.0 collective-permute-done.10.refs_12_
  46.6 0.0 collective-permute-done.9.refs_11_
  46.6 4.2 %project.1 = (f32[256,256]{1,0:T(8,128)S(1)}, bf16[1024,128]{1,0:T(8,128)(2,1)S(1)}, bf16[1024,128]{1,0:T(8,128)(2,1)S(1)}, bf16[512,256]{1,0:T(8,128)(2,1)S(1)}, bf16[64,128]{1,0:T(8,128)(2,1)S(1)}) custom-call(s32[1]{0:T(128)} %bitcast.1.me_ref, s32[1]{0:T(128)S(6)} %sub.3.turn_ref, s32[1,32]{1,0:T(1,128)S(1)} %add_bitcast_fusion.route_ref, ...), custom_call_target="tpu_custom_call" | custom-call | flops 1073741824 | bytes 8388608 | tf_op jit(solution)/shard_map/project/pallas_call | solution.py:202
  50.8 4.0 %collective-permute-done.13.refs_1_ = bf16[128,1024]{1,0:T(8,128)(2,1)S(1)} collective-permute-done((bf16[128,1024]{1,0:T(8,128)(2,1)}, bf16[128,1024]{1,0:T(8,128)(2,1)S(1)}, u32[]{:S(2)}, u32[]{:S(2)}) %collective-permute-start.13) | collective-permute-done | bytes 262176 | tf_op jit(solution)/shard_map/ppermute | solution.py:37
  54.8 0.6 pack.1
  55.4 57.9 %all_to_all.5 = bf16[16,34,2,128]{3,2,1,0:T(2,128)(2,1)S(1)} all-to-all(bf16[16,34,2,128]{3,2,1,0:T(2,128)(2,1)S(1)} %bitcast.6), channel_id=1, replica_groups={{0,16,32,48,64,80,96,112,128,144,160,176,192,208,224,240},{8,24,40,56,7..., dimensions={0} | all-to-all | bytes 557056 | tf_op jit(solution)/shard_map/all_to_all | solution.py:235
  113.3 7.5 %collective-permute-start.14 = (bf16[1088,128]{1,0:T(8,128)(2,1)S(1)}, bf16[1088,128]{1,0:T(8,128)(2,1)S(1)}, u32[]{:S(2)}, u32[]{:S(2)}) collective-permute-start(bf16[1088,128]{1,0:T(8,128)(2,1)S(1)} %bitcast.7), channel_id=1, source_target_pairs={{0,8},{8,0},{16,24},{24,16},{32,40},{40,32},{48,56},{56,48},{64,72... | collective-permute-start | bytes 835592 | tf_op jit(solution)/shard_map/ppermute | solution.py:238
  120.8 0.4 place_own.1.total_ref
  121.2 0.7 collective-permute-done.14.other_ref
  122.0 1.1 place.1
  (5 shorter events, 0.0 us)
Async XLA Ops:
  1.7 14.8 %collective-permute-start = (bf16[128,1024]{1,0:T(8,128)(2,1)S(1)}, bf16[128,1024]{1,0:T(8,128)(2,1)S(1)}, u32[]{:S(2)}, u32[]{:S(2)}) collective-permute-start(bf16[128,1024]{1,0:T(8,128)(2,1)S(1)} %get-tuple-element.13.refs_0_), channel_id=1, source_target_pairs={{0,1},{1,2},{2,3},{3,4},{4,5},{5,6},{6,7},{7,0},{8,15},{9,8},{10,9... | collective-permute-start | bytes 786440 | tf_op jit(solution)/shard_map/ppermute | solution.py:31
  8.0 11.9 %collective-permute-start.3 = (bf16[128,1024]{1,0:T(8,128)(2,1)S(1)}, bf16[128,1024]{1,0:T(8,128)(2,1)S(1)}, u32[]{:S(2)}, u32[]{:S(2)}) collective-permute-start(bf16[128,1024]{1,0:T(8,128)(2,1)S(1)} %get-tuple-element.12.refs_1_), channel_id=1, source_target_pairs={{0,7},{1,0},{2,1},{3,2},{4,3},{5,4},{6,5},{7,6},{8,9},{9,10},{10,1... | collective-permute-start | bytes 786440 | tf_op jit(solution)/shard_map/ppermute | solution.py:32
  10.0 12.0 %collective-permute-start.2 = (bf16[128,1024]{1,0:T(8,128)(2,1)S(1)}, bf16[128,1024]{1,0:T(8,128)(2,1)S(1)}, u32[]{:S(2)}, u32[]{:S(2)}) collective-permute-start(bf16[128,1024]{1,0:T(8,128)(2,1)S(1)} %get-tuple-element.13.refs_0_), channel_id=1, source_target_pairs={{0,7},{1,0},{2,1},{3,2},{4,3},{5,4},{6,5},{7,6},{8,9},{9,10},{10,1... | collective-permute-start | bytes 786440 | tf_op jit(solution)/shard_map/ppermute | solution.py:32
  11.9 12.0 %collective-permute-start.1 = (bf16[128,1024]{1,0:T(8,128)(2,1)S(1)}, bf16[128,1024]{1,0:T(8,128)(2,1)S(1)}, u32[]{:S(2)}, u32[]{:S(2)}) collective-permute-start(bf16[128,1024]{1,0:T(8,128)(2,1)S(1)} %get-tuple-element.12.refs_1_), channel_id=1, source_target_pairs={{0,1},{1,2},{2,3},{3,4},{4,5},{5,6},{6,7},{7,0},{8,15},{9,8},{10,9... | collective-permute-start | bytes 786440 | tf_op jit(solution)/shard_map/ppermute | solution.py:31
  16.5 12.0 %collective-permute-start.4 = (bf16[128,1024]{1,0:T(8,128)(2,1)S(1)}, bf16[128,1024]{1,0:T(8,128)(2,1)S(1)}, u32[]{:S(2)}, u32[]{:S(2)}) collective-permute-start(bf16[128,1024]{1,0:T(8,128)(2,1)S(1)} %collective-permute-done.refs_2_), channel_id=1, source_target_pairs={{0,1},{1,2},{2,3},{3,4},{4,5},{5,6},{6,7},{7,0},{8,15},{9,8},{10,9... | collective-permute-start | bytes 786440 | tf_op jit(solution)/shard_map/ppermute | solution.py:31
  20.0 12.0 %collective-permute-start.7 = (bf16[128,1024]{1,0:T(8,128)(2,1)S(1)}, bf16[128,1024]{1,0:T(8,128)(2,1)S(1)}, u32[]{:S(2)}, u32[]{:S(2)}) collective-permute-start(bf16[128,1024]{1,0:T(8,128)(2,1)S(1)} %collective-permute-done.3.refs_5_), channel_id=1, source_target_pairs={{0,7},{1,0},{2,1},{3,2},{4,3},{5,4},{6,5},{7,6},{8,9},{9,10},{10,1... | collective-permute-start | bytes 786440 | tf_op jit(solution)/shard_map/ppermute | solution.py:32
  21.9 12.0 %collective-permute-start.6 = (bf16[128,1024]{1,0:T(8,128)(2,1)S(1)}, bf16[128,1024]{1,0:T(8,128)(2,1)S(1)}, u32[]{:S(2)}, u32[]{:S(2)}) collective-permute-start(bf16[128,1024]{1,0:T(8,128)(2,1)S(1)} %collective-permute-done.2.refs_4_), channel_id=1, source_target_pairs={{0,7},{1,0},{2,1},{3,2},{4,3},{5,4},{6,5},{7,6},{8,9},{9,10},{10,1... | collective-permute-start | bytes 786440 | tf_op jit(solution)/shard_map/ppermute | solution.py:32
  23.9 12.0 %collective-permute-start.5 = (bf16[128,1024]{1,0:T(8,128)(2,1)S(1)}, bf16[128,1024]{1,0:T(8,128)(2,1)S(1)}, u32[]{:S(2)}, u32[]{:S(2)}) collective-permute-start(bf16[128,1024]{1,0:T(8,128)(2,1)S(1)} %collective-permute-done.1.refs_3_), channel_id=1, source_target_pairs={{0,1},{1,2},{2,3},{3,4},{4,5},{5,6},{6,7},{7,0},{8,15},{9,8},{10,9... | collective-permute-start | bytes 786440 | tf_op jit(solution)/shard_map/ppermute | solution.py:31
  28.5 12.0 %collective-permute-start.8 = (bf16[128,1024]{1,0:T(8,128)(2,1)S(1)}, bf16[128,1024]{1,0:T(8,128)(2,1)S(1)}, u32[]{:S(2)}, u32[]{:S(2)}) collective-permute-start(bf16[128,1024]{1,0:T(8,128)(2,1)S(1)} %collective-permute-done.4.refs_6_), channel_id=1, source_target_pairs={{0,1},{1,2},{2,3},{3,4},{4,5},{5,6},{6,7},{7,0},{8,15},{9,8},{10,9... | collective-permute-start | bytes 786440 | tf_op jit(solution)/shard_map/ppermute | solution.py:31
  31.9 12.0 %collective-permute-start.11 = (bf16[128,1024]{1,0:T(8,128)(2,1)S(1)}, bf16[128,1024]{1,0:T(8,128)(2,1)}, u32[]{:S(2)}, u32[]{:S(2)}) collective-permute-start(bf16[128,1024]{1,0:T(8,128)(2,1)S(1)} %collective-permute-done.7.refs_9_), channel_id=1, source_target_pairs={{0,7},{1,0},{2,1},{3,2},{4,3},{5,4},{6,5},{7,6},{8,9},{9,10},{10,1... | collective-permute-start | bytes 786440 | tf_op jit(solution)/shard_map/ppermute | solution.py:32
  33.9 12.7 %collective-permute-start.10 = (bf16[128,1024]{1,0:T(8,128)(2,1)S(1)}, bf16[128,1024]{1,0:T(8,128)(2,1)S(1)}, u32[]{:S(2)}, u32[]{:S(2)}) collective-permute-start(bf16[128,1024]{1,0:T(8,128)(2,1)S(1)} %collective-permute-done.6.refs_8_), channel_id=1, source_target_pairs={{0,7},{1,0},{2,1},{3,2},{4,3},{5,4},{6,5},{7,6},{8,9},{9,10},{10,1... | collective-permute-start | bytes 786440 | tf_op jit(solution)/shard_map/ppermute | solution.py:32
  35.9 10.7 %collective-permute-start.9 = (bf16[128,1024]{1,0:T(8,128)(2,1)S(1)}, bf16[128,1024]{1,0:T(8,128)(2,1)S(1)}, u32[]{:S(2)}, u32[]{:S(2)}) collective-permute-start(bf16[128,1024]{1,0:T(8,128)(2,1)S(1)} %collective-permute-done.5.refs_7_), channel_id=1, source_target_pairs={{0,1},{1,2},{2,3},{3,4},{4,5},{5,6},{6,7},{7,0},{8,15},{9,8},{10,9... | collective-permute-start | bytes 786440 | tf_op jit(solution)/shard_map/ppermute | solution.py:31
  40.5 10.3 %collective-permute-start.12 = (bf16[128,1024]{1,0:T(8,128)(2,1)S(1)}, bf16[128,1024]{1,0:T(8,128)(2,1)S(1)}, u32[]{:S(2)}, u32[]{:S(2)}) collective-permute-start(bf16[128,1024]{1,0:T(8,128)(2,1)S(1)} %collective-permute-done.8.refs_10_), channel_id=1, source_target_pairs={{0,1},{1,2},{2,3},{3,4},{4,5},{5,6},{6,7},{7,0},{8,15},{9,8},{10,9... | collective-permute-start | bytes 786440 | tf_op jit(solution)/shard_map/ppermute | solution.py:37
  43.9 10.8 %collective-permute-start.13 = (bf16[128,1024]{1,0:T(8,128)(2,1)}, bf16[128,1024]{1,0:T(8,128)(2,1)S(1)}, u32[]{:S(2)}, u32[]{:S(2)}) collective-permute-start(bf16[128,1024]{1,0:T(8,128)(2,1)} %collective-permute-done.11.refs_13_), channel_id=1, source_target_pairs={{0,7},{1,0},{2,1},{3,2},{4,3},{5,4},{6,5},{7,6},{8,9},{9,10},{10,1... | collective-permute-start | bytes 786440 | tf_op jit(solution)/shard_map/ppermute | solution.py:37
  113.3 8.7 %collective-permute-start.14 = (bf16[1088,128]{1,0:T(8,128)(2,1)S(1)}, bf16[1088,128]{1,0:T(8,128)(2,1)S(1)}, u32[]{:S(2)}, u32[]{:S(2)}) collective-permute-start(bf16[1088,128]{1,0:T(8,128)(2,1)S(1)} %bitcast.7), channel_id=1, source_target_pairs={{0,8},{8,0},{16,24},{24,16},{32,40},{40,32},{48,56},{56,48},{64,72... | collective-permute-start | bytes 835592 | tf_op jit(solution)/shard_map/ppermute | solution.py:238
